TPU v7x, 256 devices: a 4x2x16 block of a 4x16x16 slice. The times are simulated.
256 devices in a mesh: groups: 2 (over y), ep: 128 (over x, z, core).
Axes of the slice: x: 4, y: 2, z: 16, core: 2. Of those that a mesh axis runs over, the one named last changes fastest.
The devices are a block of a 4x16x16 slice.
Arguments:
- tokens: bfloat16 [1024, 7168], P(('groups', 'ep')), parts along dimension 0, may hold values from -6 to 6
- routes: int32 [1024, 8], P(('groups', 'ep')), parts along dimension 0, may hold values from 0 to 15, as said below
- gates: float32 [1024, 8], P(('groups', 'ep')), parts along dimension 0, may hold values from 0.05 to 0.6
- gate_weight: bfloat16 [7168, 32768], P(None, 'ep'), may hold values from -0.0625 to 0.0625
- up_weight: bfloat16 [7168, 32768], P(None, 'ep'), may hold values from -0.0625 to 0.0625
- down_weight: bfloat16 [32768, 7168], P('ep'), may hold values from -0.125 to 0.125
Outputs:
- mixed: bfloat16 [1024, 7168], P(('groups', 'ep')), parts along dimension 0
There are 2 independent parts, one for each index of `groups`. A program takes and returns all parts, laid end to end along the dimension named above; an argument that names none is the same for every part. Nothing has to cross between parts.
Inputs may be any that keep to these rules, and one draw needn't show every extreme that they name: `routes`: each token names 8 different experts. Among the 4 tokens of one device no expert is named by more than 3 of them, and in every draw one expert is named by exactly 3 tokens of every device.
All inputs are finite; a program needn't handle non-finite values.
Results may differ from a plain program's by a relative error of at most 0.0085.
Values may be sent and summed in bfloat16 or wider, within the bound.
No kernel may reach another device: no remote copies, remote signals or barrier semaphores. Data moves between devices by JAX's collectives and lax.ppermute only.
A program may use at most 128 MiB of HBM per device.

v0:
```python
import functools

import jax
import jax.numpy as jnp
from jax import lax
from jax.experimental import pallas as pl
from jax.experimental.pallas import tpu as pltpu
from jax.sharding import Mesh
from jax.sharding import PartitionSpec as P


EXPERTS = 16
LANES = 128
EP = ("ep_0", "ep_1", "ep_2")
GROUPS_EP = ("groups", "ep_0", "ep_1", "ep_2")
FAR = (8, 4, 12)
Z_OFFSETS = (0, 8, 4, 12, 1, 9, 5, 13, 15, 7, 3, 11, 2, 10, 14, 6)
LOW, HIGH = jnp.bfloat16, jnp.float32


def take_from(value, axis, offset):
    count = lax.axis_size(axis)
    return lax.ppermute(value, axis, [((i + offset) % count, i) for i in range(count)])


def give_to(value, axis, offset):
    count = lax.axis_size(axis)
    return lax.ppermute(value, axis, [(i, (i + offset) % count) for i in range(count)])


def other_core(value):
    return give_to(value, "ep_2", 1)


def gate_columns(routes, gates):
    member = routes[:, :, None] == jnp.arange(EXPERTS, dtype=routes.dtype)
    left = jnp.sum(jnp.where(member, gates[:, :, None], 0.0), axis=1)
    parts = []
    for _ in range(3):
        part = lax.reduce_precision(left, 8, 7)
        parts.append(part.astype(LOW))
        left = left - part
    columns = jnp.concatenate(parts, axis=1)
    return jnp.pad(columns, ((0, 0), (0, LANES - columns.shape[1])))


def row_order(tok_rows):
    count = lax.axis_size("ep_1")
    wanted = (lax.axis_index("ep_1") + jnp.array(Z_OFFSETS, jnp.int32)) % count
    wanted = (wanted[:, None] * tok_rows + jnp.arange(tok_rows, dtype=jnp.int32)).reshape(-1)
    return (wanted[:, None] == jnp.arange(count * tok_rows, dtype=jnp.int32)).astype(LOW)


def hidden_kernel(blocks, expert_ref, order_ref, *refs):
    row_refs, column_refs = refs[:blocks], refs[blocks : 2 * blocks]
    gate_ref, up_ref, hidden_ref, weight_ref, gate_sum, up_sum = refs[2 * blocks :]
    step = pl.program_id(0)

    @pl.when(step == 0)
    def _():
        gate_sum[...] = jnp.zeros_like(gate_sum)
        up_sum[...] = jnp.zeros_like(up_sum)

    rows = jnp.concatenate([r[...] for r in row_refs], axis=0)
    gate_sum[...] += jnp.dot(rows, gate_ref[...], preferred_element_type=HIGH)
    up_sum[...] += jnp.dot(rows, up_ref[...], preferred_element_type=HIGH)

    @pl.when(step == pl.num_programs(0) - 1)
    def _():
        gate_act = gate_sum[...]
        hidden = (gate_act / (1.0 + jnp.exp(-gate_act)) * up_sum[...]).astype(LOW)
        columns = jnp.concatenate([r[...] for r in column_refs], axis=0)
        order = order_ref[...]
        count = order.shape[0]
        index = lax.broadcasted_iota(jnp.int32, (count, LANES), 1)
        mine = (lax.rem(index, EXPERTS) == expert_ref[0]) & (index < 3 * EXPERTS)
        for at in range(0, hidden.shape[0], count):
            moved = jnp.dot(order, hidden[at : at + count], preferred_element_type=HIGH)
            hidden_ref[at : at + count, :] = moved.astype(LOW)
            moved = jnp.dot(order, columns[at : at + count], preferred_element_type=HIGH)
            weight = jnp.sum(jnp.where(mine, moved, 0.0), axis=1, keepdims=True)
            weight_ref[at : at + count, :] = jnp.broadcast_to(weight, (count, LANES))


def hidden_of(expert, order, blocks, gate_weight, up_weight):
    width, units = gate_weight.shape
    chunk = width // 4
    rows = sum(block.shape[0] for block in blocks)
    whole = lambda k: (0, 0)
    return pl.pallas_call(
        functools.partial(hidden_kernel, len(blocks)),
        grid=(width // chunk,),
        in_specs=[
            pl.BlockSpec(memory_space=pltpu.SMEM),
            pl.BlockSpec(order.shape, whole),
            *[pl.BlockSpec((block.shape[0], chunk), lambda k: (0, k)) for block in blocks],
            *[pl.BlockSpec((block.shape[0], LANES), lambda k: (0, width // LANES)) for block in blocks],
            pl.BlockSpec((chunk, units), lambda k: (k, 0)),
            pl.BlockSpec((chunk, units), lambda k: (k, 0)),
        ],
        out_specs=[pl.BlockSpec((rows, units), whole), pl.BlockSpec((rows, LANES), whole)],
        out_shape=[
            jax.ShapeDtypeStruct((rows, units), LOW),
            jax.ShapeDtypeStruct((rows, LANES), HIGH),
        ],
        scratch_shapes=[pltpu.VMEM((rows, units), HIGH) for _ in range(2)],
        cost_estimate=pl.CostEstimate(
            flops=2 * rows * width * 2 * units,
            bytes_accessed=2 * width * (rows + 2 * units),
            transcendentals=rows * units,
        ),
        name="hidden",
    )(expert, order, *blocks, *blocks, gate_weight, up_weight)


def partial_kernel(hidden_ref, weight_ref, down_ref, mine_ref, other_ref):
    result = jnp.dot(hidden_ref[...], down_ref[...], preferred_element_type=HIGH)
    result = result * weight_ref[:, :1]
    count = mine_ref.shape[0]
    mine_ref[...] = result[:count]
    other_ref[...] = result[count:].astype(LOW)


def partial_of(hidden, weight, down_weight):
    rows, units = hidden.shape
    width = down_weight.shape[1]
    chunk = width // 4
    whole = lambda k: (0, 0)
    half = pl.BlockSpec((rows // 2, chunk), lambda k: (0, k))
    return pl.pallas_call(
        partial_kernel,
        grid=(width // chunk,),
        in_specs=[
            pl.BlockSpec((rows, units), whole),
            pl.BlockSpec((rows, LANES), whole),
            pl.BlockSpec((units, chunk), lambda k: (0, k)),
        ],
        out_specs=[half, half],
        out_shape=[jax.ShapeDtypeStruct((rows // 2, width), t) for t in (HIGH, LOW)],
        cost_estimate=pl.CostEstimate(
            flops=2 * rows * units * width,
            bytes_accessed=2 * width * (units + 2 * rows),
            transcendentals=0,
        ),
        name="partial",
    )(hidden, weight, down_weight)


def near_sum(kept, pieces):
    got = []
    for piece, k in zip(pieces, (1, -1, 2, -2)):
        got.append(give_to(piece, "ep_1", k))
    total = kept + got[0].astype(HIGH) + got[1].astype(HIGH)
    half = got[2].shape[-2]
    top = total[..., :half, :] + got[2].astype(HIGH) + got[3].astype(HIGH)
    return jnp.concatenate([top, total[..., half:, :]], axis=-2)


def far_sum(rows):
    count = rows.shape[-2] // 4
    total = rows[..., :count, :]
    for i, k in enumerate(FAR):
        piece = rows[..., (i + 1) * count : (i + 2) * count, :]
        total = total + give_to(piece.astype(LOW), "ep_1", k).astype(HIGH)
    return total


def layer(tokens, routes, gates, gate_weight, up_weight, down_weight):
    expert = lax.axis_index(EP) // (lax.axis_size(EP) // EXPERTS)
    expert = expert.astype(jnp.int32).reshape(1)
    order = row_order(tokens.shape[0])

    def hidden_and_partial(blocks):
        with_core = blocks + [other_core(block) for block in blocks]
        hidden = hidden_of(expert, order, with_core, gate_weight, up_weight)

        def partial():
            return partial_of(*hidden, down_weight)

        return partial

    own = jnp.concatenate([tokens, gate_columns(routes, gates)], axis=1)
    near = lax.all_gather(own, "ep_1", axis=0, tiled=True)
    half = near.shape[0] // 2
    up = take_from(near, "ep_0", 1)
    down = take_from(near, "ep_0", -1)
    far_up = take_from(up[:half], "ep_0", 1)
    far_down = take_from(down[half:], "ep_0", -1)
    near_partial = hidden_and_partial([near])
    next_partial = hidden_and_partial([up, down])
    far_partial = hidden_and_partial([far_up, far_down])

    far_mine, far_sent = far_partial()
    far_total = far_mine + other_core(far_sent).astype(HIGH)
    next_mine, next_sent = next_partial()
    next_total = next_mine + other_core(next_sent).astype(HIGH)
    near_mine, near_sent = near_partial()
    near_total = near_mine + other_core(near_sent).astype(HIGH)
    from_down = give_to(far_total[:half].astype(LOW), "ep_0", 1)
    from_up = give_to(far_total[half:].astype(LOW), "ep_0", -1)
    to_up, to_down = next_total[: 2 * half], next_total[2 * half :]
    to_up = jnp.concatenate([to_up[:half] + from_down.astype(HIGH), to_up[half:]], axis=0)
    to_down = jnp.concatenate([to_down[:half], to_down[half:] + from_up.astype(HIGH)], axis=0)
    below = give_to(to_up.astype(LOW), "ep_0", 1)
    above = give_to(to_down.astype(LOW), "ep_0", -1)
    total = near_total + below.astype(HIGH) + above.astype(HIGH)
    n = total.shape[0] // 8
    cut = [total[i * n : j * n].astype(LOW) for i, j in ((2, 4), (4, 6), (6, 7), (7, 8))]
    return far_sum(near_sum(total[: 2 * n], cut)).astype(LOW)


def solution(mesh):
    torus = Mesh(
        mesh.devices.reshape(mesh.shape["groups"], 4, 16, 2), ("groups", "ep_0", "ep_1", "ep_2")
    )
    placed = (
        P(GROUPS_EP, None),
        P(GROUPS_EP, None),
        P(GROUPS_EP, None),
        P(None, EP),
        P(None, EP),
        P(EP, None),
    )
    return jax.shard_map(layer, mesh=torus, in_specs=placed, out_specs=P(GROUPS_EP, None), check_vma=False)
```

profile of v0, /device:TPU:38, one launch (start us, length us, event | category | flops | bytes accessed | tf_op | source)
XLA Modules:
  0.0 195.5 jit_solution(9784005714176561648)
XLA Ops:
  1.7 53.7 %all-gather = bf16[16,4,7296]{2,1,0:T(4,128)(2,1)S(1)} all-gather(bf16[1,4,7296]{2,1,0:T(4,128)(2,1)S(1)} %maximum_bitcast_fusion), channel_id=1, replica_groups=mesh['groups'=2,'ep_0'=4,'ep_1'=16,'ep_2'=2] {'ep_1'}, dimensions={0}, use_global_device_ids=true | all-gather | bytes 992256 | tf_op jit(solution)/shard_map/all_gather | solution.py:183
  55.8 2.0 %collective-permute-start.2 = (bf16[64,7296]{1,0:T(8,128)(2,1)S(1)}, bf16[64,7296]{1,0:T(8,128)(2,1)S(1)}, u32[]{:S(2)}, u32[]{:S(2)}) collective-permute-start(bf16[64,7296]{1,0:T(8,128)(2,1)S(1)} %reshape.23.refs_0_.refs_2_), channel_id=1, source_target_pairs={{32,0},{64,32},{96,64},{0,96},{33,1},{65,33},{97,65},{1,97},{34,2}... | collective-permute-start | bytes 2801672 | tf_op jit(solution)/shard_map/ppermute | solution.py:23
  57.8 17.8 %collective-permute-done.3.refs_1_.refs_5_ = bf16[64,7296]{1,0:T(8,128)(2,1)S(1)} collective-permute-done((bf16[64,7296]{1,0:T(8,128)(2,1)S(1)}, bf16[64,7296]{1,0:T(8,128)(2,1)S(1)}, u32[]{:S(2)}, u32[]{:S(2)}) %collective-permute-start.3) | collective-permute-done | bytes 933920 | tf_op jit(solution)/shard_map/ppermute | solution.py:23
  77.4 2.0 %collective-permute-start.7 = (bf16[32,7296]{1,0:T(8,128)(2,1)}, bf16[32,7296]{1,0:T(8,128)(2,1)}, u32[]{:S(2)}, u32[]{:S(2)}) collective-permute-start(bf16[32,7296]{1,0:T(8,128)(2,1)} %slice.93), channel_id=1, source_target_pairs={{32,0},{64,32},{96,64},{0,96},{33,1},{65,33},{97,65},{1,97},{34,2}... | collective-permute-start | bytes 1400840 | tf_op jit(solution)/shard_map/ppermute | solution.py:23
  79.3 5.9 %collective-permute-done.8.refs_1_.refs_5_ = bf16[32,7296]{1,0:T(8,128)(2,1)S(1)} collective-permute-done((bf16[32,7296]{1,0:T(8,128)(2,1)}, bf16[32,7296]{1,0:T(8,128)(2,1)S(1)}, u32[]{:S(2)}, u32[]{:S(2)}) %collective-permute-start.8) | collective-permute-done | bytes 466976 | tf_op jit(solution)/shard_map/ppermute | solution.py:23
  85.2 2.3 %collective-permute-done.7.refs_0_.refs_4_ = bf16[32,7296]{1,0:T(8,128)(2,1)} collective-permute-done((bf16[32,7296]{1,0:T(8,128)(2,1)}, bf16[32,7296]{1,0:T(8,128)(2,1)}, u32[]{:S(2)}, u32[]{:S(2)}) %collective-permute-start.7) | collective-permute-done | bytes 466976 | tf_op jit(solution)/shard_map/ppermute | solution.py:23
  89.6 6.0 %hidden.5 = (bf16[128,256]{1,0:T(8,128)(2,1)}, f32[128,128]{1,0:T(8,128)}) custom-call(s32[1]{0:T(128)} %bitcast.expert_ref, bf16[64,64]{1,0:T(8,128)(2,1)} %fusion.7.order_ref, bf16[32,7296]{1,0:T(8,128)(2,1)} %collective-permute-done.7.refs_0_.refs_4_, bf16[32,7296]{1,0:T(8,128)(2,1)} %copy-done.4, ...), custom_call_target="tpu_custom_call" | custom-call | flops 939524096 | bytes 9175040 | tf_op jit(solution)/shard_map/hidden/pallas_call | solution.py:90
  95.7 4.8 %partial.5 = (f32[64,7168]{1,0:T(8,128)}, bf16[64,7168]{1,0:T(8,128)(2,1)}) custom-call(bf16[128,256]{1,0:T(8,128)(2,1)} %get-tuple-element.25.hidden_ref, f32[128,128]{1,0:T(8,128)} %get-tuple-element.26.weight_ref, bf16[256,7168]{1,0:T(8,128)(2,1)} %down_ref.5), custom_call_target="tpu_custom_call" | custom-call | flops 469762048 | bytes 7340032 | tf_op jit(solution)/shard_map/partial/pallas_call | solution.py:130
  100.6 6.0 %hidden.3 = (bf16[128,256]{1,0:T(8,128)(2,1)}, f32[128,128]{1,0:T(8,128)}) custom-call(s32[1]{0:T(128)} %bitcast.expert_ref, bf16[64,64]{1,0:T(8,128)(2,1)} %fusion.7.order_ref, bf16[64,7296]{1,0:T(8,128)(2,1)} %copy-done, bf16[64,7296]{1,0:T(8,128)(2,1)} %collective-permute-done.refs_1_.refs_3_, bf16[64,7296]{1,0:T(8,128)(2,1)} %copy-done, ...), custom_call_target="tpu_custom_call" | custom-call | flops 939524096 | bytes 9175040 | tf_op jit(solution)/shard_map/hidden/pallas_call | solution.py:90
  106.5 4.9 %partial.3 = (f32[64,7168]{1,0:T(8,128)}, bf16[64,7168]{1,0:T(8,128)(2,1)}) custom-call(bf16[128,256]{1,0:T(8,128)(2,1)} %get-tuple-element.17.hidden_ref, f32[128,128]{1,0:T(8,128)} %get-tuple-element.18.weight_ref, bf16[256,7168]{1,0:T(8,128)(2,1)} %down_ref.5), custom_call_target="tpu_custom_call" | custom-call | flops 469762048 | bytes 7340032 | tf_op jit(solution)/shard_map/partial/pallas_call | solution.py:130
  111.8 7.0 %hidden.4 = (bf16[256,256]{1,0:T(8,128)(2,1)}, f32[256,128]{1,0:T(8,128)}) custom-call(s32[1]{0:T(128)} %bitcast.expert_ref, bf16[64,64]{1,0:T(8,128)(2,1)} %fusion.7.order_ref, bf16[64,7296]{1,0:T(8,128)(2,1)} %copy-done.2, bf16[64,7296]{1,0:T(8,128)(2,1)} %copy-done.1, bf16[64,7296]{1,0:T(8,128)(2,1)} %collective-permute-done.4.refs_2_.refs_6_, ...), custom_call_target="tpu_custom_call" | custom-call | flops 1879048192 | bytes 11010048 | tf_op jit(solution)/shard_map/hidden/pallas_call | solution.py:90
  118.9 5.8 %partial.4 = (f32[128,7168]{1,0:T(8,128)}, bf16[128,7168]{1,0:T(8,128)(2,1)}) custom-call(bf16[256,256]{1,0:T(8,128)(2,1)} %get-tuple-element.21.hidden_ref, f32[256,128]{1,0:T(8,128)} %get-tuple-element.22.weight_ref, bf16[256,7168]{1,0:T(8,128)(2,1)} %down_ref.5), custom_call_target="tpu_custom_call" | custom-call | flops 939524096 | bytes 11010048 | tf_op jit(solution)/shard_map/partial/pallas_call | solution.py:130
  126.8 1.9 collective-permute-start.14
  129.3 10.1 %collective-permute-done.12 = bf16[32,7168]{1,0:T(8,128)(2,1)S(1)} collective-permute-done((bf16[32,7168]{1,0:T(8,128)(2,1)S(1)}, bf16[32,7168]{1,0:T(8,128)(2,1)S(1)}, u32[]{:S(2)}, u32[]{:S(2)}) %collective-permute-start.12) | collective-permute-done | bytes 458784 | tf_op jit(solution)/shard_map/ppermute | solution.py:28
  141.6 1.7 collective-permute-start.15
  143.4 19.6 %collective-permute-done.13 = bf16[64,7168]{1,0:T(8,128)(2,1)S(1)} collective-permute-done((bf16[64,7168]{1,0:T(8,128)(2,1)S(1)}, bf16[64,7168]{1,0:T(8,128)(2,1)S(1)}, u32[]{:S(2)}, u32[]{:S(2)}) %collective-permute-start.13) | collective-permute-done | bytes 917536 | tf_op jit(solution)/shard_map/ppermute | solution.py:28
  166.2 3.2 %collective-permute-start.17 = (bf16[16,7168]{1,0:T(8,128)(2,1)S(1)}, bf16[16,7168]{1,0:T(8,128)(2,1)S(1)}, u32[]{:S(2)}, u32[]{:S(2)}) collective-permute-start(bf16[16,7168]{1,0:T(8,128)(2,1)S(1)} %get-tuple-element.42), channel_id=1, source_target_pairs={{0,30},{2,0},{4,2},{6,4},{8,6},{10,8},{12,10},{14,12},{16,14},{18,... | collective-permute-start | bytes 688136 | tf_op jit(solution)/shard_map/ppermute | solution.py:28
  169.6 4.1 %collective-permute-start.19 = (bf16[8,7168]{1,0:T(8,128)(2,1)S(1)}, bf16[8,7168]{1,0:T(8,128)(2,1)S(1)}, u32[]{:S(2)}, u32[]{:S(2)}) collective-permute-start(bf16[8,7168]{1,0:T(8,128)(2,1)S(1)} %get-tuple-element.40), channel_id=1, source_target_pairs={{0,28},{2,30},{4,0},{6,2},{8,4},{10,6},{12,8},{14,10},{16,12},{18,... | collective-permute-start | bytes 344072 | tf_op jit(solution)/shard_map/ppermute | solution.py:28
  173.7 2.6 %collective-permute-done.16 = bf16[16,7168]{1,0:T(8,128)(2,1)S(1)} collective-permute-done((bf16[16,7168]{1,0:T(8,128)(2,1)S(1)}, bf16[16,7168]{1,0:T(8,128)(2,1)S(1)}, u32[]{:S(2)}, u32[]{:S(2)}) %collective-permute-start.16) | collective-permute-done | bytes 229408 | tf_op jit(solution)/shard_map/ppermute | solution.py:28
  177.7 3.8 %collective-permute-start.20 = (bf16[4,7168]{1,0:T(4,128)(2,1)S(1)}, bf16[4,7168]{1,0:T(4,128)(2,1)S(1)}, u32[]{:S(2)}, u32[]{:S(2)}) collective-permute-start(bf16[4,7168]{1,0:T(4,128)(2,1)S(1)} %slice.130), channel_id=1, source_target_pairs={{0,16},{2,18},{4,20},{6,22},{8,24},{10,26},{12,28},{14,30},{16,0},... | collective-permute-start | bytes 172040 | tf_op jit(solution)/shard_map/ppermute | solution.py:28
  181.6 4.2 %collective-permute-start.21 = (bf16[4,7168]{1,0:T(4,128)(2,1)S(1)}, bf16[4,7168]{1,0:T(4,128)(2,1)S(1)}, u32[]{:S(2)}, u32[]{:S(2)}) collective-permute-start(bf16[4,7168]{1,0:T(4,128)(2,1)S(1)} %get-tuple-element.45), channel_id=1, source_target_pairs={{0,8},{2,10},{4,12},{6,14},{8,16},{10,18},{12,20},{14,22},{16,24},... | collective-permute-start | bytes 172040 | tf_op jit(solution)/shard_map/ppermute | solution.py:28
  185.8 1.9 collective-permute-start.22
  187.6 5.4 %collective-permute-done.20 = bf16[4,7168]{1,0:T(4,128)(2,1)S(1)} collective-permute-done((bf16[4,7168]{1,0:T(4,128)(2,1)S(1)}, bf16[4,7168]{1,0:T(4,128)(2,1)S(1)}, u32[]{:S(2)}, u32[]{:S(2)}) %collective-permute-start.20) | collective-permute-done | bytes 57376 | tf_op jit(solution)/shard_map/ppermute | solution.py:28
  193.0 1.8 collective-permute-done.22
  (71 shorter events, 17.0 us)
Async XLA Ops:
  55.6 40.0 %copy-start = (bf16[64,7296]{1,0:T(8,128)(2,1)}, bf16[64,7296]{1,0:T(8,128)(2,1)S(1)}, u32[]{:S(2)}) copy-start(bf16[64,7296]{1,0:T(8,128)(2,1)S(1)} %reshape.23.refs_0_.refs_2_) | copy-start | bytes 2801668
  55.6 19.9 %collective-permute-start.3 = (bf16[64,7296]{1,0:T(8,128)(2,1)S(1)}, bf16[64,7296]{1,0:T(8,128)(2,1)S(1)}, u32[]{:S(2)}, u32[]{:S(2)}) collective-permute-start(bf16[64,7296]{1,0:T(8,128)(2,1)S(1)} %reshape.23.refs_0_.refs_2_), channel_id=1, source_target_pairs={{96,0},{0,32},{32,64},{64,96},{97,1},{1,33},{33,65},{65,97},{98,2}... | collective-permute-start | bytes 2801672 | tf_op jit(solution)/shard_map/ppermute | solution.py:23
  55.8 20.7 %collective-permute-start.2 = (bf16[64,7296]{1,0:T(8,128)(2,1)S(1)}, bf16[64,7296]{1,0:T(8,128)(2,1)S(1)}, u32[]{:S(2)}, u32[]{:S(2)}) collective-permute-start(bf16[64,7296]{1,0:T(8,128)(2,1)S(1)} %reshape.23.refs_0_.refs_2_), channel_id=1, source_target_pairs={{32,0},{64,32},{96,64},{0,96},{33,1},{65,33},{97,65},{1,97},{34,2}... | collective-permute-start | bytes 2801672 | tf_op jit(solution)/shard_map/ppermute | solution.py:23
  76.4 8.8 %collective-permute-start.8 = (bf16[32,7296]{1,0:T(8,128)(2,1)}, bf16[32,7296]{1,0:T(8,128)(2,1)S(1)}, u32[]{:S(2)}, u32[]{:S(2)}) collective-permute-start(bf16[32,7296]{1,0:T(8,128)(2,1)} %slice.94), channel_id=1, source_target_pairs={{96,0},{0,32},{32,64},{64,96},{97,1},{1,33},{33,65},{65,97},{98,2}... | collective-permute-start | bytes 1400840 | tf_op jit(solution)/shard_map/ppermute | solution.py:23
  77.4 10.1 %collective-permute-start.7 = (bf16[32,7296]{1,0:T(8,128)(2,1)}, bf16[32,7296]{1,0:T(8,128)(2,1)}, u32[]{:S(2)}, u32[]{:S(2)}) collective-permute-start(bf16[32,7296]{1,0:T(8,128)(2,1)} %slice.93), channel_id=1, source_target_pairs={{32,0},{64,32},{96,64},{0,96},{33,1},{65,33},{97,65},{1,97},{34,2}... | collective-permute-start | bytes 1400840 | tf_op jit(solution)/shard_map/ppermute | solution.py:23
  79.3 21.2 %collective-permute-start = (bf16[64,7296]{1,0:T(8,128)(2,1)S(1)}, bf16[64,7296]{1,0:T(8,128)(2,1)}, u32[]{:S(2)}, u32[]{:S(2)}) collective-permute-start(bf16[64,7296]{1,0:T(8,128)(2,1)S(1)} %reshape.23.refs_0_.refs_2_), channel_id=1, source_target_pairs={{0,1},{1,0},{2,3},{3,2},{4,5},{5,4},{6,7},{7,6},{8,9},{9,8},{10,11... | collective-permute-start | bytes 2801672 | tf_op jit(solution)/shard_map/ppermute | solution.py:28
  85.2 3.9 %collective-permute-start.10 = (bf16[32,7296]{1,0:T(8,128)(2,1)S(1)}, bf16[32,7296]{1,0:T(8,128)(2,1)}, u32[]{:S(2)}, u32[]{:S(2)}) collective-permute-start(bf16[32,7296]{1,0:T(8,128)(2,1)S(1)} %collective-permute-done.8.refs_1_.refs_5_), channel_id=1, source_target_pairs={{0,1},{1,0},{2,3},{3,2},{4,5},{5,4},{6,7},{7,6},{8,9},{9,8},{10,11... | collective-permute-start | bytes 1400840 | tf_op jit(solution)/shard_map/ppermute | solution.py:28
  87.5 2.2 %collective-permute-start.9 = (bf16[32,7296]{1,0:T(8,128)(2,1)}, bf16[32,7296]{1,0:T(8,128)(2,1)}, u32[]{:S(2)}, u32[]{:S(2)}) collective-permute-start(bf16[32,7296]{1,0:T(8,128)(2,1)} %collective-permute-done.7.refs_0_.refs_4_), channel_id=1, source_target_pairs={{0,1},{1,0},{2,3},{3,2},{4,5},{5,4},{6,7},{7,6},{8,9},{9,8},{10,11... | collective-permute-start | bytes 1400840 | tf_op jit(solution)/shard_map/ppermute | solution.py:28
  87.7 24.1 %collective-permute-start.4 = (bf16[64,7296]{1,0:T(8,128)(2,1)S(1)}, bf16[64,7296]{1,0:T(8,128)(2,1)}, u32[]{:S(2)}, u32[]{:S(2)}) collective-permute-start(bf16[64,7296]{1,0:T(8,128)(2,1)S(1)} %collective-permute-done.2.refs_0_.refs_4_), channel_id=1, source_target_pairs={{0,1},{1,0},{2,3},{3,2},{4,5},{5,4},{6,7},{7,6},{8,9},{9,8},{10,11... | collective-permute-start | bytes 2801672 | tf_op jit(solution)/shard_map/ppermute | solution.py:28
  88.3 23.5 %collective-permute-start.5 = (bf16[64,7296]{1,0:T(8,128)(2,1)S(1)}, bf16[64,7296]{1,0:T(8,128)(2,1)}, u32[]{:S(2)}, u32[]{:S(2)}) collective-permute-start(bf16[64,7296]{1,0:T(8,128)(2,1)S(1)} %collective-permute-done.3.refs_1_.refs_5_), channel_id=1, source_target_pairs={{0,1},{1,0},{2,3},{3,2},{4,5},{5,4},{6,7},{7,6},{8,9},{9,8},{10,11... | collective-permute-start | bytes 2801672 | tf_op jit(solution)/shard_map/ppermute | solution.py:28
  100.4 24.4 %collective-permute-start.11 = (bf16[64,7168]{1,0:T(8,128)(2,1)}, bf16[64,7168]{1,0:T(8,128)(2,1)}, u32[]{:S(2)}, u32[]{:S(2)}) collective-permute-start(bf16[64,7168]{1,0:T(8,128)(2,1)} %get-tuple-element.28), channel_id=1, source_target_pairs={{0,1},{1,0},{2,3},{3,2},{4,5},{5,4},{6,7},{7,6},{8,9},{9,8},{10,11... | collective-permute-start | bytes 2752520 | tf_op jit(solution)/shard_map/ppermute | solution.py:28
  111.4 31.9 %collective-permute-start.1 = (bf16[64,7168]{1,0:T(8,128)(2,1)}, bf16[64,7168]{1,0:T(8,128)(2,1)}, u32[]{:S(2)}, u32[]{:S(2)}) collective-permute-start(bf16[64,7168]{1,0:T(8,128)(2,1)} %get-tuple-element.20), channel_id=1, source_target_pairs={{0,1},{1,0},{2,3},{3,2},{4,5},{5,4},{6,7},{7,6},{8,9},{9,8},{10,11... | collective-permute-start | bytes 2752520 | tf_op jit(solution)/shard_map/ppermute | solution.py:28
  124.7 4.0 %collective-permute-start.6 = (bf16[128,7168]{1,0:T(8,128)(2,1)}, bf16[128,7168]{1,0:T(8,128)(2,1)S(1)}, u32[]{:S(2)}, u32[]{:S(2)}) collective-permute-start(bf16[128,7168]{1,0:T(8,128)(2,1)} %get-tuple-element.24), channel_id=1, source_target_pairs={{0,1},{1,0},{2,3},{3,2},{4,5},{5,4},{6,7},{7,6},{8,9},{9,8},{10,11... | collective-permute-start | bytes 5505032 | tf_op jit(solution)/shard_map/ppermute | solution.py:28
  126.4 13.1 %collective-permute-start.12 = (bf16[32,7168]{1,0:T(8,128)(2,1)S(1)}, bf16[32,7168]{1,0:T(8,128)(2,1)S(1)}, u32[]{:S(2)}, u32[]{:S(2)}) collective-permute-start(bf16[32,7168]{1,0:T(8,128)(2,1)S(1)} %get-tuple-element.43), channel_id=1, source_target_pairs={{0,32},{32,64},{64,96},{96,0},{1,33},{33,65},{65,97},{97,1},{2,34}... | collective-permute-start | bytes 1376264 | tf_op jit(solution)/shard_map/ppermute | solution.py:28
  126.8 14.1 %collective-permute-start.14 = (bf16[32,7168]{1,0:T(8,128)(2,1)S(1)}, bf16[32,7168]{1,0:T(8,128)(2,1)S(1)}, u32[]{:S(2)}, u32[]{:S(2)}) collective-permute-start(bf16[32,7168]{1,0:T(8,128)(2,1)S(1)} %get-tuple-element.44), channel_id=1, source_target_pairs={{0,96},{32,0},{64,32},{96,64},{1,97},{33,1},{65,33},{97,65},{2,98}... | collective-permute-start | bytes 1376264 | tf_op jit(solution)/shard_map/ppermute | solution.py:28
  141.1 21.9 %collective-permute-start.13 = (bf16[64,7168]{1,0:T(8,128)(2,1)S(1)}, bf16[64,7168]{1,0:T(8,128)(2,1)S(1)}, u32[]{:S(2)}, u32[]{:S(2)}) collective-permute-start(bf16[64,7168]{1,0:T(8,128)(2,1)S(1)} %pad_maximum_fusion), channel_id=1, source_target_pairs={{0,32},{32,64},{64,96},{96,0},{1,33},{33,65},{65,97},{97,1},{2,34}... | collective-permute-start | bytes 2752520 | tf_op jit(solution)/shard_map/ppermute | solution.py:28
  141.6 22.8 %collective-permute-start.15 = (bf16[64,7168]{1,0:T(8,128)(2,1)S(1)}, bf16[64,7168]{1,0:T(8,128)(2,1)S(1)}, u32[]{:S(2)}, u32[]{:S(2)}) collective-permute-start(bf16[64,7168]{1,0:T(8,128)(2,1)S(1)} %pad_maximum_fusion.1), channel_id=1, source_target_pairs={{0,96},{32,0},{64,32},{96,64},{1,97},{33,1},{65,33},{97,65},{2,98}... | collective-permute-start | bytes 2752520 | tf_op jit(solution)/shard_map/ppermute | solution.py:28
  166.1 10.2 %collective-permute-start.16 = (bf16[16,7168]{1,0:T(8,128)(2,1)S(1)}, bf16[16,7168]{1,0:T(8,128)(2,1)S(1)}, u32[]{:S(2)}, u32[]{:S(2)}) collective-permute-start(bf16[16,7168]{1,0:T(8,128)(2,1)S(1)} %get-tuple-element.41), channel_id=1, source_target_pairs={{0,2},{2,4},{4,6},{6,8},{8,10},{10,12},{12,14},{14,16},{16,18},{18... | collective-permute-start | bytes 688136 | tf_op jit(solution)/shard_map/ppermute | solution.py:28
  166.2 10.2 %collective-permute-start.17 = (bf16[16,7168]{1,0:T(8,128)(2,1)S(1)}, bf16[16,7168]{1,0:T(8,128)(2,1)S(1)}, u32[]{:S(2)}, u32[]{:S(2)}) collective-permute-start(bf16[16,7168]{1,0:T(8,128)(2,1)S(1)} %get-tuple-element.42), channel_id=1, source_target_pairs={{0,30},{2,0},{4,2},{6,4},{8,6},{10,8},{12,10},{14,12},{16,14},{18,... | collective-permute-start | bytes 688136 | tf_op jit(solution)/shard_map/ppermute | solution.py:28
  169.4 8.1 %collective-permute-start.18 = (bf16[8,7168]{1,0:T(8,128)(2,1)S(1)}, bf16[8,7168]{1,0:T(8,128)(2,1)S(1)}, u32[]{:S(2)}, u32[]{:S(2)}) collective-permute-start(bf16[8,7168]{1,0:T(8,128)(2,1)S(1)} %get-tuple-element.39), channel_id=1, source_target_pairs={{0,4},{2,6},{4,8},{6,10},{8,12},{10,14},{12,16},{14,18},{16,20},{1... | collective-permute-start | bytes 344072 | tf_op jit(solution)/shard_map/ppermute | solution.py:28
  169.6 8.1 %collective-permute-start.19 = (bf16[8,7168]{1,0:T(8,128)(2,1)S(1)}, bf16[8,7168]{1,0:T(8,128)(2,1)S(1)}, u32[]{:S(2)}, u32[]{:S(2)}) collective-permute-start(bf16[8,7168]{1,0:T(8,128)(2,1)S(1)} %get-tuple-element.40), channel_id=1, source_target_pairs={{0,28},{2,30},{4,0},{6,2},{8,4},{10,6},{12,8},{14,10},{16,12},{18,... | collective-permute-start | bytes 344072 | tf_op jit(solution)/shard_map/ppermute | solution.py:28
  177.7 15.3 %collective-permute-start.20 = (bf16[4,7168]{1,0:T(4,128)(2,1)S(1)}, bf16[4,7168]{1,0:T(4,128)(2,1)S(1)}, u32[]{:S(2)}, u32[]{:S(2)}) collective-permute-start(bf16[4,7168]{1,0:T(4,128)(2,1)S(1)} %slice.130), channel_id=1, source_target_pairs={{0,16},{2,18},{4,20},{6,22},{8,24},{10,26},{12,28},{14,30},{16,0},... | collective-permute-start | bytes 172040 | tf_op jit(solution)/shard_map/ppermute | solution.py:28
  181.6 11.4 %collective-permute-start.21 = (bf16[4,7168]{1,0:T(4,128)(2,1)S(1)}, bf16[4,7168]{1,0:T(4,128)(2,1)S(1)}, u32[]{:S(2)}, u32[]{:S(2)}) collective-permute-start(bf16[4,7168]{1,0:T(4,128)(2,1)S(1)} %get-tuple-element.45), channel_id=1, source_target_pairs={{0,8},{2,10},{4,12},{6,14},{8,16},{10,18},{12,20},{14,22},{16,24},... | collective-permute-start | bytes 172040 | tf_op jit(solution)/shard_map/ppermute | solution.py:28
  185.8 9.0 %collective-permute-start.22 = (bf16[4,7168]{1,0:T(4,128)(2,1)S(1)}, bf16[4,7168]{1,0:T(4,128)(2,1)S(1)}, u32[]{:S(2)}, u32[]{:S(2)}) collective-permute-start(bf16[4,7168]{1,0:T(4,128)(2,1)S(1)} %get-tuple-element.46), channel_id=1, source_target_pairs={{0,24},{2,26},{4,28},{6,30},{8,0},{10,2},{12,4},{14,6},{16,8},{18,... | collective-permute-start | bytes 172040 | tf_op jit(solution)/shard_map/ppermute | solution.py:28
  (7 other events, 109.0 us)
where the time goes:
time: 196 us; the launch traced here: 195 us
  waiting for transfers between devices  70 us (36%)
  blocking collectives  53.7 us (27%)
  Pallas kernels  34.5 us (18%)
  starting transfers between devices  27.6 us (14%)
  other arithmetic  7.19 us (4%)
  local copies, waits for them, and re-layouts  2.32 us (1%)
    all_gather x1, blocking collectives, layer(): near = lax.all_gather(own, 'ep_1', axis=0, tiled=True)  53.7 us
    ppermute x19, waiting for transfers between devices, give_to(): lax.ppermute(value, axis, [(i, (i + offset) % count) for i in range(count)])  44.1 us
    ppermute x4, waiting for transfers between devices, take_from(): lax.ppermute(value, axis, [((i + offset) % count, i) for i in range(count)])  25.9 us
    ppermute x19, starting transfers between devices, give_to(): lax.ppermute(value, axis, [(i, (i + offset) % count) for i in range(count)])  23.4 us
    pallas_call x3, Pallas kernels, hidden_of(): pl.pallas_call(functools.partial(hidden_kernel, len(blocks)), grid=(width...  19 us
    pallas_call x3, Pallas kernels, partial_of(): pl.pallas_call(partial_kernel, grid=(width // chunk,), in_specs=[pl.Block...  15.5 us
    ppermute x4, starting transfers between devices, take_from(): lax.ppermute(value, axis, [((i + offset) % count, i) for i in range(count)])  4.16 us
  transfers between devices with their start and end apart: 23, of which 14 were waited for; matrix products, arithmetic and copies ran while one was open for 3% of the time, Pallas kernels for 18%

commit v1 on v0

v1 whole, which is shorter than its diff:
```python
import functools

import jax
import jax.numpy as jnp
from jax import lax
from jax.experimental import pallas as pl
from jax.experimental.pallas import tpu as pltpu
from jax.sharding import Mesh
from jax.sharding import PartitionSpec as P


EXPERTS = 16
LANES = 128
EP = ("ep_0", "ep_1", "ep_2")
GROUPS_EP = ("groups", "ep_0", "ep_1", "ep_2")
FAR = (8, 4, 12)
Z_OFFSETS = (0, 8, 4, 12, 1, 9, 5, 13, 15, 7, 3, 11, 2, 10, 14, 6)
LOW, HIGH = jnp.bfloat16, jnp.float32


def take_from(value, axis, offset):
    count = lax.axis_size(axis)
    return lax.ppermute(value, axis, [((i + offset) % count, i) for i in range(count)])


def give_to(value, axis, offset):
    count = lax.axis_size(axis)
    return lax.ppermute(value, axis, [(i, (i + offset) % count) for i in range(count)])


def other_core(value):
    return give_to(value, "ep_2", 1)


def gate_columns(routes, gates):
    member = routes[:, :, None] == jnp.arange(EXPERTS, dtype=routes.dtype)
    left = jnp.sum(jnp.where(member, gates[:, :, None], 0.0), axis=1)
    parts = []
    for _ in range(3):
        part = lax.reduce_precision(left, 8, 7)
        parts.append(part.astype(LOW))
        left = left - part
    columns = jnp.concatenate(parts, axis=1)
    return jnp.pad(columns, ((0, 0), (0, LANES - columns.shape[1])))


def row_order(tok_rows):
    count = lax.axis_size("ep_1")
    wanted = (lax.axis_index("ep_1") + jnp.array(Z_OFFSETS, jnp.int32)) % count
    wanted = (wanted[:, None] * tok_rows + jnp.arange(tok_rows, dtype=jnp.int32)).reshape(-1)
    return (wanted[:, None] == jnp.arange(count * tok_rows, dtype=jnp.int32)).astype(LOW)


def expert_kernel(blocks, steps, expert_ref, order_ref, *refs):
    row_refs, column_refs = refs[:blocks], refs[blocks : 2 * blocks]
    gate_ref, up_ref, down_ref, mine_ref, other_ref = refs[2 * blocks : 2 * blocks + 5]
    gate_sum, up_sum, hidden_ref, weight_ref = refs[2 * blocks + 5 :]
    step = pl.program_id(0)

    @pl.when(step == 0)
    def _():
        gate_sum[...] = jnp.zeros_like(gate_sum)
        up_sum[...] = jnp.zeros_like(up_sum)

    @pl.when(step < steps)
    def _():
        rows = jnp.concatenate([r[...] for r in row_refs], axis=0)
        gate_sum[...] += jnp.dot(rows, gate_ref[...], preferred_element_type=HIGH)
        up_sum[...] += jnp.dot(rows, up_ref[...], preferred_element_type=HIGH)

    @pl.when(step == steps - 1)
    def _():
        gate_act = gate_sum[...]
        hidden = (gate_act / (1.0 + jnp.exp(-gate_act)) * up_sum[...]).astype(LOW)
        columns = jnp.concatenate([r[...] for r in column_refs], axis=0)
        order = order_ref[...]
        count = order.shape[0]
        index = lax.broadcasted_iota(jnp.int32, (count, LANES), 1)
        mine = (lax.rem(index, EXPERTS) == expert_ref[0]) & (index < 3 * EXPERTS)
        for at in range(0, hidden.shape[0], count):
            moved = jnp.dot(order, hidden[at : at + count], preferred_element_type=HIGH)
            hidden_ref[at : at + count, :] = moved.astype(LOW)
            moved = jnp.dot(order, columns[at : at + count], preferred_element_type=HIGH)
            weight = jnp.sum(jnp.where(mine, moved, 0.0), axis=1, keepdims=True)
            weight_ref[at : at + count, :] = jnp.broadcast_to(weight, (count, LANES))

    @pl.when(step >= steps)
    def _():
        result = jnp.dot(hidden_ref[...], down_ref[...], preferred_element_type=HIGH)
        result = result * weight_ref[:, :1]
        count = mine_ref.shape[0]
        mine_ref[...] = result[:count]
        other_ref[...] = result[count:].astype(LOW)


def expert_of(expert, order, blocks, gate_weight, up_weight, down_weight):
    width, units = gate_weight.shape
    steps = 4
    chunk = width // steps
    rows = sum(block.shape[0] for block in blocks)
    whole = lambda k: (0, 0)
    first = lambda k: jnp.minimum(k, steps - 1)
    second = lambda k: jnp.maximum(k - steps, 0)
    half = pl.BlockSpec((rows // 2, chunk), lambda k: (0, second(k)))
    return pl.pallas_call(
        functools.partial(expert_kernel, len(blocks), steps),
        grid=(2 * steps,),
        in_specs=[
            pl.BlockSpec(memory_space=pltpu.SMEM),
            pl.BlockSpec(order.shape, whole),
            *[pl.BlockSpec((block.shape[0], chunk), lambda k: (0, first(k))) for block in blocks],
            *[pl.BlockSpec((block.shape[0], LANES), lambda k: (0, width // LANES)) for block in blocks],
            pl.BlockSpec((chunk, units), lambda k: (first(k), 0)),
            pl.BlockSpec((chunk, units), lambda k: (first(k), 0)),
            pl.BlockSpec((units, chunk), lambda k: (0, second(k))),
        ],
        out_specs=[half, half],
        out_shape=[jax.ShapeDtypeStruct((rows // 2, width), t) for t in (HIGH, LOW)],
        scratch_shapes=[
            pltpu.VMEM((rows, units), HIGH),
            pltpu.VMEM((rows, units), HIGH),
            pltpu.VMEM((rows, units), LOW),
            pltpu.VMEM((rows, LANES), HIGH),
        ],
        cost_estimate=pl.CostEstimate(
            flops=2 * rows * width * 3 * units,
            bytes_accessed=2 * width * (3 * rows + 3 * units),
            transcendentals=rows * units,
        ),
        name="expert",
    )(expert, order, *blocks, *blocks, gate_weight, up_weight, down_weight)


def near_sum(kept, pieces):
    got = []
    for piece, k in zip(pieces, (1, -1, 2, -2)):
        got.append(give_to(piece, "ep_1", k))
    total = kept + got[0].astype(HIGH) + got[1].astype(HIGH)
    half = got[2].shape[-2]
    top = total[..., :half, :] + got[2].astype(HIGH) + got[3].astype(HIGH)
    return jnp.concatenate([top, total[..., half:, :]], axis=-2)


def far_sum(rows):
    count = rows.shape[-2] // 4
    total = rows[..., :count, :]
    for i, k in enumerate(FAR):
        piece = rows[..., (i + 1) * count : (i + 2) * count, :]
        total = total + give_to(piece.astype(LOW), "ep_1", k).astype(HIGH)
    return total


def layer(tokens, routes, gates, gate_weight, up_weight, down_weight):
    expert = lax.axis_index(EP) // (lax.axis_size(EP) // EXPERTS)
    expert = expert.astype(jnp.int32).reshape(1)
    order = row_order(tokens.shape[0])

    def total_of(blocks):
        with_core = blocks + [other_core(block) for block in blocks]
        mine, sent = expert_of(expert, order, with_core, gate_weight, up_weight, down_weight)
        got = other_core(sent)
        return mine + got.astype(HIGH)

    def moved(value, move, offset):
        return move(value.astype(LOW), "ep_0", offset)

    own = jnp.concatenate([tokens, gate_columns(routes, gates)], axis=1)
    near = lax.all_gather(own, "ep_1", axis=0, tiled=True)
    half = near.shape[0] // 2
    up = moved(near, take_from, 1)
    down = moved(near, take_from, -1)
    far_up = moved(up[:half], take_from, 1)
    far_down = moved(down[half:], take_from, -1)

    near_total = total_of([near])
    next_total = total_of([up, down])
    to_up, to_down = next_total[: 2 * half], next_total[2 * half :]
    below_b = moved(to_up[half:], give_to, 1)
    above_b = moved(to_down[:half], give_to, -1)
    far_total = total_of([far_up, far_down])
    from_below = moved(far_total[:half], give_to, 1)
    from_above = moved(far_total[half:], give_to, -1)
    below_a = moved(to_up[:half] + from_below.astype(HIGH), give_to, 1)
    above_a = moved(to_down[half:] + from_above.astype(HIGH), give_to, -1)
    top = near_total[:half] + above_b.astype(HIGH) + below_a.astype(HIGH)
    bottom = near_total[half:] + below_b.astype(HIGH) + above_a.astype(HIGH)
    total = jnp.concatenate([top, bottom], axis=0)
    n = total.shape[0] // 8
    cut = [total[i * n : j * n].astype(LOW) for i, j in ((2, 4), (4, 6), (6, 7), (7, 8))]
    return far_sum(near_sum(total[: 2 * n], cut)).astype(LOW)


def solution(mesh):
    torus = Mesh(
        mesh.devices.reshape(mesh.shape["groups"], 4, 16, 2), ("groups", "ep_0", "ep_1", "ep_2")
    )
    placed = (
        P(GROUPS_EP, None),
        P(GROUPS_EP, None),
        P(GROUPS_EP, None),
        P(None, EP),
        P(None, EP),
        P(EP, None),
    )
    return jax.shard_map(layer, mesh=torus, in_specs=placed, out_specs=P(GROUPS_EP, None), check_vma=False)
```

time: 196 us -> 195 us (level)
  starting transfers between devices: 27.6 us -> 34 us
  waiting for transfers between devices: 70 us -> 65.8 us
  Pallas kernels: 34.5 us -> 31.5 us
    ppermute x19 -> x21, starting transfers between devices: 23.4 us -> 27.4 us  [give_to(): lax.ppermute(value, axis, [(i, (i + offset) % count) for i in range(count)])]
    pallas_call x6 -> x3, Pallas kernels: 34.5 us -> 31.5 us  [expert_of(): pl.pallas_call(functools.partial(expert_kernel, len(blocks), steps), grid...]
    ppermute x4, waiting for transfers between devices: 25.9 us -> 22.9 us  [take_from(): lax.ppermute(value, axis, [((i + offset) % count, i) for i in range(count)])]
    ppermute x4, starting transfers between devices: 4.16 us -> 6.58 us  [take_from(): lax.ppermute(value, axis, [((i + offset) % count, i) for i in range(count)])]
    ppermute x19 -> x21, waiting for transfers between devices: 44.1 us -> 42.9 us  [give_to(): lax.ppermute(value, axis, [(i, (i + offset) % count) for i in range(count)])]
  transfers between devices with their start and end apart: 23 -> 25, of which waited for: 14 -> 16; matrix products, arithmetic and copies ran while one was open for 3% -> 3% of each run, Pallas kernels for 18% -> 16%
where the time goes in v1:
time: 195 us; the launch traced here: 194 us
  waiting for transfers between devices  65.8 us (34%)
  blocking collectives  53.7 us (28%)
  starting transfers between devices  34 us (17%)
  Pallas kernels  31.5 us (16%)
  other arithmetic  6.5 us (3%)
  local copies, waits for them, and re-layouts  2.33 us (1%)
    all_gather x1, blocking collectives, layer(): near = lax.all_gather(own, 'ep_1', axis=0, tiled=True)  53.7 us
    ppermute x21, waiting for transfers between devices, give_to(): lax.ppermute(value, axis, [(i, (i + offset) % count) for i in range(count)])  42.9 us
    pallas_call x3, Pallas kernels, expert_of(): pl.pallas_call(functools.partial(expert_kernel, len(blocks), steps), grid...  31.5 us
    ppermute x21, starting transfers between devices, give_to(): lax.ppermute(value, axis, [(i, (i + offset) % count) for i in range(count)])  27.4 us
    ppermute x4, waiting for transfers between devices, take_from(): lax.ppermute(value, axis, [((i + offset) % count, i) for i in range(count)])  22.9 us
    ppermute x4, starting transfers between devices, take_from(): lax.ppermute(value, axis, [((i + offset) % count, i) for i in range(count)])  6.58 us
  transfers between devices with their start and end apart: 25, of which 16 were waited for; matrix products, arithmetic and copies ran while one was open for 3% of the time, Pallas kernels for 16%

profile of v1, /device:TPU:38, one launch (start us, length us, event | category | flops | bytes accessed | tf_op | source)
XLA Modules:
  0.0 194.1 jit_solution(6691166022169447130)
XLA Ops:
  1.7 53.7 %all-gather = bf16[16,4,7296]{2,1,0:T(4,128)(2,1)S(1)} all-gather(bf16[1,4,7296]{2,1,0:T(4,128)(2,1)S(1)} %maximum_bitcast_fusion), channel_id=1, replica_groups=mesh['groups'=2,'ep_0'=4,'ep_1'=16,'ep_2'=2] {'ep_1'}, dimensions={0}, use_global_device_ids=true | all-gather | bytes 992256 | tf_op jit(solution)/shard_map/all_gather | solution.py:168
  56.5 2.5 %collective-permute-start.3 = (bf16[64,7296]{1,0:T(8,128)(2,1)S(1)}, bf16[64,7296]{1,0:T(8,128)(2,1)S(1)}, u32[]{:S(2)}, u32[]{:S(2)}) collective-permute-start(bf16[64,7296]{1,0:T(8,128)(2,1)S(1)} %reshape.23.refs_0_.refs_2_), channel_id=1, source_target_pairs={{96,0},{0,32},{32,64},{64,96},{97,1},{1,33},{33,65},{65,97},{98,2}... | collective-permute-start | bytes 2801672 | tf_op jit(solution)/shard_map/ppermute | solution.py:23
  59.0 16.6 %collective-permute-done.2.refs_0_.refs_4_ = bf16[64,7296]{1,0:T(8,128)(2,1)S(1)} collective-permute-done((bf16[64,7296]{1,0:T(8,128)(2,1)S(1)}, bf16[64,7296]{1,0:T(8,128)(2,1)S(1)}, u32[]{:S(2)}, u32[]{:S(2)}) %collective-permute-start.2) | collective-permute-done | bytes 933920 | tf_op jit(solution)/shard_map/ppermute | solution.py:23
  77.3 3.2 %collective-permute-start.9 = (bf16[32,7296]{1,0:T(8,128)(2,1)}, bf16[32,7296]{1,0:T(8,128)(2,1)}, u32[]{:S(2)}, u32[]{:S(2)}) collective-permute-start(bf16[32,7296]{1,0:T(8,128)(2,1)} %slice.104), channel_id=1, source_target_pairs={{96,0},{0,32},{32,64},{64,96},{97,1},{1,33},{33,65},{65,97},{98,2}... | collective-permute-start | bytes 1400840 | tf_op jit(solution)/shard_map/ppermute | solution.py:23
  80.5 5.9 %collective-permute-done.8.refs_0_.refs_4_ = bf16[32,7296]{1,0:T(8,128)(2,1)S(1)} collective-permute-done((bf16[32,7296]{1,0:T(8,128)(2,1)}, bf16[32,7296]{1,0:T(8,128)(2,1)S(1)}, u32[]{:S(2)}, u32[]{:S(2)}) %collective-permute-start.8) | collective-permute-done | bytes 466976 | tf_op jit(solution)/shard_map/ppermute | solution.py:23
  89.1 9.9 %expert.5 = (f32[64,7168]{1,0:T(8,128)}, bf16[64,7168]{1,0:T(8,128)(2,1)}) custom-call(s32[1]{0:T(128)} %bitcast.expert_ref, bf16[64,64]{1,0:T(8,128)(2,1)} %fusion.10.order_ref, bf16[32,7296]{1,0:T(8,128)(2,1)} %copy-done.4, bf16[32,7296]{1,0:T(8,128)(2,1)} %collective-permute-done.9.refs_1_.refs_5_, ...), custom_call_target="tpu_custom_call" | custom-call | flops 1409286144 | bytes 16515072 | tf_op jit(solution)/shard_map/expert/pallas_call | solution.py:105
  99.3 9.9 %expert.3 = (f32[64,7168]{1,0:T(8,128)}, bf16[64,7168]{1,0:T(8,128)(2,1)}) custom-call(s32[1]{0:T(128)} %bitcast.expert_ref, bf16[64,64]{1,0:T(8,128)(2,1)} %fusion.10.order_ref, bf16[64,7296]{1,0:T(8,128)(2,1)} %copy-done, bf16[64,7296]{1,0:T(8,128)(2,1)} %collective-permute-done.refs_1_.refs_3_, bf16[64,7296]{1,0:T(8,128)(2,1)} %copy-done, ...), custom_call_target="tpu_custom_call" | custom-call | flops 1409286144 | bytes 16515072 | tf_op jit(solution)/shard_map/expert/pallas_call | solution.py:105
  109.6 11.7 %expert.4 = (f32[128,7168]{1,0:T(8,128)}, bf16[128,7168]{1,0:T(8,128)(2,1)}) custom-call(s32[1]{0:T(128)} %bitcast.expert_ref, bf16[64,64]{1,0:T(8,128)(2,1)} %fusion.10.order_ref, bf16[64,7296]{1,0:T(8,128)(2,1)} %copy-done.1, bf16[64,7296]{1,0:T(8,128)(2,1)} %copy-done.2, bf16[64,7296]{1,0:T(8,128)(2,1)} %collective-permute-done.4.refs_2_.refs_6_, ...), custom_call_target="tpu_custom_call" | custom-call | flops 2818572288 | bytes 22020096 | tf_op jit(solution)/shard_map/expert/pallas_call | solution.py:105
  121.5 2.0 %add_convert_fusion = bf16[64,7168]{1,0:T(8,128)(2,1)S(1)} fusion(f32[64,7168]{1,0:T(8,128)} %get-tuple-element.15, bf16[64,7168]{1,0:T(8,128)(2,1)} %collective-permute-done.12), kind=kLoop, calls=%fused_computation.1 | loop fusion | flops 1376256 | bytes 3670016 | tf_op jit(solution)/shard_map/convert.9
  123.6 4.0 %collective-permute-start.13 = (bf16[32,7168]{1,0:T(8,128)(2,1)S(1)}, bf16[32,7168]{1,0:T(8,128)(2,1)S(1)}, u32[]{:S(2)}, u32[]{:S(2)}) collective-permute-start(bf16[32,7168]{1,0:T(8,128)(2,1)S(1)} %get-tuple-element.27), channel_id=1, source_target_pairs={{0,32},{32,64},{64,96},{96,0},{1,33},{33,65},{65,97},{97,1},{2,34}... | collective-permute-start | bytes 1376264 | tf_op jit(solution)/shard_map/ppermute | solution.py:28
  128.1 9.7 %collective-permute-done.13 = bf16[32,7168]{1,0:T(8,128)(2,1)S(1)} collective-permute-done((bf16[32,7168]{1,0:T(8,128)(2,1)S(1)}, bf16[32,7168]{1,0:T(8,128)(2,1)S(1)}, u32[]{:S(2)}, u32[]{:S(2)}) %collective-permute-start.13) | collective-permute-done | bytes 458784 | tf_op jit(solution)/shard_map/ppermute | solution.py:28
  137.9 3.4 %collective-permute-done.17 = bf16[32,7168]{1,0:T(8,128)(2,1)S(1)} collective-permute-done((bf16[32,7168]{1,0:T(8,128)(2,1)S(1)}, bf16[32,7168]{1,0:T(8,128)(2,1)S(1)}, u32[]{:S(2)}, u32[]{:S(2)}) %collective-permute-start.17) | collective-permute-done | bytes 458784 | tf_op jit(solution)/shard_map/ppermute | solution.py:28
  141.9 1.7 collective-permute-start.18
  143.7 1.6 collective-permute-start.16
  146.0 8.9 %collective-permute-done.14 = bf16[32,7168]{1,0:T(8,128)(2,1)S(1)} collective-permute-done((bf16[32,7168]{1,0:T(8,128)(2,1)S(1)}, bf16[32,7168]{1,0:T(8,128)(2,1)S(1)}, u32[]{:S(2)}, u32[]{:S(2)}) %collective-permute-start.14) | collective-permute-done | bytes 458784 | tf_op jit(solution)/shard_map/ppermute | solution.py:28
  156.5 6.6 %collective-permute-done.16 = bf16[32,7168]{1,0:T(8,128)(2,1)S(1)} collective-permute-done((bf16[32,7168]{1,0:T(8,128)(2,1)S(1)}, bf16[32,7168]{1,0:T(8,128)(2,1)S(1)}, u32[]{:S(2)}, u32[]{:S(2)}) %collective-permute-start.16) | collective-permute-done | bytes 458784 | tf_op jit(solution)/shard_map/ppermute | solution.py:28
  165.0 3.3 %collective-permute-start.19 = (bf16[16,7168]{1,0:T(8,128)(2,1)S(1)}, bf16[16,7168]{1,0:T(8,128)(2,1)S(1)}, u32[]{:S(2)}, u32[]{:S(2)}) collective-permute-start(bf16[16,7168]{1,0:T(8,128)(2,1)S(1)} %slice.112), channel_id=1, source_target_pairs={{0,30},{2,0},{4,2},{6,4},{8,6},{10,8},{12,10},{14,12},{16,14},{18,... | collective-permute-start | bytes 688136 | tf_op jit(solution)/shard_map/ppermute | solution.py:28
  168.5 4.1 %collective-permute-start.21 = (bf16[8,7168]{1,0:T(8,128)(2,1)S(1)}, bf16[8,7168]{1,0:T(8,128)(2,1)S(1)}, u32[]{:S(2)}, u32[]{:S(2)}) collective-permute-start(bf16[8,7168]{1,0:T(8,128)(2,1)S(1)} %get-tuple-element.30), channel_id=1, source_target_pairs={{0,28},{2,30},{4,0},{6,2},{8,4},{10,6},{12,8},{14,10},{16,12},{18,... | collective-permute-start | bytes 344072 | tf_op jit(solution)/shard_map/ppermute | solution.py:28
  172.6 2.4 %collective-permute-done.15 = bf16[16,7168]{1,0:T(8,128)(2,1)S(1)} collective-permute-done((bf16[16,7168]{1,0:T(8,128)(2,1)S(1)}, bf16[16,7168]{1,0:T(8,128)(2,1)S(1)}, u32[]{:S(2)}, u32[]{:S(2)}) %collective-permute-start.15) | collective-permute-done | bytes 229408 | tf_op jit(solution)/shard_map/ppermute | solution.py:28
  176.6 3.8 %collective-permute-start.22 = (bf16[4,7168]{1,0:T(4,128)(2,1)S(1)}, bf16[4,7168]{1,0:T(4,128)(2,1)S(1)}, u32[]{:S(2)}, u32[]{:S(2)}) collective-permute-start(bf16[4,7168]{1,0:T(4,128)(2,1)S(1)} %slice.150), channel_id=1, source_target_pairs={{0,16},{2,18},{4,20},{6,22},{8,24},{10,26},{12,28},{14,30},{16,0},... | collective-permute-start | bytes 172040 | tf_op jit(solution)/shard_map/ppermute | solution.py:28
  180.5 4.2 %collective-permute-start.23 = (bf16[4,7168]{1,0:T(4,128)(2,1)S(1)}, bf16[4,7168]{1,0:T(4,128)(2,1)S(1)}, u32[]{:S(2)}, u32[]{:S(2)}) collective-permute-start(bf16[4,7168]{1,0:T(4,128)(2,1)S(1)} %get-tuple-element.31), channel_id=1, source_target_pairs={{0,8},{2,10},{4,12},{6,14},{8,16},{10,18},{12,20},{14,22},{16,24},... | collective-permute-start | bytes 172040 | tf_op jit(solution)/shard_map/ppermute | solution.py:28
  184.7 1.9 collective-permute-start.24
  186.6 3.1 %collective-permute-done.22 = bf16[4,7168]{1,0:T(4,128)(2,1)S(1)} collective-permute-done((bf16[4,7168]{1,0:T(4,128)(2,1)S(1)}, bf16[4,7168]{1,0:T(4,128)(2,1)S(1)}, u32[]{:S(2)}, u32[]{:S(2)}) %collective-permute-start.22) | collective-permute-done | bytes 57376 | tf_op jit(solution)/shard_map/ppermute | solution.py:28
  189.7 3.7 %collective-permute-done.24 = bf16[4,7168]{1,0:T(4,128)(2,1)S(1)} collective-permute-done((bf16[4,7168]{1,0:T(4,128)(2,1)S(1)}, bf16[4,7168]{1,0:T(4,128)(2,1)S(1)}, u32[]{:S(2)}, u32[]{:S(2)}) %collective-permute-start.24) | collective-permute-done | bytes 57376 | tf_op jit(solution)/shard_map/ppermute | solution.py:28
  (70 shorter events, 15.9 us)
Async XLA Ops:
  55.6 19.9 %collective-permute-start.2 = (bf16[64,7296]{1,0:T(8,128)(2,1)S(1)}, bf16[64,7296]{1,0:T(8,128)(2,1)S(1)}, u32[]{:S(2)}, u32[]{:S(2)}) collective-permute-start(bf16[64,7296]{1,0:T(8,128)(2,1)S(1)} %reshape.23.refs_0_.refs_2_), channel_id=1, source_target_pairs={{32,0},{64,32},{96,64},{0,96},{33,1},{65,33},{97,65},{1,97},{34,2}... | collective-permute-start | bytes 2801672 | tf_op jit(solution)/shard_map/ppermute | solution.py:23
  56.5 20.0 %collective-permute-start.3 = (bf16[64,7296]{1,0:T(8,128)(2,1)S(1)}, bf16[64,7296]{1,0:T(8,128)(2,1)S(1)}, u32[]{:S(2)}, u32[]{:S(2)}) collective-permute-start(bf16[64,7296]{1,0:T(8,128)(2,1)S(1)} %reshape.23.refs_0_.refs_2_), channel_id=1, source_target_pairs={{96,0},{0,32},{32,64},{64,96},{97,1},{1,33},{33,65},{65,97},{98,2}... | collective-permute-start | bytes 2801672 | tf_op jit(solution)/shard_map/ppermute | solution.py:23
  76.4 10.0 %collective-permute-start.8 = (bf16[32,7296]{1,0:T(8,128)(2,1)}, bf16[32,7296]{1,0:T(8,128)(2,1)S(1)}, u32[]{:S(2)}, u32[]{:S(2)}) collective-permute-start(bf16[32,7296]{1,0:T(8,128)(2,1)} %slice.103), channel_id=1, source_target_pairs={{32,0},{64,32},{96,64},{0,96},{33,1},{65,33},{97,65},{1,97},{34,2}... | collective-permute-start | bytes 1400840 | tf_op jit(solution)/shard_map/ppermute | solution.py:23
  77.3 9.6 %collective-permute-start.9 = (bf16[32,7296]{1,0:T(8,128)(2,1)}, bf16[32,7296]{1,0:T(8,128)(2,1)}, u32[]{:S(2)}, u32[]{:S(2)}) collective-permute-start(bf16[32,7296]{1,0:T(8,128)(2,1)} %slice.104), channel_id=1, source_target_pairs={{96,0},{0,32},{32,64},{64,96},{97,1},{1,33},{33,65},{65,97},{98,2}... | collective-permute-start | bytes 1400840 | tf_op jit(solution)/shard_map/ppermute | solution.py:23
  80.5 18.7 %collective-permute-start = (bf16[64,7296]{1,0:T(8,128)(2,1)S(1)}, bf16[64,7296]{1,0:T(8,128)(2,1)}, u32[]{:S(2)}, u32[]{:S(2)}) collective-permute-start(bf16[64,7296]{1,0:T(8,128)(2,1)S(1)} %reshape.23.refs_0_.refs_2_), channel_id=1, source_target_pairs={{0,1},{1,0},{2,3},{3,2},{4,5},{5,4},{6,7},{7,6},{8,9},{9,8},{10,11... | collective-permute-start | bytes 2801672 | tf_op jit(solution)/shard_map/ppermute | solution.py:28
  86.4 2.2 %collective-permute-start.10 = (bf16[32,7296]{1,0:T(8,128)(2,1)S(1)}, bf16[32,7296]{1,0:T(8,128)(2,1)}, u32[]{:S(2)}, u32[]{:S(2)}) collective-permute-start(bf16[32,7296]{1,0:T(8,128)(2,1)S(1)} %collective-permute-done.8.refs_0_.refs_4_), channel_id=1, source_target_pairs={{0,1},{1,0},{2,3},{3,2},{4,5},{5,4},{6,7},{7,6},{8,9},{9,8},{10,11... | collective-permute-start | bytes 1400840 | tf_op jit(solution)/shard_map/ppermute | solution.py:28
  87.1 22.4 %collective-permute-start.4 = (bf16[64,7296]{1,0:T(8,128)(2,1)S(1)}, bf16[64,7296]{1,0:T(8,128)(2,1)}, u32[]{:S(2)}, u32[]{:S(2)}) collective-permute-start(bf16[64,7296]{1,0:T(8,128)(2,1)S(1)} %collective-permute-done.2.refs_0_.refs_4_), channel_id=1, source_target_pairs={{0,1},{1,0},{2,3},{3,2},{4,5},{5,4},{6,7},{7,6},{8,9},{9,8},{10,11... | collective-permute-start | bytes 2801672 | tf_op jit(solution)/shard_map/ppermute | solution.py:28
  87.8 21.8 %collective-permute-start.5 = (bf16[64,7296]{1,0:T(8,128)(2,1)S(1)}, bf16[64,7296]{1,0:T(8,128)(2,1)}, u32[]{:S(2)}, u32[]{:S(2)}) collective-permute-start(bf16[64,7296]{1,0:T(8,128)(2,1)S(1)} %collective-permute-done.3.refs_1_.refs_5_), channel_id=1, source_target_pairs={{0,1},{1,0},{2,3},{3,2},{4,5},{5,4},{6,7},{7,6},{8,9},{9,8},{10,11... | collective-permute-start | bytes 2801672 | tf_op jit(solution)/shard_map/ppermute | solution.py:28
  99.0 22.4 %collective-permute-start.12 = (bf16[64,7168]{1,0:T(8,128)(2,1)}, bf16[64,7168]{1,0:T(8,128)(2,1)}, u32[]{:S(2)}, u32[]{:S(2)}) collective-permute-start(bf16[64,7168]{1,0:T(8,128)(2,1)} %get-tuple-element.16), channel_id=1, source_target_pairs={{0,1},{1,0},{2,3},{3,2},{4,5},{5,4},{6,7},{7,6},{8,9},{9,8},{10,11... | collective-permute-start | bytes 2752520 | tf_op jit(solution)/shard_map/ppermute | solution.py:28
  109.2 36.6 %collective-permute-start.1 = (bf16[64,7168]{1,0:T(8,128)(2,1)}, bf16[64,7168]{1,0:T(8,128)(2,1)S(1)}, u32[]{:S(2)}, u32[]{:S(2)}) collective-permute-start(bf16[64,7168]{1,0:T(8,128)(2,1)} %get-tuple-element.12), channel_id=1, source_target_pairs={{0,1},{1,0},{2,3},{3,2},{4,5},{5,4},{6,7},{7,6},{8,9},{9,8},{10,11... | collective-permute-start | bytes 2752520 | tf_op jit(solution)/shard_map/ppermute | solution.py:28
  121.3 6.3 %collective-permute-start.6 = (bf16[128,7168]{1,0:T(8,128)(2,1)}, bf16[128,7168]{1,0:T(8,128)(2,1)S(1)}, u32[]{:S(2)}, u32[]{:S(2)}) collective-permute-start(bf16[128,7168]{1,0:T(8,128)(2,1)} %get-tuple-element.14), channel_id=1, source_target_pairs={{0,1},{1,0},{2,3},{3,2},{4,5},{5,4},{6,7},{7,6},{8,9},{9,8},{10,11... | collective-permute-start | bytes 5505032 | tf_op jit(solution)/shard_map/ppermute | solution.py:28
  123.6 14.3 %collective-permute-start.13 = (bf16[32,7168]{1,0:T(8,128)(2,1)S(1)}, bf16[32,7168]{1,0:T(8,128)(2,1)S(1)}, u32[]{:S(2)}, u32[]{:S(2)}) collective-permute-start(bf16[32,7168]{1,0:T(8,128)(2,1)S(1)} %get-tuple-element.27), channel_id=1, source_target_pairs={{0,32},{32,64},{64,96},{96,0},{1,33},{33,65},{65,97},{97,1},{2,34}... | collective-permute-start | bytes 1376264 | tf_op jit(solution)/shard_map/ppermute | solution.py:28
  127.6 13.7 %collective-permute-start.17 = (bf16[32,7168]{1,0:T(8,128)(2,1)S(1)}, bf16[32,7168]{1,0:T(8,128)(2,1)S(1)}, u32[]{:S(2)}, u32[]{:S(2)}) collective-permute-start(bf16[32,7168]{1,0:T(8,128)(2,1)S(1)} %get-tuple-element.28), channel_id=1, source_target_pairs={{0,96},{32,0},{64,32},{96,64},{1,97},{33,1},{65,33},{97,65},{2,98}... | collective-permute-start | bytes 1376264 | tf_op jit(solution)/shard_map/ppermute | solution.py:28
  141.5 13.5 %collective-permute-start.14 = (bf16[32,7168]{1,0:T(8,128)(2,1)S(1)}, bf16[32,7168]{1,0:T(8,128)(2,1)S(1)}, u32[]{:S(2)}, u32[]{:S(2)}) collective-permute-start(bf16[32,7168]{1,0:T(8,128)(2,1)S(1)} %get-tuple-element.21), channel_id=1, source_target_pairs={{0,32},{32,64},{64,96},{96,0},{1,33},{33,65},{65,97},{97,1},{2,34}... | collective-permute-start | bytes 1376264 | tf_op jit(solution)/shard_map/ppermute | solution.py:28
  141.9 14.6 %collective-permute-start.18 = (bf16[32,7168]{1,0:T(8,128)(2,1)S(1)}, bf16[32,7168]{1,0:T(8,128)(2,1)S(1)}, u32[]{:S(2)}, u32[]{:S(2)}) collective-permute-start(bf16[32,7168]{1,0:T(8,128)(2,1)S(1)} %get-tuple-element.22), channel_id=1, source_target_pairs={{0,96},{32,0},{64,32},{96,64},{1,97},{33,1},{65,33},{97,65},{2,98}... | collective-permute-start | bytes 1376264 | tf_op jit(solution)/shard_map/ppermute | solution.py:28
  143.7 19.4 %collective-permute-start.16 = (bf16[32,7168]{1,0:T(8,128)(2,1)S(1)}, bf16[32,7168]{1,0:T(8,128)(2,1)S(1)}, u32[]{:S(2)}, u32[]{:S(2)}) collective-permute-start(bf16[32,7168]{1,0:T(8,128)(2,1)S(1)} %get-tuple-element.26), channel_id=1, source_target_pairs={{0,32},{32,64},{64,96},{96,0},{1,33},{33,65},{65,97},{97,1},{2,34}... | collective-permute-start | bytes 1376264 | tf_op jit(solution)/shard_map/ppermute | solution.py:28
  145.3 19.3 %collective-permute-start.7 = (bf16[32,7168]{1,0:T(8,128)(2,1)S(1)}, bf16[32,7168]{1,0:T(8,128)(2,1)S(1)}, u32[]{:S(2)}, u32[]{:S(2)}) collective-permute-start(bf16[32,7168]{1,0:T(8,128)(2,1)S(1)} %get-tuple-element.25), channel_id=1, source_target_pairs={{0,96},{32,0},{64,32},{96,64},{1,97},{33,1},{65,33},{97,65},{2,98}... | collective-permute-start | bytes 1376264 | tf_op jit(solution)/shard_map/ppermute | solution.py:28
  164.9 10.2 %collective-permute-start.15 = (bf16[16,7168]{1,0:T(8,128)(2,1)S(1)}, bf16[16,7168]{1,0:T(8,128)(2,1)S(1)}, u32[]{:S(2)}, u32[]{:S(2)}) collective-permute-start(bf16[16,7168]{1,0:T(8,128)(2,1)S(1)} %slice.149), channel_id=1, source_target_pairs={{0,2},{2,4},{4,6},{6,8},{8,10},{10,12},{12,14},{14,16},{16,18},{18... | collective-permute-start | bytes 688136 | tf_op jit(solution)/shard_map/ppermute | solution.py:28
  165.0 10.3 %collective-permute-start.19 = (bf16[16,7168]{1,0:T(8,128)(2,1)S(1)}, bf16[16,7168]{1,0:T(8,128)(2,1)S(1)}, u32[]{:S(2)}, u32[]{:S(2)}) collective-permute-start(bf16[16,7168]{1,0:T(8,128)(2,1)S(1)} %slice.112), channel_id=1, source_target_pairs={{0,30},{2,0},{4,2},{6,4},{8,6},{10,8},{12,10},{14,12},{16,14},{18,... | collective-permute-start | bytes 688136 | tf_op jit(solution)/shard_map/ppermute | solution.py:28
  168.4 8.0 %collective-permute-start.20 = (bf16[8,7168]{1,0:T(8,128)(2,1)S(1)}, bf16[8,7168]{1,0:T(8,128)(2,1)S(1)}, u32[]{:S(2)}, u32[]{:S(2)}) collective-permute-start(bf16[8,7168]{1,0:T(8,128)(2,1)S(1)} %get-tuple-element.29), channel_id=1, source_target_pairs={{0,4},{2,6},{4,8},{6,10},{8,12},{10,14},{12,16},{14,18},{16,20},{1... | collective-permute-start | bytes 344072 | tf_op jit(solution)/shard_map/ppermute | solution.py:28
  168.5 8.0 %collective-permute-start.21 = (bf16[8,7168]{1,0:T(8,128)(2,1)S(1)}, bf16[8,7168]{1,0:T(8,128)(2,1)S(1)}, u32[]{:S(2)}, u32[]{:S(2)}) collective-permute-start(bf16[8,7168]{1,0:T(8,128)(2,1)S(1)} %get-tuple-element.30), channel_id=1, source_target_pairs={{0,28},{2,30},{4,0},{6,2},{8,4},{10,6},{12,8},{14,10},{16,12},{18,... | collective-permute-start | bytes 344072 | tf_op jit(solution)/shard_map/ppermute | solution.py:28
  176.6 13.1 %collective-permute-start.22 = (bf16[4,7168]{1,0:T(4,128)(2,1)S(1)}, bf16[4,7168]{1,0:T(4,128)(2,1)S(1)}, u32[]{:S(2)}, u32[]{:S(2)}) collective-permute-start(bf16[4,7168]{1,0:T(4,128)(2,1)S(1)} %slice.150), channel_id=1, source_target_pairs={{0,16},{2,18},{4,20},{6,22},{8,24},{10,26},{12,28},{14,30},{16,0},... | collective-permute-start | bytes 172040 | tf_op jit(solution)/shard_map/ppermute | solution.py:28
  180.5 9.2 %collective-permute-start.23 = (bf16[4,7168]{1,0:T(4,128)(2,1)S(1)}, bf16[4,7168]{1,0:T(4,128)(2,1)S(1)}, u32[]{:S(2)}, u32[]{:S(2)}) collective-permute-start(bf16[4,7168]{1,0:T(4,128)(2,1)S(1)} %get-tuple-element.31), channel_id=1, source_target_pairs={{0,8},{2,10},{4,12},{6,14},{8,16},{10,18},{12,20},{14,22},{16,24},... | collective-permute-start | bytes 172040 | tf_op jit(solution)/shard_map/ppermute | solution.py:28
  184.7 8.7 %collective-permute-start.24 = (bf16[4,7168]{1,0:T(4,128)(2,1)S(1)}, bf16[4,7168]{1,0:T(4,128)(2,1)S(1)}, u32[]{:S(2)}, u32[]{:S(2)}) collective-permute-start(bf16[4,7168]{1,0:T(4,128)(2,1)S(1)} %get-tuple-element.32), channel_id=1, source_target_pairs={{0,24},{2,26},{4,28},{6,30},{8,0},{10,2},{12,4},{14,6},{16,8},{18,... | collective-permute-start | bytes 172040 | tf_op jit(solution)/shard_map/ppermute | solution.py:28
  (8 other events, 136.3 us)

commit v2 on v1

--- a/solution.py
+++ b/solution.py
@@ -11,6 +11,8 @@
 
 EXPERTS = 16
 LANES = 128
+STEPS = 4
+VMEM_LIMIT = 8 * 2**20
 EP = ("ep_0", "ep_1", "ep_2")
 GROUPS_EP = ("groups", "ep_0", "ep_1", "ep_2")
 FAR = (8, 4, 12)
@@ -51,84 +53,74 @@
     return (wanted[:, None] == jnp.arange(count * tok_rows, dtype=jnp.int32)).astype(LOW)
 
 
-def expert_kernel(blocks, steps, expert_ref, order_ref, *refs):
-    row_refs, column_refs = refs[:blocks], refs[blocks : 2 * blocks]
-    gate_ref, up_ref, down_ref, mine_ref, other_ref = refs[2 * blocks : 2 * blocks + 5]
-    gate_sum, up_sum, hidden_ref, weight_ref = refs[2 * blocks + 5 :]
-    step = pl.program_id(0)
+def expert_kernel(blocks, expert_ref, order_ref, *refs):
+    row_refs = refs[:blocks]
+    gate_ref, up_ref, down_ref, mine_ref, other_ref = refs[blocks : blocks + 5]
+    gate_sum, up_sum, hidden_ref, weight_ref = refs[blocks + 5 :]
+    width = gate_ref.shape[0]
+    chunk = width // STEPS
+    gate_sum[...] = jnp.zeros_like(gate_sum)
+    up_sum[...] = jnp.zeros_like(up_sum)
 
-    @pl.when(step == 0)
-    def _():
-        gate_sum[...] = jnp.zeros_like(gate_sum)
-        up_sum[...] = jnp.zeros_like(up_sum)
+    def add(k, carry):
+        at = pl.ds(pl.multiple_of(k * chunk, chunk), chunk)
+        rows = jnp.concatenate([r[:, at] for r in row_refs], axis=0)
+        gate_sum[...] += jnp.dot(rows, gate_ref[at, :], preferred_element_type=HIGH)
+        up_sum[...] += jnp.dot(rows, up_ref[at, :], preferred_element_type=HIGH)
+        return carry
 
-    @pl.when(step < steps)
-    def _():
-        rows = jnp.concatenate([r[...] for r in row_refs], axis=0)
-        gate_sum[...] += jnp.dot(rows, gate_ref[...], preferred_element_type=HIGH)
-        up_sum[...] += jnp.dot(rows, up_ref[...], preferred_element_type=HIGH)
+    lax.fori_loop(0, STEPS, add, 0)
+    gate_act = gate_sum[...]
+    hidden = (gate_act / (1.0 + jnp.exp(-gate_act)) * up_sum[...]).astype(LOW)
+    columns = jnp.concatenate([r[:, width:] for r in row_refs], axis=0)
+    order = order_ref[...]
+    count = order.shape[0]
+    index = lax.broadcasted_iota(jnp.int32, (count, LANES), 1)
+    mine = (lax.rem(index, EXPERTS) == expert_ref[0]) & (index < 3 * EXPERTS)
+    for at in range(0, hidden.shape[0], count):
+        moved = jnp.dot(order, hidden[at : at + count], preferred_element_type=HIGH)
+        hidden_ref[at : at + count, :] = moved.astype(LOW)
+        moved = jnp.dot(order, columns[at : at + count], preferred_element_type=HIGH)
+        weight = jnp.sum(jnp.where(mine, moved, 0.0), axis=1, keepdims=True)
+        weight_ref[at : at + count, :] = jnp.broadcast_to(weight, (count, LANES))
 
-    @pl.when(step == steps - 1)
-    def _():
-        gate_act = gate_sum[...]
-        hidden = (gate_act / (1.0 + jnp.exp(-gate_act)) * up_sum[...]).astype(LOW)
-        columns = jnp.concatenate([r[...] for r in column_refs], axis=0)
-        order = order_ref[...]
-        count = order.shape[0]
-        index = lax.broadcasted_iota(jnp.int32, (count, LANES), 1)
-        mine = (lax.rem(index, EXPERTS) == expert_ref[0]) & (index < 3 * EXPERTS)
-        for at in range(0, hidden.shape[0], count):
-            moved = jnp.dot(order, hidden[at : at + count], preferred_element_type=HIGH)
-            hidden_ref[at : at + count, :] = moved.astype(LOW)
-            moved = jnp.dot(order, columns[at : at + count], preferred_element_type=HIGH)
-            weight = jnp.sum(jnp.where(mine, moved, 0.0), axis=1, keepdims=True)
-            weight_ref[at : at + count, :] = jnp.broadcast_to(weight, (count, LANES))
+    def give(k, carry):
+        at = pl.ds(pl.multiple_of(k * chunk, chunk), chunk)
+        result = jnp.dot(hidden_ref[...], down_ref[:, at], preferred_element_type=HIGH)
+        result = result * weight_ref[:, :1]
+        half = mine_ref.shape[0]
+        mine_ref[:, at] = result[:half]
+        other_ref[:, at] = result[half:].astype(LOW)
+        return carry
 
-    @pl.when(step >= steps)
-    def _():
-        result = jnp.dot(hidden_ref[...], down_ref[...], preferred_element_type=HIGH)
-        result = result * weight_ref[:, :1]
-        count = mine_ref.shape[0]
-        mine_ref[...] = result[:count]
-        other_ref[...] = result[count:].astype(LOW)
+    lax.fori_loop(0, STEPS, give, 0)
 
 
 def expert_of(expert, order, blocks, gate_weight, up_weight, down_weight):
     width, units = gate_weight.shape
-    steps = 4
-    chunk = width // steps
     rows = sum(block.shape[0] for block in blocks)
-    whole = lambda k: (0, 0)
-    first = lambda k: jnp.minimum(k, steps - 1)
-    second = lambda k: jnp.maximum(k - steps, 0)
-    half = pl.BlockSpec((rows // 2, chunk), lambda k: (0, second(k)))
+    operands = [order, *blocks, gate_weight, up_weight, down_weight]
+    operands = [pltpu.with_memory_space_constraint(value, pltpu.VMEM) for value in operands]
+    in_vmem = pl.BlockSpec(memory_space=pltpu.VMEM)
     return pl.pallas_call(
-        functools.partial(expert_kernel, len(blocks), steps),
-        grid=(2 * steps,),
-        in_specs=[
-            pl.BlockSpec(memory_space=pltpu.SMEM),
-            pl.BlockSpec(order.shape, whole),
-            *[pl.BlockSpec((block.shape[0], chunk), lambda k: (0, first(k))) for block in blocks],
-            *[pl.BlockSpec((block.shape[0], LANES), lambda k: (0, width // LANES)) for block in blocks],
-            pl.BlockSpec((chunk, units), lambda k: (first(k), 0)),
-            pl.BlockSpec((chunk, units), lambda k: (first(k), 0)),
-            pl.BlockSpec((units, chunk), lambda k: (0, second(k))),
-        ],
-        out_specs=[half, half],
-        out_shape=[jax.ShapeDtypeStruct((rows // 2, width), t) for t in (HIGH, LOW)],
+        functools.partial(expert_kernel, len(blocks)),
+        in_specs=[pl.BlockSpec(memory_space=pltpu.SMEM)] + [in_vmem for _ in operands],
+        out_specs=[in_vmem, in_vmem],
+        out_shape=[pltpu.VMEM((rows // 2, width), t) for t in (HIGH, LOW)],
         scratch_shapes=[
             pltpu.VMEM((rows, units), HIGH),
             pltpu.VMEM((rows, units), HIGH),
             pltpu.VMEM((rows, units), LOW),
             pltpu.VMEM((rows, LANES), HIGH),
         ],
+        compiler_params=pltpu.CompilerParams(vmem_limit_bytes=VMEM_LIMIT),
         cost_estimate=pl.CostEstimate(
             flops=2 * rows * width * 3 * units,
             bytes_accessed=2 * width * (3 * rows + 3 * units),
             transcendentals=rows * units,
         ),
         name="expert",
-    )(expert, order, *blocks, *blocks, gate_weight, up_weight, down_weight)
+    )(expert, *operands)
 
 
 def near_sum(kept, pieces):

time: 195 us -> 181 us (0.928)
  Pallas kernels: 31.5 us -> 13.5 us
  local copies, waits for them, and re-layouts: 2.33 us -> 8.28 us
  other arithmetic: 6.5 us -> 4.05 us
    pallas_call x3, Pallas kernels: 31.5 us -> 13.5 us  [expert_of(): pl.pallas_call(functools.partial(expert_kernel, len(blocks)), in_specs=[p...]
    unnamed x15 -> x11, local copies, waits for them, and re-layouts: 0.24 us -> 6.33 us
  transfers between devices with their start and end apart: 25 -> 25, of which waited for: 16 -> 17; matrix products, arithmetic and copies ran while one was open for 3% -> 2% of each run, Pallas kernels for 16% -> 7%
where the time goes in v2:
time: 181 us
  waiting for transfers between devices  66.6 us (37%)
  blocking collectives  53.7 us (30%)
  starting transfers between devices  34.2 us (19%)
  Pallas kernels  13.5 us (7%)
  local copies, waits for them, and re-layouts  8.28 us (5%)
  other arithmetic  4.05 us (2%)
    all_gather x1, blocking collectives, layer(): near = lax.all_gather(own, 'ep_1', axis=0, tiled=True)  53.7 us
    ppermute x21, waiting for transfers between devices, give_to(): lax.ppermute(value, axis, [(i, (i + offset) % count) for i in range(count)])  43.6 us
    ppermute x21, starting transfers between devices, give_to(): lax.ppermute(value, axis, [(i, (i + offset) % count) for i in range(count)])  27.6 us
    ppermute x4, waiting for transfers between devices, take_from(): lax.ppermute(value, axis, [((i + offset) % count, i) for i in range(count)])  23 us
    pallas_call x3, Pallas kernels, expert_of(): pl.pallas_call(functools.partial(expert_kernel, len(blocks)), in_specs=[p...  13.5 us
    ppermute x4, starting transfers between devices, take_from(): lax.ppermute(value, axis, [((i + offset) % count, i) for i in range(count)])  6.58 us
    unnamed x11, local copies, waits for them, and re-layouts  6.33 us
  transfers between devices with their start and end apart: 25, of which 17 were waited for; matrix products, arithmetic and copies ran while one was open for 2% of the time, Pallas kernels for 7%

profile of v2, /device:TPU:38, one launch (start us, length us, event | category | flops | bytes accessed | tf_op | source)
XLA Modules:
  0.0 180.5 jit_solution(2803322236273049501)
XLA Ops:
  1.7 53.7 %all-gather = bf16[16,4,7296]{2,1,0:T(4,128)(2,1)S(1)} all-gather(bf16[1,4,7296]{2,1,0:T(4,128)(2,1)S(1)} %maximum_bitcast_fusion), channel_id=1, replica_groups=mesh['groups'=2,'ep_0'=4,'ep_1'=16,'ep_2'=2] {'ep_1'}, dimensions={0}, use_global_device_ids=true | all-gather | bytes 992256 | tf_op jit(solution)/shard_map/all_gather | solution.py:160
  56.4 2.5 %collective-permute-start.3 = (bf16[64,7296]{1,0:T(8,128)(2,1)S(1)}, bf16[64,7296]{1,0:T(8,128)(2,1)S(1)}, u32[]{:S(2)}, u32[]{:S(2)}) collective-permute-start(bf16[64,7296]{1,0:T(8,128)(2,1)S(1)} %reshape.23.refs_0_), channel_id=1, source_target_pairs={{96,0},{0,32},{32,64},{64,96},{97,1},{1,33},{33,65},{65,97},{98,2}... | collective-permute-start | bytes 2801672 | tf_op jit(solution)/shard_map/ppermute | solution.py:25
  59.0 16.6 %collective-permute-done.2.refs_0_ = bf16[64,7296]{1,0:T(8,128)(2,1)S(1)} collective-permute-done((bf16[64,7296]{1,0:T(8,128)(2,1)S(1)}, bf16[64,7296]{1,0:T(8,128)(2,1)S(1)}, u32[]{:S(2)}, u32[]{:S(2)}) %collective-permute-start.2) | collective-permute-done | bytes 933920 | tf_op jit(solution)/shard_map/ppermute | solution.py:25
  77.2 3.2 %collective-permute-start.9 = (bf16[32,7296]{1,0:T(8,128)(2,1)}, bf16[32,7296]{1,0:T(8,128)(2,1)}, u32[]{:S(2)}, u32[]{:S(2)}) collective-permute-start(bf16[32,7296]{1,0:T(8,128)(2,1)} %slice.104), channel_id=1, source_target_pairs={{96,0},{0,32},{32,64},{64,96},{97,1},{1,33},{33,65},{65,97},{98,2}... | collective-permute-start | bytes 1400840 | tf_op jit(solution)/shard_map/ppermute | solution.py:25
  80.5 5.9 %collective-permute-done.8.refs_0_ = bf16[32,7296]{1,0:T(8,128)(2,1)S(1)} collective-permute-done((bf16[32,7296]{1,0:T(8,128)(2,1)}, bf16[32,7296]{1,0:T(8,128)(2,1)S(1)}, u32[]{:S(2)}, u32[]{:S(2)}) %collective-permute-start.8) | collective-permute-done | bytes 466976 | tf_op jit(solution)/shard_map/ppermute | solution.py:25
  89.0 2.0 %copy-done = bf16[7168,256]{1,0:T(8,128)(2,1)S(1)} copy-done((bf16[7168,256]{1,0:T(8,128)(2,1)S(1)}, bf16[7168,256]{1,0:T(8,128)(2,1)}, u32[]{:S(2)}) %copy-start) | copy-done | bytes 3670040
  91.1 2.0 %copy-done.2 = bf16[7168,256]{1,0:T(8,128)(2,1)S(1)} copy-done((bf16[7168,256]{1,0:T(8,128)(2,1)S(1)}, bf16[7168,256]{1,0:T(8,128)(2,1)}, u32[]{:S(2)}) %copy-start.2) | copy-done | bytes 3670040
  93.1 2.0 %copy-done.3 = bf16[256,7168]{1,0:T(8,128)(2,1)S(1)} copy-done((bf16[256,7168]{1,0:T(8,128)(2,1)S(1)}, bf16[256,7168]{1,0:T(8,128)(2,1)}, u32[]{:S(2)}) %copy-start.3) | copy-done | bytes 3670040
  95.2 4.6 %expert.5 = (f32[64,7168]{1,0:T(8,128)S(1)}, bf16[64,7168]{1,0:T(8,128)(2,1)S(1)}) custom-call(s32[1]{0:T(128)} %bitcast.expert_ref, bf16[64,64]{1,0:T(8,128)(2,1)S(1)} %fusion.10.order_ref, bf16[32,7296]{1,0:T(8,128)(2,1)S(1)} %collective-permute-done.8.refs_0_, bf16[32,7296]{1,0:T(8,128)(2,1)} %collective-permute-done.9.refs_1_, ...), custom_call_target="tpu_custom_call" | custom-call | flops 1409286144 | bytes 16515072 | tf_op jit(solution)/shard_map/expert/pallas_call | solution.py:105
  100.0 4.3 %expert.3 = (f32[64,7168]{1,0:T(8,128)S(1)}, bf16[64,7168]{1,0:T(8,128)(2,1)S(1)}) custom-call(s32[1]{0:T(128)} %bitcast.expert_ref, bf16[64,64]{1,0:T(8,128)(2,1)S(1)} %fusion.10.order_ref, bf16[64,7296]{1,0:T(8,128)(2,1)S(1)} %reshape.23.refs_0_, bf16[64,7296]{1,0:T(8,128)(2,1)} %collective-permute-done.refs_1_, bf16[7168,256]{1,0:T(8,128)(2,1)S(1)} %copy-done.1, ...), custom_call_target="tpu_custom_call" | custom-call | flops 1409286144 | bytes 16515072 | tf_op jit(solution)/shard_map/expert/pallas_call | solution.py:105
  104.9 4.6 %expert.4 = (f32[128,7168]{1,0:T(8,128)S(1)}, bf16[128,7168]{1,0:T(8,128)(2,1)S(1)}) custom-call(s32[1]{0:T(128)} %bitcast.expert_ref, bf16[64,64]{1,0:T(8,128)(2,1)S(1)} %fusion.10.order_ref, bf16[64,7296]{1,0:T(8,128)(2,1)S(1)} %collective-permute-done.2.refs_0_, bf16[64,7296]{1,0:T(8,128)(2,1)S(1)} %collective-permute-done.3.refs_1_, ...), custom_call_target="tpu_custom_call" | custom-call | flops 2818572288 | bytes 22020096 | tf_op jit(solution)/shard_map/expert/pallas_call | solution.py:105
  110.0 4.0 %collective-permute-start.13 = (bf16[32,7168]{1,0:T(8,128)(2,1)S(1)}, bf16[32,7168]{1,0:T(8,128)(2,1)S(1)}, u32[]{:S(2)}, u32[]{:S(2)}) collective-permute-start(bf16[32,7168]{1,0:T(8,128)(2,1)S(1)} %get-tuple-element.27), channel_id=1, source_target_pairs={{0,32},{32,64},{64,96},{96,0},{1,33},{33,65},{65,97},{97,1},{2,34}... | collective-permute-start | bytes 1376264 | tf_op jit(solution)/shard_map/ppermute | solution.py:30
  114.5 9.7 %collective-permute-done.13 = bf16[32,7168]{1,0:T(8,128)(2,1)S(1)} collective-permute-done((bf16[32,7168]{1,0:T(8,128)(2,1)S(1)}, bf16[32,7168]{1,0:T(8,128)(2,1)S(1)}, u32[]{:S(2)}, u32[]{:S(2)}) %collective-permute-start.13) | collective-permute-done | bytes 458784 | tf_op jit(solution)/shard_map/ppermute | solution.py:30
  124.3 3.4 %collective-permute-done.17 = bf16[32,7168]{1,0:T(8,128)(2,1)S(1)} collective-permute-done((bf16[32,7168]{1,0:T(8,128)(2,1)S(1)}, bf16[32,7168]{1,0:T(8,128)(2,1)S(1)}, u32[]{:S(2)}, u32[]{:S(2)}) %collective-permute-start.17) | collective-permute-done | bytes 458784 | tf_op jit(solution)/shard_map/ppermute | solution.py:30
  132.4 9.0 %collective-permute-done.14 = bf16[32,7168]{1,0:T(8,128)(2,1)S(1)} collective-permute-done((bf16[32,7168]{1,0:T(8,128)(2,1)S(1)}, bf16[32,7168]{1,0:T(8,128)(2,1)S(1)}, u32[]{:S(2)}, u32[]{:S(2)}) %collective-permute-start.14) | collective-permute-done | bytes 458784 | tf_op jit(solution)/shard_map/ppermute | solution.py:30
  142.9 6.6 %collective-permute-done.16 = bf16[32,7168]{1,0:T(8,128)(2,1)S(1)} collective-permute-done((bf16[32,7168]{1,0:T(8,128)(2,1)S(1)}, bf16[32,7168]{1,0:T(8,128)(2,1)S(1)}, u32[]{:S(2)}, u32[]{:S(2)}) %collective-permute-start.16) | collective-permute-done | bytes 458784 | tf_op jit(solution)/shard_map/ppermute | solution.py:30
  151.5 3.3 %collective-permute-start.19 = (bf16[16,7168]{1,0:T(8,128)(2,1)S(1)}, bf16[16,7168]{1,0:T(8,128)(2,1)S(1)}, u32[]{:S(2)}, u32[]{:S(2)}) collective-permute-start(bf16[16,7168]{1,0:T(8,128)(2,1)S(1)} %slice.112), channel_id=1, source_target_pairs={{0,30},{2,0},{4,2},{6,4},{8,6},{10,8},{12,10},{14,12},{16,14},{18,... | collective-permute-start | bytes 688136 | tf_op jit(solution)/shard_map/ppermute | solution.py:30
  155.0 4.1 %collective-permute-start.21 = (bf16[8,7168]{1,0:T(8,128)(2,1)S(1)}, bf16[8,7168]{1,0:T(8,128)(2,1)S(1)}, u32[]{:S(2)}, u32[]{:S(2)}) collective-permute-start(bf16[8,7168]{1,0:T(8,128)(2,1)S(1)} %get-tuple-element.30), channel_id=1, source_target_pairs={{0,28},{2,30},{4,0},{6,2},{8,4},{10,6},{12,8},{14,10},{16,12},{18,... | collective-permute-start | bytes 344072 | tf_op jit(solution)/shard_map/ppermute | solution.py:30
  159.1 2.4 %collective-permute-done.15 = bf16[16,7168]{1,0:T(8,128)(2,1)S(1)} collective-permute-done((bf16[16,7168]{1,0:T(8,128)(2,1)S(1)}, bf16[16,7168]{1,0:T(8,128)(2,1)S(1)}, u32[]{:S(2)}, u32[]{:S(2)}) %collective-permute-start.15) | collective-permute-done | bytes 229408 | tf_op jit(solution)/shard_map/ppermute | solution.py:30
  163.1 3.8 %collective-permute-start.22 = (bf16[4,7168]{1,0:T(4,128)(2,1)S(1)}, bf16[4,7168]{1,0:T(4,128)(2,1)S(1)}, u32[]{:S(2)}, u32[]{:S(2)}) collective-permute-start(bf16[4,7168]{1,0:T(4,128)(2,1)S(1)} %slice.150), channel_id=1, source_target_pairs={{0,16},{2,18},{4,20},{6,22},{8,24},{10,26},{12,28},{14,30},{16,0},... | collective-permute-start | bytes 172040 | tf_op jit(solution)/shard_map/ppermute | solution.py:30
  166.9 4.2 %collective-permute-start.23 = (bf16[4,7168]{1,0:T(4,128)(2,1)S(1)}, bf16[4,7168]{1,0:T(4,128)(2,1)S(1)}, u32[]{:S(2)}, u32[]{:S(2)}) collective-permute-start(bf16[4,7168]{1,0:T(4,128)(2,1)S(1)} %get-tuple-element.31), channel_id=1, source_target_pairs={{0,8},{2,10},{4,12},{6,14},{8,16},{10,18},{12,20},{14,22},{16,24},... | collective-permute-start | bytes 172040 | tf_op jit(solution)/shard_map/ppermute | solution.py:30
  171.2 1.8 %collective-permute-start.24 = (bf16[4,7168]{1,0:T(4,128)(2,1)S(1)}, bf16[4,7168]{1,0:T(4,128)(2,1)S(1)}, u32[]{:S(2)}, u32[]{:S(2)}) collective-permute-start(bf16[4,7168]{1,0:T(4,128)(2,1)S(1)} %get-tuple-element.32), channel_id=1, source_target_pairs={{0,24},{2,26},{4,28},{6,30},{8,0},{10,2},{12,4},{14,6},{16,8},{18,... | collective-permute-start | bytes 172040 | tf_op jit(solution)/shard_map/ppermute | solution.py:30
  173.0 3.2 %collective-permute-done.22 = bf16[4,7168]{1,0:T(4,128)(2,1)S(1)} collective-permute-done((bf16[4,7168]{1,0:T(4,128)(2,1)S(1)}, bf16[4,7168]{1,0:T(4,128)(2,1)S(1)}, u32[]{:S(2)}, u32[]{:S(2)}) %collective-permute-start.22) | collective-permute-done | bytes 57376 | tf_op jit(solution)/shard_map/ppermute | solution.py:30
  176.2 3.7 %collective-permute-done.24 = bf16[4,7168]{1,0:T(4,128)(2,1)S(1)} collective-permute-done((bf16[4,7168]{1,0:T(4,128)(2,1)S(1)}, bf16[4,7168]{1,0:T(4,128)(2,1)S(1)}, u32[]{:S(2)}, u32[]{:S(2)}) %collective-permute-start.24) | collective-permute-done | bytes 57376 | tf_op jit(solution)/shard_map/ppermute | solution.py:30
  (66 shorter events, 19.4 us)
Async XLA Ops:
  55.6 20.0 %collective-permute-start.2 = (bf16[64,7296]{1,0:T(8,128)(2,1)S(1)}, bf16[64,7296]{1,0:T(8,128)(2,1)S(1)}, u32[]{:S(2)}, u32[]{:S(2)}) collective-permute-start(bf16[64,7296]{1,0:T(8,128)(2,1)S(1)} %reshape.23.refs_0_), channel_id=1, source_target_pairs={{32,0},{64,32},{96,64},{0,96},{33,1},{65,33},{97,65},{1,97},{34,2}... | collective-permute-start | bytes 2801672 | tf_op jit(solution)/shard_map/ppermute | solution.py:25
  56.4 20.0 %collective-permute-start.3 = (bf16[64,7296]{1,0:T(8,128)(2,1)S(1)}, bf16[64,7296]{1,0:T(8,128)(2,1)S(1)}, u32[]{:S(2)}, u32[]{:S(2)}) collective-permute-start(bf16[64,7296]{1,0:T(8,128)(2,1)S(1)} %reshape.23.refs_0_), channel_id=1, source_target_pairs={{96,0},{0,32},{32,64},{64,96},{97,1},{1,33},{33,65},{65,97},{98,2}... | collective-permute-start | bytes 2801672 | tf_op jit(solution)/shard_map/ppermute | solution.py:25
  76.4 10.0 %collective-permute-start.8 = (bf16[32,7296]{1,0:T(8,128)(2,1)}, bf16[32,7296]{1,0:T(8,128)(2,1)S(1)}, u32[]{:S(2)}, u32[]{:S(2)}) collective-permute-start(bf16[32,7296]{1,0:T(8,128)(2,1)} %slice.103), channel_id=1, source_target_pairs={{32,0},{64,32},{96,64},{0,96},{33,1},{65,33},{97,65},{1,97},{34,2}... | collective-permute-start | bytes 1400840 | tf_op jit(solution)/shard_map/ppermute | solution.py:25
  77.2 9.6 %collective-permute-start.9 = (bf16[32,7296]{1,0:T(8,128)(2,1)}, bf16[32,7296]{1,0:T(8,128)(2,1)}, u32[]{:S(2)}, u32[]{:S(2)}) collective-permute-start(bf16[32,7296]{1,0:T(8,128)(2,1)} %slice.104), channel_id=1, source_target_pairs={{96,0},{0,32},{32,64},{64,96},{97,1},{1,33},{33,65},{65,97},{98,2}... | collective-permute-start | bytes 1400840 | tf_op jit(solution)/shard_map/ppermute | solution.py:25
  80.5 19.6 %collective-permute-start = (bf16[64,7296]{1,0:T(8,128)(2,1)S(1)}, bf16[64,7296]{1,0:T(8,128)(2,1)}, u32[]{:S(2)}, u32[]{:S(2)}) collective-permute-start(bf16[64,7296]{1,0:T(8,128)(2,1)S(1)} %reshape.23.refs_0_), channel_id=1, source_target_pairs={{0,1},{1,0},{2,3},{3,2},{4,5},{5,4},{6,7},{7,6},{8,9},{9,8},{10,11... | collective-permute-start | bytes 2801672 | tf_op jit(solution)/shard_map/ppermute | solution.py:30
  86.9 2.2 %collective-permute-start.11 = (bf16[32,7296]{1,0:T(8,128)(2,1)}, bf16[32,7296]{1,0:T(8,128)(2,1)}, u32[]{:S(2)}, u32[]{:S(2)}) collective-permute-start(bf16[32,7296]{1,0:T(8,128)(2,1)} %collective-permute-done.9.refs_1_), channel_id=1, source_target_pairs={{0,1},{1,0},{2,3},{3,2},{4,5},{5,4},{6,7},{7,6},{8,9},{9,8},{10,11... | collective-permute-start | bytes 1400840 | tf_op jit(solution)/shard_map/ppermute | solution.py:30
  87.1 17.8 %collective-permute-start.4 = (bf16[64,7296]{1,0:T(8,128)(2,1)S(1)}, bf16[64,7296]{1,0:T(8,128)(2,1)S(1)}, u32[]{:S(2)}, u32[]{:S(2)}) collective-permute-start(bf16[64,7296]{1,0:T(8,128)(2,1)S(1)} %collective-permute-done.2.refs_0_), channel_id=1, source_target_pairs={{0,1},{1,0},{2,3},{3,2},{4,5},{5,4},{6,7},{7,6},{8,9},{9,8},{10,11... | collective-permute-start | bytes 2801672 | tf_op jit(solution)/shard_map/ppermute | solution.py:30
  87.7 17.2 %collective-permute-start.5 = (bf16[64,7296]{1,0:T(8,128)(2,1)S(1)}, bf16[64,7296]{1,0:T(8,128)(2,1)S(1)}, u32[]{:S(2)}, u32[]{:S(2)}) collective-permute-start(bf16[64,7296]{1,0:T(8,128)(2,1)S(1)} %collective-permute-done.3.refs_1_), channel_id=1, source_target_pairs={{0,1},{1,0},{2,3},{3,2},{4,5},{5,4},{6,7},{7,6},{8,9},{9,8},{10,11... | collective-permute-start | bytes 2801672 | tf_op jit(solution)/shard_map/ppermute | solution.py:30
  99.8 10.0 %collective-permute-start.12 = (bf16[64,7168]{1,0:T(8,128)(2,1)S(1)}, bf16[64,7168]{1,0:T(8,128)(2,1)S(1)}, u32[]{:S(2)}, u32[]{:S(2)}) collective-permute-start(bf16[64,7168]{1,0:T(8,128)(2,1)S(1)} %get-tuple-element.16), channel_id=1, source_target_pairs={{0,1},{1,0},{2,3},{3,2},{4,5},{5,4},{6,7},{7,6},{8,9},{9,8},{10,11... | collective-permute-start | bytes 2752520 | tf_op jit(solution)/shard_map/ppermute | solution.py:30
  104.4 27.8 %collective-permute-start.1 = (bf16[64,7168]{1,0:T(8,128)(2,1)S(1)}, bf16[64,7168]{1,0:T(8,128)(2,1)S(1)}, u32[]{:S(2)}, u32[]{:S(2)}) collective-permute-start(bf16[64,7168]{1,0:T(8,128)(2,1)S(1)} %get-tuple-element.12), channel_id=1, source_target_pairs={{0,1},{1,0},{2,3},{3,2},{4,5},{5,4},{6,7},{7,6},{8,9},{9,8},{10,11... | collective-permute-start | bytes 2752520 | tf_op jit(solution)/shard_map/ppermute | solution.py:30
  109.5 4.5 %collective-permute-start.6 = (bf16[128,7168]{1,0:T(8,128)(2,1)S(1)}, bf16[128,7168]{1,0:T(8,128)(2,1)S(1)}, u32[]{:S(2)}, u32[]{:S(2)}) collective-permute-start(bf16[128,7168]{1,0:T(8,128)(2,1)S(1)} %get-tuple-element.14), channel_id=1, source_target_pairs={{0,1},{1,0},{2,3},{3,2},{4,5},{5,4},{6,7},{7,6},{8,9},{9,8},{10,11... | collective-permute-start | bytes 5505032 | tf_op jit(solution)/shard_map/ppermute | solution.py:30
  110.0 14.3 %collective-permute-start.13 = (bf16[32,7168]{1,0:T(8,128)(2,1)S(1)}, bf16[32,7168]{1,0:T(8,128)(2,1)S(1)}, u32[]{:S(2)}, u32[]{:S(2)}) collective-permute-start(bf16[32,7168]{1,0:T(8,128)(2,1)S(1)} %get-tuple-element.27), channel_id=1, source_target_pairs={{0,32},{32,64},{64,96},{96,0},{1,33},{33,65},{65,97},{97,1},{2,34}... | collective-permute-start | bytes 1376264 | tf_op jit(solution)/shard_map/ppermute | solution.py:30
  114.0 13.7 %collective-permute-start.17 = (bf16[32,7168]{1,0:T(8,128)(2,1)S(1)}, bf16[32,7168]{1,0:T(8,128)(2,1)S(1)}, u32[]{:S(2)}, u32[]{:S(2)}) collective-permute-start(bf16[32,7168]{1,0:T(8,128)(2,1)S(1)} %get-tuple-element.28), channel_id=1, source_target_pairs={{0,96},{32,0},{64,32},{96,64},{1,97},{33,1},{65,33},{97,65},{2,98}... | collective-permute-start | bytes 1376264 | tf_op jit(solution)/shard_map/ppermute | solution.py:30
  127.9 13.5 %collective-permute-start.14 = (bf16[32,7168]{1,0:T(8,128)(2,1)S(1)}, bf16[32,7168]{1,0:T(8,128)(2,1)S(1)}, u32[]{:S(2)}, u32[]{:S(2)}) collective-permute-start(bf16[32,7168]{1,0:T(8,128)(2,1)S(1)} %get-tuple-element.21), channel_id=1, source_target_pairs={{0,32},{32,64},{64,96},{96,0},{1,33},{33,65},{65,97},{97,1},{2,34}... | collective-permute-start | bytes 1376264 | tf_op jit(solution)/shard_map/ppermute | solution.py:30
  128.3 14.6 %collective-permute-start.18 = (bf16[32,7168]{1,0:T(8,128)(2,1)S(1)}, bf16[32,7168]{1,0:T(8,128)(2,1)S(1)}, u32[]{:S(2)}, u32[]{:S(2)}) collective-permute-start(bf16[32,7168]{1,0:T(8,128)(2,1)S(1)} %get-tuple-element.22), channel_id=1, source_target_pairs={{0,96},{32,0},{64,32},{96,64},{1,97},{33,1},{65,33},{97,65},{2,98}... | collective-permute-start | bytes 1376264 | tf_op jit(solution)/shard_map/ppermute | solution.py:30
  130.1 19.4 %collective-permute-start.16 = (bf16[32,7168]{1,0:T(8,128)(2,1)S(1)}, bf16[32,7168]{1,0:T(8,128)(2,1)S(1)}, u32[]{:S(2)}, u32[]{:S(2)}) collective-permute-start(bf16[32,7168]{1,0:T(8,128)(2,1)S(1)} %get-tuple-element.26), channel_id=1, source_target_pairs={{0,32},{32,64},{64,96},{96,0},{1,33},{33,65},{65,97},{97,1},{2,34}... | collective-permute-start | bytes 1376264 | tf_op jit(solution)/shard_map/ppermute | solution.py:30
  131.7 19.3 %collective-permute-start.7 = (bf16[32,7168]{1,0:T(8,128)(2,1)S(1)}, bf16[32,7168]{1,0:T(8,128)(2,1)S(1)}, u32[]{:S(2)}, u32[]{:S(2)}) collective-permute-start(bf16[32,7168]{1,0:T(8,128)(2,1)S(1)} %get-tuple-element.25), channel_id=1, source_target_pairs={{0,96},{32,0},{64,32},{96,64},{1,97},{33,1},{65,33},{97,65},{2,98}... | collective-permute-start | bytes 1376264 | tf_op jit(solution)/shard_map/ppermute | solution.py:30
  151.3 10.2 %collective-permute-start.15 = (bf16[16,7168]{1,0:T(8,128)(2,1)S(1)}, bf16[16,7168]{1,0:T(8,128)(2,1)S(1)}, u32[]{:S(2)}, u32[]{:S(2)}) collective-permute-start(bf16[16,7168]{1,0:T(8,128)(2,1)S(1)} %slice.149), channel_id=1, source_target_pairs={{0,2},{2,4},{4,6},{6,8},{8,10},{10,12},{12,14},{14,16},{16,18},{18... | collective-permute-start | bytes 688136 | tf_op jit(solution)/shard_map/ppermute | solution.py:30
  151.5 10.3 %collective-permute-start.19 = (bf16[16,7168]{1,0:T(8,128)(2,1)S(1)}, bf16[16,7168]{1,0:T(8,128)(2,1)S(1)}, u32[]{:S(2)}, u32[]{:S(2)}) collective-permute-start(bf16[16,7168]{1,0:T(8,128)(2,1)S(1)} %slice.112), channel_id=1, source_target_pairs={{0,30},{2,0},{4,2},{6,4},{8,6},{10,8},{12,10},{14,12},{16,14},{18,... | collective-permute-start | bytes 688136 | tf_op jit(solution)/shard_map/ppermute | solution.py:30
  154.8 8.1 %collective-permute-start.20 = (bf16[8,7168]{1,0:T(8,128)(2,1)S(1)}, bf16[8,7168]{1,0:T(8,128)(2,1)S(1)}, u32[]{:S(2)}, u32[]{:S(2)}) collective-permute-start(bf16[8,7168]{1,0:T(8,128)(2,1)S(1)} %get-tuple-element.29), channel_id=1, source_target_pairs={{0,4},{2,6},{4,8},{6,10},{8,12},{10,14},{12,16},{14,18},{16,20},{1... | collective-permute-start | bytes 344072 | tf_op jit(solution)/shard_map/ppermute | solution.py:30
  155.0 8.0 %collective-permute-start.21 = (bf16[8,7168]{1,0:T(8,128)(2,1)S(1)}, bf16[8,7168]{1,0:T(8,128)(2,1)S(1)}, u32[]{:S(2)}, u32[]{:S(2)}) collective-permute-start(bf16[8,7168]{1,0:T(8,128)(2,1)S(1)} %get-tuple-element.30), channel_id=1, source_target_pairs={{0,28},{2,30},{4,0},{6,2},{8,4},{10,6},{12,8},{14,10},{16,12},{18,... | collective-permute-start | bytes 344072 | tf_op jit(solution)/shard_map/ppermute | solution.py:30
  163.1 13.1 %collective-permute-start.22 = (bf16[4,7168]{1,0:T(4,128)(2,1)S(1)}, bf16[4,7168]{1,0:T(4,128)(2,1)S(1)}, u32[]{:S(2)}, u32[]{:S(2)}) collective-permute-start(bf16[4,7168]{1,0:T(4,128)(2,1)S(1)} %slice.150), channel_id=1, source_target_pairs={{0,16},{2,18},{4,20},{6,22},{8,24},{10,26},{12,28},{14,30},{16,0},... | collective-permute-start | bytes 172040 | tf_op jit(solution)/shard_map/ppermute | solution.py:30
  166.9 9.2 %collective-permute-start.23 = (bf16[4,7168]{1,0:T(4,128)(2,1)S(1)}, bf16[4,7168]{1,0:T(4,128)(2,1)S(1)}, u32[]{:S(2)}, u32[]{:S(2)}) collective-permute-start(bf16[4,7168]{1,0:T(4,128)(2,1)S(1)} %get-tuple-element.31), channel_id=1, source_target_pairs={{0,8},{2,10},{4,12},{6,14},{8,16},{10,18},{12,20},{14,22},{16,24},... | collective-permute-start | bytes 172040 | tf_op jit(solution)/shard_map/ppermute | solution.py:30
  171.2 8.7 %collective-permute-start.24 = (bf16[4,7168]{1,0:T(4,128)(2,1)S(1)}, bf16[4,7168]{1,0:T(4,128)(2,1)S(1)}, u32[]{:S(2)}, u32[]{:S(2)}) collective-permute-start(bf16[4,7168]{1,0:T(4,128)(2,1)S(1)} %get-tuple-element.32), channel_id=1, source_target_pairs={{0,24},{2,26},{4,28},{6,30},{8,0},{10,2},{12,4},{14,6},{16,8},{18,... | collective-permute-start | bytes 172040 | tf_op jit(solution)/shard_map/ppermute | solution.py:30
  (6 other events, 44.5 us)

commit v3 on v2

--- a/solution.py
+++ b/solution.py
@@ -123,6 +123,21 @@
     )(expert, *operands)
 
 
+def copied(value):
+    def copy_kernel(from_ref, to_ref):
+        to_ref[...] = from_ref[...]
+
+    in_vmem = pl.BlockSpec(memory_space=pltpu.VMEM)
+    return pl.pallas_call(
+        copy_kernel,
+        in_specs=[in_vmem],
+        out_specs=in_vmem,
+        out_shape=pltpu.VMEM(value.shape, value.dtype),
+        compiler_params=pltpu.CompilerParams(vmem_limit_bytes=2**20),
+        name="copied",
+    )(pltpu.with_memory_space_constraint(value, pltpu.VMEM))
+
+
 def near_sum(kept, pieces):
     got = []
     for piece, k in zip(pieces, (1, -1, 2, -2)):
@@ -145,9 +160,10 @@
 def layer(tokens, routes, gates, gate_weight, up_weight, down_weight):
     expert = lax.axis_index(EP) // (lax.axis_size(EP) // EXPERTS)
     expert = expert.astype(jnp.int32).reshape(1)
-    order = row_order(tokens.shape[0])
-
-    def total_of(blocks):
+    order_near = row_order(tokens.shape[0])
+    order_next = copied(order_near)
+
+    def total_of(blocks, order):
         with_core = blocks + [other_core(block) for block in blocks]
         mine, sent = expert_of(expert, order, with_core, gate_weight, up_weight, down_weight)
         got = other_core(sent)
@@ -159,17 +175,19 @@
     own = jnp.concatenate([tokens, gate_columns(routes, gates)], axis=1)
     near = lax.all_gather(own, "ep_1", axis=0, tiled=True)
     half = near.shape[0] // 2
-    up = moved(near, take_from, 1)
-    down = moved(near, take_from, -1)
-    far_up = moved(up[:half], take_from, 1)
-    far_down = moved(down[half:], take_from, -1)
-
-    near_total = total_of([near])
-    next_total = total_of([up, down])
+    up_a = moved(near[:half], take_from, 1)
+    down_b = moved(near[half:], take_from, -1)
+    up_b = moved(near[half:], take_from, 1)
+    down_a = moved(near[:half], take_from, -1)
+    far_up = moved(up_a, take_from, 1)
+    far_down = moved(down_b, take_from, -1)
+
+    near_total = total_of([near], order_near)
+    next_total = total_of([up_a, up_b, down_a, down_b], order_next)
     to_up, to_down = next_total[: 2 * half], next_total[2 * half :]
     below_b = moved(to_up[half:], give_to, 1)
     above_b = moved(to_down[:half], give_to, -1)
-    far_total = total_of([far_up, far_down])
+    far_total = total_of([far_up, far_down], order_next)
     from_below = moved(far_total[:half], give_to, 1)
     from_above = moved(far_total[half:], give_to, -1)
     below_a = moved(to_up[:half] + from_below.astype(HIGH), give_to, 1)
@@ -194,4 +212,6 @@
         P(None, EP),
         P(EP, None),
     )
-    return jax.shard_map(layer, mesh=torus, in_specs=placed, out_specs=P(GROUPS_EP, None), check_vma=False)
+    return jax.shard_map(
+        layer, mesh=torus, in_specs=placed, out_specs=P(GROUPS_EP, None), check_vma=False
+    )

time: 181 us -> 182 us (level)
  waiting for transfers between devices: 66.6 us -> 57.9 us
  local copies, waits for them, and re-layouts: 8.28 us -> 14 us
  starting transfers between devices: 34.2 us -> 37.4 us
    ppermute x4 -> x6, waiting for transfers between devices: 23 us -> 16.4 us  [take_from(): lax.ppermute(value, axis, [((i + offset) % count, i) for i in range(count)])]
    unnamed x11 -> x21, local copies, waits for them, and re-layouts: 6.33 us -> 11.6 us
    ppermute x4 -> x6, starting transfers between devices: 6.58 us -> 10.1 us  [take_from(): lax.ppermute(value, axis, [((i + offset) % count, i) for i in range(count)])]
    ppermute x21 -> x23, waiting for transfers between devices: 43.6 us -> 41.5 us  [give_to(): lax.ppermute(value, axis, [(i, (i + offset) % count) for i in range(count)])]
    ppermute x21 -> x23, starting transfers between devices: 27.6 us -> 27.3 us  [give_to(): lax.ppermute(value, axis, [(i, (i + offset) % count) for i in range(count)])]
  transfers between devices with their start and end apart: 25 -> 29, of which waited for: 17 -> 15; matrix products, arithmetic and copies ran while one was open for 2% -> 2% of each run, Pallas kernels for 7% -> 7%
where the time goes in v3:
time: 182 us; the launch traced here: 181 us
  waiting for transfers between devices  57.9 us (32%)
  blocking collectives  53.7 us (30%)
  starting transfers between devices  37.4 us (21%)
  local copies, waits for them, and re-layouts  14 us (8%)
  Pallas kernels  13.4 us (7%)
  other arithmetic  4.03 us (2%)
    all_gather x1, blocking collectives, layer(): near = lax.all_gather(own, 'ep_1', axis=0, tiled=True)  53.7 us
    ppermute x23, waiting for transfers between devices, give_to(): lax.ppermute(value, axis, [(i, (i + offset) % count) for i in range(count)])  41.5 us
    ppermute x23, starting transfers between devices, give_to(): lax.ppermute(value, axis, [(i, (i + offset) % count) for i in range(count)])  27.3 us
    ppermute x6, waiting for transfers between devices, take_from(): lax.ppermute(value, axis, [((i + offset) % count, i) for i in range(count)])  16.4 us
    pallas_call x3, Pallas kernels, expert_of(): pl.pallas_call(functools.partial(expert_kernel, len(blocks)), in_specs=[p...  13.4 us
    unnamed x21, local copies, waits for them, and re-layouts  11.6 us
    ppermute x6, starting transfers between devices, take_from(): lax.ppermute(value, axis, [((i + offset) % count, i) for i in range(count)])  10.1 us
  transfers between devices with their start and end apart: 29, of which 15 were waited for; matrix products, arithmetic and copies ran while one was open for 2% of the time, Pallas kernels for 7%

profile of v3, /device:TPU:38, one launch (start us, length us, event | category | flops | bytes accessed | tf_op | source)
XLA Modules:
  0.0 180.7 jit_solution(18138711302844279664)
XLA Ops:
  1.7 53.7 %all-gather = bf16[16,4,7296]{2,1,0:T(4,128)(2,1)S(1)} all-gather(bf16[1,4,7296]{2,1,0:T(4,128)(2,1)S(1)} %maximum_bitcast_fusion), channel_id=1, replica_groups=mesh['groups'=2,'ep_0'=4,'ep_1'=16,'ep_2'=2] {'ep_1'}, dimensions={0}, use_global_device_ids=true | all-gather | bytes 992256 | tf_op jit(solution)/shard_map/all_gather | solution.py:176
  59.2 2.5 %collective-permute-start.5 = (bf16[32,7296]{1,0:T(8,128)(2,1)}, bf16[32,7296]{1,0:T(8,128)(2,1)S(1)}, u32[]{:S(2)}, u32[]{:S(2)}) collective-permute-start(bf16[32,7296]{1,0:T(8,128)(2,1)} %reshape.25), channel_id=1, source_target_pairs={{96,0},{0,32},{32,64},{64,96},{97,1},{1,33},{33,65},{65,97},{98,2}... | collective-permute-start | bytes 1400840 | tf_op jit(solution)/shard_map/ppermute | solution.py:25
  61.7 10.2 %collective-permute-done.2.refs_0_ = bf16[32,7296]{1,0:T(8,128)(2,1)S(1)} collective-permute-done((bf16[32,7296]{1,0:T(8,128)(2,1)}, bf16[32,7296]{1,0:T(8,128)(2,1)S(1)}, u32[]{:S(2)}, u32[]{:S(2)}) %collective-permute-start.2) | collective-permute-done | bytes 466976 | tf_op jit(solution)/shard_map/ppermute | solution.py:25
  72.7 3.6 %collective-permute-start.13 = (bf16[32,7296]{1,0:T(8,128)(2,1)S(1)}, bf16[32,7296]{1,0:T(8,128)(2,1)}, u32[]{:S(2)}, u32[]{:S(2)}) collective-permute-start(bf16[32,7296]{1,0:T(8,128)(2,1)S(1)} %collective-permute-done.5.refs_3_), channel_id=1, source_target_pairs={{96,0},{0,32},{32,64},{64,96},{97,1},{1,33},{33,65},{65,97},{98,2}... | collective-permute-start | bytes 1400840 | tf_op jit(solution)/shard_map/ppermute | solution.py:25
  76.3 5.4 %collective-permute-done.12.refs_0_ = bf16[32,7296]{1,0:T(8,128)(2,1)S(1)} collective-permute-done((bf16[32,7296]{1,0:T(8,128)(2,1)S(1)}, bf16[32,7296]{1,0:T(8,128)(2,1)S(1)}, u32[]{:S(2)}, u32[]{:S(2)}) %collective-permute-start.12) | collective-permute-done | bytes 466976 | tf_op jit(solution)/shard_map/ppermute | solution.py:25
  81.7 3.2 %collective-permute-start.4 = (bf16[32,7296]{1,0:T(8,128)(2,1)}, bf16[32,7296]{1,0:T(8,128)(2,1)}, u32[]{:S(2)}, u32[]{:S(2)}) collective-permute-start(bf16[32,7296]{1,0:T(8,128)(2,1)} %reshape.24), channel_id=1, source_target_pairs={{96,0},{0,32},{32,64},{64,96},{97,1},{1,33},{33,65},{65,97},{98,2}... | collective-permute-start | bytes 1400840 | tf_op jit(solution)/shard_map/ppermute | solution.py:25
  90.4 2.0 %copy-done.2 = bf16[7168,256]{1,0:T(8,128)(2,1)S(1)} copy-done((bf16[7168,256]{1,0:T(8,128)(2,1)S(1)}, bf16[7168,256]{1,0:T(8,128)(2,1)}, u32[]{:S(2)}) %copy-start.2) | copy-done | bytes 3670040
  92.4 2.0 %copy-done.3 = bf16[256,7168]{1,0:T(8,128)(2,1)S(1)} copy-done((bf16[256,7168]{1,0:T(8,128)(2,1)S(1)}, bf16[256,7168]{1,0:T(8,128)(2,1)}, u32[]{:S(2)}) %copy-start.3) | copy-done | bytes 3670040
  96.5 4.3 %expert.5 = (f32[64,7168]{1,0:T(8,128)S(1)}, bf16[64,7168]{1,0:T(8,128)(2,1)S(1)}) custom-call(s32[1]{0:T(128)} %bitcast.expert_ref, bf16[64,64]{1,0:T(8,128)(2,1)S(1)} %copied.1.order_ref, bf16[32,7296]{1,0:T(8,128)(2,1)S(1)} %copy-done.5, bf16[32,7296]{1,0:T(8,128)(2,1)} %collective-permute-done.13.refs_1_, bf16[32,7296]{1,0:T(8,128)(2,1)S(1)} %copy-done.7, ...), custom_call_target="tpu_custom_call" | custom-call | flops 1409286144 | bytes 16515072 | tf_op jit(solution)/shard_map/expert/pallas_call | solution.py:105
  105.6 5.9 %expert.4 = (f32[128,7168]{1,0:T(8,128)S(1)}, bf16[128,7168]{1,0:T(8,128)(2,1)S(1)}) custom-call(s32[1]{0:T(128)} %bitcast.expert_ref, bf16[64,64]{1,0:T(8,128)(2,1)S(1)} %copied.1.order_ref, bf16[32,7296]{1,0:T(8,128)(2,1)S(1)} %collective-permute-done.2.refs_0_, bf16[32,7296]{1,0:T(8,128)(2,1)S(1)} %collective-permute-done.3.refs_1_, ...), custom_call_target="tpu_custom_call" | custom-call | flops 2818572288 | bytes 22020096 | tf_op jit(solution)/shard_map/expert/pallas_call | solution.py:105
  112.0 3.2 %expert.3 = (f32[64,7168]{1,0:T(8,128)S(1)}, bf16[64,7168]{1,0:T(8,128)(2,1)S(1)}) custom-call(s32[1]{0:T(128)} %bitcast.expert_ref, bf16[64,64]{1,0:T(8,128)(2,1)S(1)} %fusion.10.order_ref.from_ref, bf16[64,7296]{1,0:T(8,128)(2,1)S(1)} %reshape.23.refs_0_, bf16[64,7296]{1,0:T(8,128)(2,1)S(1)} %collective-permute-done.refs_1_, ...), custom_call_target="tpu_custom_call" | custom-call | flops 1409286144 | bytes 16515072 | tf_op jit(solution)/shard_map/expert/pallas_call | solution.py:105
  118.6 3.2 %collective-permute-start.20 = (bf16[32,7168]{1,0:T(8,128)(2,1)S(1)}, bf16[32,7168]{1,0:T(8,128)(2,1)S(1)}, u32[]{:S(2)}, u32[]{:S(2)}) collective-permute-start(bf16[32,7168]{1,0:T(8,128)(2,1)S(1)} %get-tuple-element.26), channel_id=1, source_target_pairs={{0,32},{32,64},{64,96},{96,0},{1,33},{33,65},{65,97},{97,1},{2,34}... | collective-permute-start | bytes 1376264 | tf_op jit(solution)/shard_map/ppermute | solution.py:30
  121.8 7.4 %collective-permute-done.17 = bf16[32,7168]{1,0:T(8,128)(2,1)S(1)} collective-permute-done((bf16[32,7168]{1,0:T(8,128)(2,1)S(1)}, bf16[32,7168]{1,0:T(8,128)(2,1)S(1)}, u32[]{:S(2)}, u32[]{:S(2)}) %collective-permute-start.17) | collective-permute-done | bytes 458784 | tf_op jit(solution)/shard_map/ppermute | solution.py:30
  129.2 2.5 %collective-permute-done.21 = bf16[32,7168]{1,0:T(8,128)(2,1)S(1)} collective-permute-done((bf16[32,7168]{1,0:T(8,128)(2,1)S(1)}, bf16[32,7168]{1,0:T(8,128)(2,1)S(1)}, u32[]{:S(2)}, u32[]{:S(2)}) %collective-permute-start.21) | collective-permute-done | bytes 458784 | tf_op jit(solution)/shard_map/ppermute | solution.py:30
  134.1 7.4 %collective-permute-done.11 = bf16[32,7168]{1,0:T(8,128)(2,1)S(1)} collective-permute-done((bf16[32,7168]{1,0:T(8,128)(2,1)S(1)}, bf16[32,7168]{1,0:T(8,128)(2,1)S(1)}, u32[]{:S(2)}, u32[]{:S(2)}) %collective-permute-start.11) | collective-permute-done | bytes 458784 | tf_op jit(solution)/shard_map/ppermute | solution.py:30
  141.5 6.8 %collective-permute-done.18 = bf16[32,7168]{1,0:T(8,128)(2,1)S(1)} collective-permute-done((bf16[32,7168]{1,0:T(8,128)(2,1)S(1)}, bf16[32,7168]{1,0:T(8,128)(2,1)S(1)}, u32[]{:S(2)}, u32[]{:S(2)}) %collective-permute-start.18) | collective-permute-done | bytes 458784 | tf_op jit(solution)/shard_map/ppermute | solution.py:30
  148.3 2.2 %collective-permute-done.22 = bf16[32,7168]{1,0:T(8,128)(2,1)S(1)} collective-permute-done((bf16[32,7168]{1,0:T(8,128)(2,1)S(1)}, bf16[32,7168]{1,0:T(8,128)(2,1)S(1)}, u32[]{:S(2)}, u32[]{:S(2)}) %collective-permute-start.22) | collective-permute-done | bytes 458784 | tf_op jit(solution)/shard_map/ppermute | solution.py:30
  150.9 3.3 %collective-permute-start.23 = (bf16[16,7168]{1,0:T(8,128)(2,1)S(1)}, bf16[16,7168]{1,0:T(8,128)(2,1)S(1)}, u32[]{:S(2)}, u32[]{:S(2)}) collective-permute-start(bf16[16,7168]{1,0:T(8,128)(2,1)S(1)} %slice.116), channel_id=1, source_target_pairs={{0,30},{2,0},{4,2},{6,4},{8,6},{10,8},{12,10},{14,12},{16,14},{18,... | collective-permute-start | bytes 688136 | tf_op jit(solution)/shard_map/ppermute | solution.py:30
  154.4 4.1 %collective-permute-start.25 = (bf16[8,7168]{1,0:T(8,128)(2,1)S(1)}, bf16[8,7168]{1,0:T(8,128)(2,1)S(1)}, u32[]{:S(2)}, u32[]{:S(2)}) collective-permute-start(bf16[8,7168]{1,0:T(8,128)(2,1)S(1)} %get-tuple-element.32), channel_id=1, source_target_pairs={{0,28},{2,30},{4,0},{6,2},{8,4},{10,6},{12,8},{14,10},{16,12},{18,... | collective-permute-start | bytes 344072 | tf_op jit(solution)/shard_map/ppermute | solution.py:30
  158.5 4.0 %collective-permute-done.19 = bf16[16,7168]{1,0:T(8,128)(2,1)S(1)} collective-permute-done((bf16[16,7168]{1,0:T(8,128)(2,1)S(1)}, bf16[16,7168]{1,0:T(8,128)(2,1)S(1)}, u32[]{:S(2)}, u32[]{:S(2)}) %collective-permute-start.19) | collective-permute-done | bytes 229408 | tf_op jit(solution)/shard_map/ppermute | solution.py:30
  163.2 3.1 %collective-permute-start.26 = (bf16[4,7168]{1,0:T(4,128)(2,1)S(1)}, bf16[4,7168]{1,0:T(4,128)(2,1)S(1)}, u32[]{:S(2)}, u32[]{:S(2)}) collective-permute-start(bf16[4,7168]{1,0:T(4,128)(2,1)S(1)} %slice.154), channel_id=1, source_target_pairs={{0,16},{2,18},{4,20},{6,22},{8,24},{10,26},{12,28},{14,30},{16,0},... | collective-permute-start | bytes 172040 | tf_op jit(solution)/shard_map/ppermute | solution.py:30
  166.4 4.7 %collective-permute-start.27 = (bf16[4,7168]{1,0:T(4,128)(2,1)S(1)}, bf16[4,7168]{1,0:T(4,128)(2,1)S(1)}, u32[]{:S(2)}, u32[]{:S(2)}) collective-permute-start(bf16[4,7168]{1,0:T(4,128)(2,1)S(1)} %get-tuple-element.33), channel_id=1, source_target_pairs={{0,8},{2,10},{4,12},{6,14},{8,16},{10,18},{12,20},{14,22},{16,24},... | collective-permute-start | bytes 172040 | tf_op jit(solution)/shard_map/ppermute | solution.py:30
  172.4 4.0 %collective-permute-done.26 = bf16[4,7168]{1,0:T(4,128)(2,1)S(1)} collective-permute-done((bf16[4,7168]{1,0:T(4,128)(2,1)S(1)}, bf16[4,7168]{1,0:T(4,128)(2,1)S(1)}, u32[]{:S(2)}, u32[]{:S(2)}) %collective-permute-start.26) | collective-permute-done | bytes 57376 | tf_op jit(solution)/shard_map/ppermute | solution.py:30
  176.4 3.6 %collective-permute-done.28 = bf16[4,7168]{1,0:T(4,128)(2,1)S(1)} collective-permute-done((bf16[4,7168]{1,0:T(4,128)(2,1)S(1)}, bf16[4,7168]{1,0:T(4,128)(2,1)S(1)}, u32[]{:S(2)}, u32[]{:S(2)}) %collective-permute-start.28) | collective-permute-done | bytes 57376 | tf_op jit(solution)/shard_map/ppermute | solution.py:30
  (86 shorter events, 28.1 us)
Async XLA Ops:
  57.6 14.3 %collective-permute-start.2 = (bf16[32,7296]{1,0:T(8,128)(2,1)}, bf16[32,7296]{1,0:T(8,128)(2,1)S(1)}, u32[]{:S(2)}, u32[]{:S(2)}) collective-permute-start(bf16[32,7296]{1,0:T(8,128)(2,1)} %reshape.24), channel_id=1, source_target_pairs={{32,0},{64,32},{96,64},{0,96},{33,1},{65,33},{97,65},{1,97},{34,2}... | collective-permute-start | bytes 1400840 | tf_op jit(solution)/shard_map/ppermute | solution.py:25
  59.2 13.5 %collective-permute-start.5 = (bf16[32,7296]{1,0:T(8,128)(2,1)}, bf16[32,7296]{1,0:T(8,128)(2,1)S(1)}, u32[]{:S(2)}, u32[]{:S(2)}) collective-permute-start(bf16[32,7296]{1,0:T(8,128)(2,1)} %reshape.25), channel_id=1, source_target_pairs={{96,0},{0,32},{32,64},{64,96},{97,1},{1,33},{33,65},{65,97},{98,2}... | collective-permute-start | bytes 1400840 | tf_op jit(solution)/shard_map/ppermute | solution.py:25
  71.9 9.8 %collective-permute-start.12 = (bf16[32,7296]{1,0:T(8,128)(2,1)S(1)}, bf16[32,7296]{1,0:T(8,128)(2,1)S(1)}, u32[]{:S(2)}, u32[]{:S(2)}) collective-permute-start(bf16[32,7296]{1,0:T(8,128)(2,1)S(1)} %collective-permute-done.2.refs_0_), channel_id=1, source_target_pairs={{32,0},{64,32},{96,64},{0,96},{33,1},{65,33},{97,65},{1,97},{34,2}... | collective-permute-start | bytes 1400840 | tf_op jit(solution)/shard_map/ppermute | solution.py:25
  72.7 12.2 %collective-permute-start.13 = (bf16[32,7296]{1,0:T(8,128)(2,1)S(1)}, bf16[32,7296]{1,0:T(8,128)(2,1)}, u32[]{:S(2)}, u32[]{:S(2)}) collective-permute-start(bf16[32,7296]{1,0:T(8,128)(2,1)S(1)} %collective-permute-done.5.refs_3_), channel_id=1, source_target_pairs={{96,0},{0,32},{32,64},{64,96},{97,1},{1,33},{33,65},{65,97},{98,2}... | collective-permute-start | bytes 1400840 | tf_op jit(solution)/shard_map/ppermute | solution.py:25
  81.7 19.8 %collective-permute-start.3 = (bf16[32,7296]{1,0:T(8,128)(2,1)}, bf16[32,7296]{1,0:T(8,128)(2,1)S(1)}, u32[]{:S(2)}, u32[]{:S(2)}) collective-permute-start(bf16[32,7296]{1,0:T(8,128)(2,1)} %reshape.25), channel_id=1, source_target_pairs={{32,0},{64,32},{96,64},{0,96},{33,1},{65,33},{97,65},{1,97},{34,2}... | collective-permute-start | bytes 1400840 | tf_op jit(solution)/shard_map/ppermute | solution.py:25
  81.7 19.9 %collective-permute-start.4 = (bf16[32,7296]{1,0:T(8,128)(2,1)}, bf16[32,7296]{1,0:T(8,128)(2,1)}, u32[]{:S(2)}, u32[]{:S(2)}) collective-permute-start(bf16[32,7296]{1,0:T(8,128)(2,1)} %reshape.24), channel_id=1, source_target_pairs={{96,0},{0,32},{32,64},{64,96},{97,1},{1,33},{33,65},{65,97},{98,2}... | collective-permute-start | bytes 1400840 | tf_op jit(solution)/shard_map/ppermute | solution.py:25
  84.9 17.0 %collective-permute-start.6 = (bf16[32,7296]{1,0:T(8,128)(2,1)S(1)}, bf16[32,7296]{1,0:T(8,128)(2,1)}, u32[]{:S(2)}, u32[]{:S(2)}) collective-permute-start(bf16[32,7296]{1,0:T(8,128)(2,1)S(1)} %collective-permute-done.2.refs_0_), channel_id=1, source_target_pairs={{0,1},{1,0},{2,3},{3,2},{4,5},{5,4},{6,7},{7,6},{8,9},{9,8},{10,11... | collective-permute-start | bytes 1400840 | tf_op jit(solution)/shard_map/ppermute | solution.py:30
  88.2 23.8 %collective-permute-start = (bf16[64,7296]{1,0:T(8,128)(2,1)S(1)}, bf16[64,7296]{1,0:T(8,128)(2,1)S(1)}, u32[]{:S(2)}, u32[]{:S(2)}) collective-permute-start(bf16[64,7296]{1,0:T(8,128)(2,1)S(1)} %reshape.23.refs_0_), channel_id=1, source_target_pairs={{0,1},{1,0},{2,3},{3,2},{4,5},{5,4},{6,7},{7,6},{8,9},{9,8},{10,11... | collective-permute-start | bytes 2801672 | tf_op jit(solution)/shard_map/ppermute | solution.py:30
  100.8 14.6 %collective-permute-start.16 = (bf16[64,7168]{1,0:T(8,128)(2,1)S(1)}, bf16[64,7168]{1,0:T(8,128)(2,1)S(1)}, u32[]{:S(2)}, u32[]{:S(2)}) collective-permute-start(bf16[64,7168]{1,0:T(8,128)(2,1)S(1)} %get-tuple-element.16), channel_id=1, source_target_pairs={{0,1},{1,0},{2,3},{3,2},{4,5},{5,4},{6,7},{7,6},{8,9},{9,8},{10,11... | collective-permute-start | bytes 2752520 | tf_op jit(solution)/shard_map/ppermute | solution.py:30
  111.5 6.4 %collective-permute-start.10 = (bf16[128,7168]{1,0:T(8,128)(2,1)S(1)}, bf16[128,7168]{1,0:T(8,128)(2,1)S(1)}, u32[]{:S(2)}, u32[]{:S(2)}) collective-permute-start(bf16[128,7168]{1,0:T(8,128)(2,1)S(1)} %get-tuple-element.14), channel_id=1, source_target_pairs={{0,1},{1,0},{2,3},{3,2},{4,5},{5,4},{6,7},{7,6},{8,9},{9,8},{10,11... | collective-permute-start | bytes 5505032 | tf_op jit(solution)/shard_map/ppermute | solution.py:30
  115.2 18.8 %collective-permute-start.1 = (bf16[64,7168]{1,0:T(8,128)(2,1)S(1)}, bf16[64,7168]{1,0:T(8,128)(2,1)S(1)}, u32[]{:S(2)}, u32[]{:S(2)}) collective-permute-start(bf16[64,7168]{1,0:T(8,128)(2,1)S(1)} %get-tuple-element.12), channel_id=1, source_target_pairs={{0,1},{1,0},{2,3},{3,2},{4,5},{5,4},{6,7},{7,6},{8,9},{9,8},{10,11... | collective-permute-start | bytes 2752520 | tf_op jit(solution)/shard_map/ppermute | solution.py:30
  115.7 13.5 %collective-permute-start.17 = (bf16[32,7168]{1,0:T(8,128)(2,1)S(1)}, bf16[32,7168]{1,0:T(8,128)(2,1)S(1)}, u32[]{:S(2)}, u32[]{:S(2)}) collective-permute-start(bf16[32,7168]{1,0:T(8,128)(2,1)S(1)} %get-tuple-element.29), channel_id=1, source_target_pairs={{0,32},{32,64},{64,96},{96,0},{1,33},{33,65},{65,97},{97,1},{2,34}... | collective-permute-start | bytes 1376264 | tf_op jit(solution)/shard_map/ppermute | solution.py:30
  117.1 14.6 %collective-permute-start.21 = (bf16[32,7168]{1,0:T(8,128)(2,1)S(1)}, bf16[32,7168]{1,0:T(8,128)(2,1)S(1)}, u32[]{:S(2)}, u32[]{:S(2)}) collective-permute-start(bf16[32,7168]{1,0:T(8,128)(2,1)S(1)} %get-tuple-element.30), channel_id=1, source_target_pairs={{0,96},{32,0},{64,32},{96,64},{1,97},{33,1},{65,33},{97,65},{2,98}... | collective-permute-start | bytes 1376264 | tf_op jit(solution)/shard_map/ppermute | solution.py:30
  118.5 23.0 %collective-permute-start.11 = (bf16[32,7168]{1,0:T(8,128)(2,1)S(1)}, bf16[32,7168]{1,0:T(8,128)(2,1)S(1)}, u32[]{:S(2)}, u32[]{:S(2)}) collective-permute-start(bf16[32,7168]{1,0:T(8,128)(2,1)S(1)} %get-tuple-element.25), channel_id=1, source_target_pairs={{0,96},{32,0},{64,32},{96,64},{1,97},{33,1},{65,33},{97,65},{2,98}... | collective-permute-start | bytes 1376264 | tf_op jit(solution)/shard_map/ppermute | solution.py:30
  118.6 22.9 %collective-permute-start.20 = (bf16[32,7168]{1,0:T(8,128)(2,1)S(1)}, bf16[32,7168]{1,0:T(8,128)(2,1)S(1)}, u32[]{:S(2)}, u32[]{:S(2)}) collective-permute-start(bf16[32,7168]{1,0:T(8,128)(2,1)S(1)} %get-tuple-element.26), channel_id=1, source_target_pairs={{0,32},{32,64},{64,96},{96,0},{1,33},{33,65},{65,97},{97,1},{2,34}... | collective-permute-start | bytes 1376264 | tf_op jit(solution)/shard_map/ppermute | solution.py:30
  131.8 16.4 %collective-permute-start.18 = (bf16[32,7168]{1,0:T(8,128)(2,1)S(1)}, bf16[32,7168]{1,0:T(8,128)(2,1)S(1)}, u32[]{:S(2)}, u32[]{:S(2)}) collective-permute-start(bf16[32,7168]{1,0:T(8,128)(2,1)S(1)} %get-tuple-element.21), channel_id=1, source_target_pairs={{0,32},{32,64},{64,96},{96,0},{1,33},{33,65},{65,97},{97,1},{2,34}... | collective-permute-start | bytes 1376264 | tf_op jit(solution)/shard_map/ppermute | solution.py:30
  132.0 18.5 %collective-permute-start.22 = (bf16[32,7168]{1,0:T(8,128)(2,1)S(1)}, bf16[32,7168]{1,0:T(8,128)(2,1)S(1)}, u32[]{:S(2)}, u32[]{:S(2)}) collective-permute-start(bf16[32,7168]{1,0:T(8,128)(2,1)S(1)} %get-tuple-element.22), channel_id=1, source_target_pairs={{0,96},{32,0},{64,32},{96,64},{1,97},{33,1},{65,33},{97,65},{2,98}... | collective-permute-start | bytes 1376264 | tf_op jit(solution)/shard_map/ppermute | solution.py:30
  150.8 11.7 %collective-permute-start.19 = (bf16[16,7168]{1,0:T(8,128)(2,1)S(1)}, bf16[16,7168]{1,0:T(8,128)(2,1)S(1)}, u32[]{:S(2)}, u32[]{:S(2)}) collective-permute-start(bf16[16,7168]{1,0:T(8,128)(2,1)S(1)} %slice.153), channel_id=1, source_target_pairs={{0,2},{2,4},{4,6},{6,8},{8,10},{10,12},{12,14},{14,16},{16,18},{18... | collective-permute-start | bytes 688136 | tf_op jit(solution)/shard_map/ppermute | solution.py:30
  150.9 11.6 %collective-permute-start.23 = (bf16[16,7168]{1,0:T(8,128)(2,1)S(1)}, bf16[16,7168]{1,0:T(8,128)(2,1)S(1)}, u32[]{:S(2)}, u32[]{:S(2)}) collective-permute-start(bf16[16,7168]{1,0:T(8,128)(2,1)S(1)} %slice.116), channel_id=1, source_target_pairs={{0,30},{2,0},{4,2},{6,4},{8,6},{10,8},{12,10},{14,12},{16,14},{18,... | collective-permute-start | bytes 688136 | tf_op jit(solution)/shard_map/ppermute | solution.py:30
  154.3 8.3 %collective-permute-start.24 = (bf16[8,7168]{1,0:T(8,128)(2,1)S(1)}, bf16[8,7168]{1,0:T(8,128)(2,1)S(1)}, u32[]{:S(2)}, u32[]{:S(2)}) collective-permute-start(bf16[8,7168]{1,0:T(8,128)(2,1)S(1)} %get-tuple-element.31), channel_id=1, source_target_pairs={{0,4},{2,6},{4,8},{6,10},{8,12},{10,14},{12,16},{14,18},{16,20},{1... | collective-permute-start | bytes 344072 | tf_op jit(solution)/shard_map/ppermute | solution.py:30
  154.4 8.7 %collective-permute-start.25 = (bf16[8,7168]{1,0:T(8,128)(2,1)S(1)}, bf16[8,7168]{1,0:T(8,128)(2,1)S(1)}, u32[]{:S(2)}, u32[]{:S(2)}) collective-permute-start(bf16[8,7168]{1,0:T(8,128)(2,1)S(1)} %get-tuple-element.32), channel_id=1, source_target_pairs={{0,28},{2,30},{4,0},{6,2},{8,4},{10,6},{12,8},{14,10},{16,12},{18,... | collective-permute-start | bytes 344072 | tf_op jit(solution)/shard_map/ppermute | solution.py:30
  163.2 13.2 %collective-permute-start.26 = (bf16[4,7168]{1,0:T(4,128)(2,1)S(1)}, bf16[4,7168]{1,0:T(4,128)(2,1)S(1)}, u32[]{:S(2)}, u32[]{:S(2)}) collective-permute-start(bf16[4,7168]{1,0:T(4,128)(2,1)S(1)} %slice.154), channel_id=1, source_target_pairs={{0,16},{2,18},{4,20},{6,22},{8,24},{10,26},{12,28},{14,30},{16,0},... | collective-permute-start | bytes 172040 | tf_op jit(solution)/shard_map/ppermute | solution.py:30
  166.4 10.0 %collective-permute-start.27 = (bf16[4,7168]{1,0:T(4,128)(2,1)S(1)}, bf16[4,7168]{1,0:T(4,128)(2,1)S(1)}, u32[]{:S(2)}, u32[]{:S(2)}) collective-permute-start(bf16[4,7168]{1,0:T(4,128)(2,1)S(1)} %get-tuple-element.33), channel_id=1, source_target_pairs={{0,8},{2,10},{4,12},{6,14},{8,16},{10,18},{12,20},{14,22},{16,24},... | collective-permute-start | bytes 172040 | tf_op jit(solution)/shard_map/ppermute | solution.py:30
  171.1 8.9 %collective-permute-start.28 = (bf16[4,7168]{1,0:T(4,128)(2,1)S(1)}, bf16[4,7168]{1,0:T(4,128)(2,1)S(1)}, u32[]{:S(2)}, u32[]{:S(2)}) collective-permute-start(bf16[4,7168]{1,0:T(4,128)(2,1)S(1)} %get-tuple-element.34), channel_id=1, source_target_pairs={{0,24},{2,26},{4,28},{6,30},{8,0},{10,2},{12,4},{14,6},{16,8},{18,... | collective-permute-start | bytes 172040 | tf_op jit(solution)/shard_map/ppermute | solution.py:30
  (15 other events, 69.4 us)

commit v4 on v3

--- a/solution.py
+++ b/solution.py
@@ -53,7 +53,7 @@
     return (wanted[:, None] == jnp.arange(count * tok_rows, dtype=jnp.int32)).astype(LOW)
 
 
-def expert_kernel(blocks, expert_ref, order_ref, *refs):
+def expert_kernel(blocks, expert_ref, *refs):
     row_refs = refs[:blocks]
     gate_ref, up_ref, down_ref, mine_ref, other_ref = refs[blocks : blocks + 5]
     gate_sum, up_sum, hidden_ref, weight_ref = refs[blocks + 5 :]
@@ -73,16 +73,11 @@
     gate_act = gate_sum[...]
     hidden = (gate_act / (1.0 + jnp.exp(-gate_act)) * up_sum[...]).astype(LOW)
     columns = jnp.concatenate([r[:, width:] for r in row_refs], axis=0)
-    order = order_ref[...]
-    count = order.shape[0]
-    index = lax.broadcasted_iota(jnp.int32, (count, LANES), 1)
+    hidden_ref[...] = hidden
+    index = lax.broadcasted_iota(jnp.int32, columns.shape, 1)
     mine = (lax.rem(index, EXPERTS) == expert_ref[0]) & (index < 3 * EXPERTS)
-    for at in range(0, hidden.shape[0], count):
-        moved = jnp.dot(order, hidden[at : at + count], preferred_element_type=HIGH)
-        hidden_ref[at : at + count, :] = moved.astype(LOW)
-        moved = jnp.dot(order, columns[at : at + count], preferred_element_type=HIGH)
-        weight = jnp.sum(jnp.where(mine, moved, 0.0), axis=1, keepdims=True)
-        weight_ref[at : at + count, :] = jnp.broadcast_to(weight, (count, LANES))
+    weight = jnp.sum(jnp.where(mine, columns.astype(HIGH), 0.0), axis=1, keepdims=True)
+    weight_ref[...] = jnp.broadcast_to(weight, weight_ref.shape)
 
     def give(k, carry):
         at = pl.ds(pl.multiple_of(k * chunk, chunk), chunk)
@@ -96,10 +91,10 @@
     lax.fori_loop(0, STEPS, give, 0)
 
 
-def expert_of(expert, order, blocks, gate_weight, up_weight, down_weight):
+def expert_of(expert, blocks, gate_weight, up_weight, down_weight):
     width, units = gate_weight.shape
     rows = sum(block.shape[0] for block in blocks)
-    operands = [order, *blocks, gate_weight, up_weight, down_weight]
+    operands = [*blocks, gate_weight, up_weight, down_weight]
     operands = [pltpu.with_memory_space_constraint(value, pltpu.VMEM) for value in operands]
     in_vmem = pl.BlockSpec(memory_space=pltpu.VMEM)
     return pl.pallas_call(
@@ -160,12 +155,11 @@
 def layer(tokens, routes, gates, gate_weight, up_weight, down_weight):
     expert = lax.axis_index(EP) // (lax.axis_size(EP) // EXPERTS)
     expert = expert.astype(jnp.int32).reshape(1)
-    order_near = row_order(tokens.shape[0])
-    order_next = copied(order_near)
-
-    def total_of(blocks, order):
+    order = copied(row_order(tokens.shape[0]))
+
+    def total_of(blocks):
         with_core = blocks + [other_core(block) for block in blocks]
-        mine, sent = expert_of(expert, order, with_core, gate_weight, up_weight, down_weight)
+        mine, sent = expert_of(expert, with_core, gate_weight, up_weight, down_weight)
         got = other_core(sent)
         return mine + got.astype(HIGH)
 
@@ -173,7 +167,7 @@
         return move(value.astype(LOW), "ep_0", offset)
 
     own = jnp.concatenate([tokens, gate_columns(routes, gates)], axis=1)
-    near = lax.all_gather(own, "ep_1", axis=0, tiled=True)
+    near = lax.optimization_barrier(lax.all_gather(own, "ep_1", axis=0, tiled=True))
     half = near.shape[0] // 2
     up_a = moved(near[:half], take_from, 1)
     down_b = moved(near[half:], take_from, -1)
@@ -182,19 +176,20 @@
     far_up = moved(up_a, take_from, 1)
     far_down = moved(down_b, take_from, -1)
 
-    near_total = total_of([near], order_near)
-    next_total = total_of([up_a, up_b, down_a, down_b], order_next)
-    to_up, to_down = next_total[: 2 * half], next_total[2 * half :]
-    below_b = moved(to_up[half:], give_to, 1)
-    above_b = moved(to_down[:half], give_to, -1)
-    far_total = total_of([far_up, far_down], order_next)
+    near_total = total_of([near])
+    total_b = total_of([up_b, down_a])
+    below_b = moved(total_b[:half], give_to, 1)
+    above_b = moved(total_b[half:], give_to, -1)
+    far_total = total_of([far_up, far_down])
     from_below = moved(far_total[:half], give_to, 1)
     from_above = moved(far_total[half:], give_to, -1)
-    below_a = moved(to_up[:half] + from_below.astype(HIGH), give_to, 1)
-    above_a = moved(to_down[half:] + from_above.astype(HIGH), give_to, -1)
+    total_a = total_of([up_a, down_b])
+    below_a = moved(total_a[:half] + from_below.astype(HIGH), give_to, 1)
+    above_a = moved(total_a[half:] + from_above.astype(HIGH), give_to, -1)
     top = near_total[:half] + above_b.astype(HIGH) + below_a.astype(HIGH)
     bottom = near_total[half:] + below_b.astype(HIGH) + above_a.astype(HIGH)
-    total = jnp.concatenate([top, bottom], axis=0)
+    total = jnp.concatenate([top, bottom], axis=0).astype(LOW)
+    total = jnp.dot(order, total, preferred_element_type=HIGH)
     n = total.shape[0] // 8
     cut = [total[i * n : j * n].astype(LOW) for i, j in ((2, 4), (4, 6), (6, 7), (7, 8))]
     return far_sum(near_sum(total[: 2 * n], cut)).astype(LOW)

time: 182 us -> 184 us (1.011)
  waiting for transfers between devices: 57.9 us -> 50.9 us
  local copies, waits for them, and re-layouts: 14 us -> 19 us
  Pallas kernels: 13.4 us -> 17.8 us
    ppermute x6, waiting for transfers between devices: 16.4 us -> 8.61 us  [take_from(): lax.ppermute(value, axis, [((i + offset) % count, i) for i in range(count)])]
    unnamed x21 -> x29, local copies, waits for them, and re-layouts: 11.6 us -> 17.9 us
    pallas_call x3 -> x4, Pallas kernels: 13.4 us -> 17.8 us  [expert_of(): pl.pallas_call(functools.partial(expert_kernel, len(blocks)), in_specs=[p...]
    ppermute x23 -> x24, waiting for transfers between devices: 41.5 us -> 42.3 us  [give_to(): lax.ppermute(value, axis, [(i, (i + offset) % count) for i in range(count)])]
    ppermute x23 -> x24, starting transfers between devices: 27.3 us -> 26.8 us  [give_to(): lax.ppermute(value, axis, [(i, (i + offset) % count) for i in range(count)])]
  transfers between devices with their start and end apart: 29 -> 30, of which waited for: 15 -> 10; matrix products, arithmetic and copies ran while one was open for 2% -> 1% of each run, Pallas kernels for 7% -> 10%
where the time goes in v4:
time: 184 us; the launch traced here: 183 us
  blocking collectives  53.7 us (29%)
  waiting for transfers between devices  50.9 us (28%)
  starting transfers between devices  36.5 us (20%)
  local copies, waits for them, and re-layouts  19 us (10%)
  Pallas kernels  17.8 us (10%)
  other arithmetic  4.93 us (3%)
    all_gather x1, blocking collectives, layer(): lax.all_gather(own, 'ep_1', axis=0, tiled=True)  53.7 us
    ppermute x24, waiting for transfers between devices, give_to(): lax.ppermute(value, axis, [(i, (i + offset) % count) for i in range(count)])  42.3 us
    ppermute x24, starting transfers between devices, give_to(): lax.ppermute(value, axis, [(i, (i + offset) % count) for i in range(count)])  26.8 us
    unnamed x29, local copies, waits for them, and re-layouts  17.9 us
    pallas_call x4, Pallas kernels, expert_of(): pl.pallas_call(functools.partial(expert_kernel, len(blocks)), in_specs=[p...  17.8 us
    ppermute x6, starting transfers between devices, take_from(): lax.ppermute(value, axis, [((i + offset) % count, i) for i in range(count)])  9.71 us
    ppermute x6, waiting for transfers between devices, take_from(): lax.ppermute(value, axis, [((i + offset) % count, i) for i in range(count)])  8.61 us
  transfers between devices with their start and end apart: 30, of which 10 were waited for; matrix products, arithmetic and copies ran while one was open for 1% of the time, Pallas kernels for 10%

profile of v4, /device:TPU:38, one launch (start us, length us, event | category | flops | bytes accessed | tf_op | source)
XLA Modules:
  0.0 183.4 jit_solution(15018009036544226567)
XLA Ops:
  1.7 53.7 %all-gather = bf16[16,4,7296]{2,1,0:T(4,128)(2,1)S(1)} all-gather(bf16[1,4,7296]{2,1,0:T(4,128)(2,1)S(1)} %maximum_bitcast_fusion), channel_id=1, replica_groups=mesh['groups'=2,'ep_0'=4,'ep_1'=16,'ep_2'=2] {'ep_1'}, dimensions={0}, use_global_device_ids=true | all-gather | bytes 992256 | tf_op jit(solution)/shard_map/all_gather | solution.py:170
  57.2 2.5 %collective-permute-start.3 = (bf16[32,7296]{1,0:T(8,128)(2,1)S(1)}, bf16[32,7296]{1,0:T(8,128)(2,1)S(1)}, u32[]{:S(2)}, u32[]{:S(2)}) collective-permute-start(bf16[32,7296]{1,0:T(8,128)(2,1)S(1)} %get-tuple-element.28), channel_id=1, source_target_pairs={{96,0},{0,32},{32,64},{64,96},{97,1},{1,33},{33,65},{65,97},{98,2}... | collective-permute-start | bytes 1400840 | tf_op jit(solution)/shard_map/ppermute | solution.py:25
  59.7 3.2 %collective-permute-start.9 = (bf16[32,7296]{1,0:T(8,128)(2,1)}, bf16[32,7296]{1,0:T(8,128)(2,1)}, u32[]{:S(2)}, u32[]{:S(2)}) collective-permute-start(bf16[32,7296]{1,0:T(8,128)(2,1)} %get-tuple-element.27), channel_id=1, source_target_pairs={{96,0},{0,32},{32,64},{64,96},{97,1},{1,33},{33,65},{65,97},{98,2}... | collective-permute-start | bytes 1400840 | tf_op jit(solution)/shard_map/ppermute | solution.py:25
  62.9 5.6 %collective-permute-done.2.refs_0_ = bf16[32,7296]{1,0:T(8,128)(2,1)S(1)} collective-permute-done((bf16[32,7296]{1,0:T(8,128)(2,1)}, bf16[32,7296]{1,0:T(8,128)(2,1)S(1)}, u32[]{:S(2)}, u32[]{:S(2)}) %collective-permute-start.2) | collective-permute-done | bytes 466976 | tf_op jit(solution)/shard_map/ppermute | solution.py:25
  70.6 3.0 %collective-permute-done.8.refs_0_ = bf16[32,7296]{1,0:T(8,128)(2,1)} collective-permute-done((bf16[32,7296]{1,0:T(8,128)(2,1)S(1)}, bf16[32,7296]{1,0:T(8,128)(2,1)}, u32[]{:S(2)}, u32[]{:S(2)}) %collective-permute-start.8) | collective-permute-done | bytes 466976 | tf_op jit(solution)/shard_map/ppermute | solution.py:25
  74.9 3.2 %collective-permute-start.14 = (bf16[32,7296]{1,0:T(8,128)(2,1)}, bf16[32,7296]{1,0:T(8,128)(2,1)}, u32[]{:S(2)}, u32[]{:S(2)}) collective-permute-start(bf16[32,7296]{1,0:T(8,128)(2,1)} %collective-permute-done.9.refs_1_), channel_id=1, source_target_pairs={{96,0},{0,32},{32,64},{64,96},{97,1},{1,33},{33,65},{65,97},{98,2}... | collective-permute-start | bytes 1400840 | tf_op jit(solution)/shard_map/ppermute | solution.py:25
  78.2 2.0 %copy-done = bf16[7168,256]{1,0:T(8,128)(2,1)S(1)} copy-done((bf16[7168,256]{1,0:T(8,128)(2,1)S(1)}, bf16[7168,256]{1,0:T(8,128)(2,1)}, u32[]{:S(2)}) %copy-start) | copy-done | bytes 3670040
  80.2 2.0 %copy-done.3 = bf16[7168,256]{1,0:T(8,128)(2,1)S(1)} copy-done((bf16[7168,256]{1,0:T(8,128)(2,1)S(1)}, bf16[7168,256]{1,0:T(8,128)(2,1)}, u32[]{:S(2)}) %copy-start.3) | copy-done | bytes 3670040
  82.3 2.0 %copy-done.5 = bf16[256,7168]{1,0:T(8,128)(2,1)S(1)} copy-done((bf16[256,7168]{1,0:T(8,128)(2,1)S(1)}, bf16[256,7168]{1,0:T(8,128)(2,1)}, u32[]{:S(2)}) %copy-start.5) | copy-done | bytes 3670040
  87.4 5.0 %expert.5 = (f32[64,7168]{1,0:T(8,128)S(1)}, bf16[64,7168]{1,0:T(8,128)(2,1)}) custom-call(s32[1]{0:T(128)} %bitcast.expert_ref, bf16[32,7296]{1,0:T(8,128)(2,1)S(1)} %copy-done.8, bf16[32,7296]{1,0:T(8,128)(2,1)S(1)} %copy-done.10, bf16[32,7296]{1,0:T(8,128)(2,1)S(1)} %copy-done.12, bf16[32,7296]{1,0:T(8,128)(2,1)} %collective-permute-done.5.refs_3_, ...), custom_call_target="tpu_custom_call" | custom-call | flops 1409286144 | bytes 16515072 | tf_op jit(solution)/shard_map/expert/pallas_call | solution.py:100
  95.9 2.0 %copy-done.4 = bf16[7168,256]{1,0:T(8,128)(2,1)S(1)} copy-done((bf16[7168,256]{1,0:T(8,128)(2,1)S(1)}, bf16[7168,256]{1,0:T(8,128)(2,1)}, u32[]{:S(2)}) %copy-start.4) | copy-done | bytes 3670040
  97.9 2.0 %copy-done.6 = bf16[256,7168]{1,0:T(8,128)(2,1)S(1)} copy-done((bf16[256,7168]{1,0:T(8,128)(2,1)S(1)}, bf16[256,7168]{1,0:T(8,128)(2,1)}, u32[]{:S(2)}) %copy-start.6) | copy-done | bytes 3670040
  99.9 4.6 %expert.6 = (f32[64,7168]{1,0:T(8,128)S(1)}, bf16[64,7168]{1,0:T(8,128)(2,1)S(1)}) custom-call(s32[1]{0:T(128)} %bitcast.expert_ref, bf16[32,7296]{1,0:T(8,128)(2,1)} %collective-permute-done.8.refs_0_, bf16[32,7296]{1,0:T(8,128)(2,1)} %collective-permute-done.9.refs_1_, bf16[32,7296]{1,0:T(8,128)(2,1)} %collective-permute-done.10.refs_2_, ...), custom_call_target="tpu_custom_call" | custom-call | flops 1409286144 | bytes 16515072 | tf_op jit(solution)/shard_map/expert/pallas_call | solution.py:100
  105.0 4.2 %expert.4 = (f32[64,7168]{1,0:T(8,128)S(1)}, bf16[64,7168]{1,0:T(8,128)(2,1)S(1)}) custom-call(s32[1]{0:T(128)} %bitcast.expert_ref, bf16[64,7296]{1,0:T(8,128)(2,1)S(1)} %reshape.23.refs_0_, bf16[64,7296]{1,0:T(8,128)(2,1)} %collective-permute-done.refs_1_, bf16[7168,256]{1,0:T(8,128)(2,1)S(1)} %copy-done.2, bf16[7168,256]{1,0:T(8,128)(2,1)S(1)} %copy-done.4, ...), custom_call_target="tpu_custom_call" | custom-call | flops 1409286144 | bytes 16515072 | tf_op jit(solution)/shard_map/expert/pallas_call | solution.py:100
  109.7 4.0 %expert.7 = (f32[64,7168]{1,0:T(8,128)S(1)}, bf16[64,7168]{1,0:T(8,128)(2,1)S(1)}) custom-call(s32[1]{0:T(128)} %bitcast.expert_ref, bf16[32,7296]{1,0:T(8,128)(2,1)S(1)} %collective-permute-done.13.refs_0_, bf16[32,7296]{1,0:T(8,128)(2,1)} %collective-permute-done.14.refs_1_, bf16[32,7296]{1,0:T(8,128)(2,1)S(1)} %collective-permute-done.15.refs_2_, ...), custom_call_target="tpu_custom_call" | custom-call | flops 1409286144 | bytes 16515072 | tf_op jit(solution)/shard_map/expert/pallas_call | solution.py:100
  120.1 18.0 %collective-permute-done.18 = bf16[32,7168]{1,0:T(8,128)(2,1)S(1)} collective-permute-done((bf16[32,7168]{1,0:T(8,128)(2,1)S(1)}, bf16[32,7168]{1,0:T(8,128)(2,1)S(1)}, u32[]{:S(2)}, u32[]{:S(2)}) %collective-permute-start.18) | collective-permute-done | bytes 458784 | tf_op jit(solution)/shard_map/ppermute | solution.py:30
  141.9 9.7 %collective-permute-done.19 = bf16[32,7168]{1,0:T(8,128)(2,1)S(1)} collective-permute-done((bf16[32,7168]{1,0:T(8,128)(2,1)S(1)}, bf16[32,7168]{1,0:T(8,128)(2,1)S(1)}, u32[]{:S(2)}, u32[]{:S(2)}) %collective-permute-start.19) | collective-permute-done | bytes 458784 | tf_op jit(solution)/shard_map/ppermute | solution.py:30
  153.9 3.2 %collective-permute-start.24 = (bf16[16,7168]{1,0:T(8,128)(2,1)S(1)}, bf16[16,7168]{1,0:T(8,128)(2,1)S(1)}, u32[]{:S(2)}, u32[]{:S(2)}) collective-permute-start(bf16[16,7168]{1,0:T(8,128)(2,1)S(1)} %get-tuple-element.32), channel_id=1, source_target_pairs={{0,30},{2,0},{4,2},{6,4},{8,6},{10,8},{12,10},{14,12},{16,14},{18,... | collective-permute-start | bytes 688136 | tf_op jit(solution)/shard_map/ppermute | solution.py:30
  157.3 4.1 %collective-permute-start.26 = (bf16[8,7168]{1,0:T(8,128)(2,1)S(1)}, bf16[8,7168]{1,0:T(8,128)(2,1)S(1)}, u32[]{:S(2)}, u32[]{:S(2)}) collective-permute-start(bf16[8,7168]{1,0:T(8,128)(2,1)S(1)} %get-tuple-element.30), channel_id=1, source_target_pairs={{0,28},{2,30},{4,0},{6,2},{8,4},{10,6},{12,8},{14,10},{16,12},{18,... | collective-permute-start | bytes 344072 | tf_op jit(solution)/shard_map/ppermute | solution.py:30
  161.4 3.2 %collective-permute-done.23 = bf16[16,7168]{1,0:T(8,128)(2,1)S(1)} collective-permute-done((bf16[16,7168]{1,0:T(8,128)(2,1)S(1)}, bf16[16,7168]{1,0:T(8,128)(2,1)S(1)}, u32[]{:S(2)}, u32[]{:S(2)}) %collective-permute-start.23) | collective-permute-done | bytes 229408 | tf_op jit(solution)/shard_map/ppermute | solution.py:30
  165.5 3.3 %collective-permute-start.27 = (bf16[4,7168]{1,0:T(4,128)(2,1)S(1)}, bf16[4,7168]{1,0:T(4,128)(2,1)S(1)}, u32[]{:S(2)}, u32[]{:S(2)}) collective-permute-start(bf16[4,7168]{1,0:T(4,128)(2,1)S(1)} %slice.146), channel_id=1, source_target_pairs={{0,16},{2,18},{4,20},{6,22},{8,24},{10,26},{12,28},{14,30},{16,0},... | collective-permute-start | bytes 172040 | tf_op jit(solution)/shard_map/ppermute | solution.py:30
  168.9 4.5 %collective-permute-start.28 = (bf16[4,7168]{1,0:T(4,128)(2,1)S(1)}, bf16[4,7168]{1,0:T(4,128)(2,1)S(1)}, u32[]{:S(2)}, u32[]{:S(2)}) collective-permute-start(bf16[4,7168]{1,0:T(4,128)(2,1)S(1)} %get-tuple-element.37), channel_id=1, source_target_pairs={{0,8},{2,10},{4,12},{6,14},{8,16},{10,18},{12,20},{14,22},{16,24},... | collective-permute-start | bytes 172040 | tf_op jit(solution)/shard_map/ppermute | solution.py:30
  175.0 3.7 %collective-permute-done.27 = bf16[4,7168]{1,0:T(4,128)(2,1)S(1)} collective-permute-done((bf16[4,7168]{1,0:T(4,128)(2,1)S(1)}, bf16[4,7168]{1,0:T(4,128)(2,1)S(1)}, u32[]{:S(2)}, u32[]{:S(2)}) %collective-permute-start.27) | collective-permute-done | bytes 57376 | tf_op jit(solution)/shard_map/ppermute | solution.py:30
  178.7 4.1 %collective-permute-done.29 = bf16[4,7168]{1,0:T(4,128)(2,1)S(1)} collective-permute-done((bf16[4,7168]{1,0:T(4,128)(2,1)S(1)}, bf16[4,7168]{1,0:T(4,128)(2,1)S(1)}, u32[]{:S(2)}, u32[]{:S(2)}) %collective-permute-start.29) | collective-permute-done | bytes 57376 | tf_op jit(solution)/shard_map/ppermute | solution.py:30
  (96 shorter events, 30.0 us)
Async XLA Ops:
  56.5 12.1 %collective-permute-start.2 = (bf16[32,7296]{1,0:T(8,128)(2,1)}, bf16[32,7296]{1,0:T(8,128)(2,1)S(1)}, u32[]{:S(2)}, u32[]{:S(2)}) collective-permute-start(bf16[32,7296]{1,0:T(8,128)(2,1)} %get-tuple-element.27), channel_id=1, source_target_pairs={{32,0},{64,32},{96,64},{0,96},{33,1},{65,33},{97,65},{1,97},{34,2}... | collective-permute-start | bytes 1400840 | tf_op jit(solution)/shard_map/ppermute | solution.py:25
  57.2 12.2 %collective-permute-start.3 = (bf16[32,7296]{1,0:T(8,128)(2,1)S(1)}, bf16[32,7296]{1,0:T(8,128)(2,1)S(1)}, u32[]{:S(2)}, u32[]{:S(2)}) collective-permute-start(bf16[32,7296]{1,0:T(8,128)(2,1)S(1)} %get-tuple-element.28), channel_id=1, source_target_pairs={{96,0},{0,32},{32,64},{64,96},{97,1},{1,33},{33,65},{65,97},{98,2}... | collective-permute-start | bytes 1400840 | tf_op jit(solution)/shard_map/ppermute | solution.py:25
  59.7 13.9 %collective-permute-start.8 = (bf16[32,7296]{1,0:T(8,128)(2,1)S(1)}, bf16[32,7296]{1,0:T(8,128)(2,1)}, u32[]{:S(2)}, u32[]{:S(2)}) collective-permute-start(bf16[32,7296]{1,0:T(8,128)(2,1)S(1)} %get-tuple-element.28), channel_id=1, source_target_pairs={{32,0},{64,32},{96,64},{0,96},{33,1},{65,33},{97,65},{1,97},{34,2}... | collective-permute-start | bytes 1400840 | tf_op jit(solution)/shard_map/ppermute | solution.py:25
  59.7 13.9 %collective-permute-start.9 = (bf16[32,7296]{1,0:T(8,128)(2,1)}, bf16[32,7296]{1,0:T(8,128)(2,1)}, u32[]{:S(2)}, u32[]{:S(2)}) collective-permute-start(bf16[32,7296]{1,0:T(8,128)(2,1)} %get-tuple-element.27), channel_id=1, source_target_pairs={{96,0},{0,32},{32,64},{64,96},{97,1},{1,33},{33,65},{65,97},{98,2}... | collective-permute-start | bytes 1400840 | tf_op jit(solution)/shard_map/ppermute | solution.py:25
  73.6 18.7 %collective-permute-start.13 = (bf16[32,7296]{1,0:T(8,128)(2,1)}, bf16[32,7296]{1,0:T(8,128)(2,1)S(1)}, u32[]{:S(2)}, u32[]{:S(2)}) collective-permute-start(bf16[32,7296]{1,0:T(8,128)(2,1)} %collective-permute-done.8.refs_0_), channel_id=1, source_target_pairs={{32,0},{64,32},{96,64},{0,96},{33,1},{65,33},{97,65},{1,97},{34,2}... | collective-permute-start | bytes 1400840 | tf_op jit(solution)/shard_map/ppermute | solution.py:25
  73.7 31.3 %collective-permute-start = (bf16[64,7296]{1,0:T(8,128)(2,1)S(1)}, bf16[64,7296]{1,0:T(8,128)(2,1)}, u32[]{:S(2)}, u32[]{:S(2)}) collective-permute-start(bf16[64,7296]{1,0:T(8,128)(2,1)S(1)} %reshape.23.refs_0_), channel_id=1, source_target_pairs={{0,1},{1,0},{2,3},{3,2},{4,5},{5,4},{6,7},{7,6},{8,9},{9,8},{10,11... | collective-permute-start | bytes 2801672 | tf_op jit(solution)/shard_map/ppermute | solution.py:30
  73.7 19.6 %collective-permute-start.10 = (bf16[32,7296]{1,0:T(8,128)(2,1)}, bf16[32,7296]{1,0:T(8,128)(2,1)}, u32[]{:S(2)}, u32[]{:S(2)}) collective-permute-start(bf16[32,7296]{1,0:T(8,128)(2,1)} %collective-permute-done.8.refs_0_), channel_id=1, source_target_pairs={{0,1},{1,0},{2,3},{3,2},{4,5},{5,4},{6,7},{7,6},{8,9},{9,8},{10,11... | collective-permute-start | bytes 1400840 | tf_op jit(solution)/shard_map/ppermute | solution.py:30
  74.9 18.1 %collective-permute-start.14 = (bf16[32,7296]{1,0:T(8,128)(2,1)}, bf16[32,7296]{1,0:T(8,128)(2,1)}, u32[]{:S(2)}, u32[]{:S(2)}) collective-permute-start(bf16[32,7296]{1,0:T(8,128)(2,1)} %collective-permute-done.9.refs_1_), channel_id=1, source_target_pairs={{96,0},{0,32},{32,64},{64,96},{97,1},{1,33},{33,65},{65,97},{98,2}... | collective-permute-start | bytes 1400840 | tf_op jit(solution)/shard_map/ppermute | solution.py:25
  78.2 15.6 %collective-permute-start.11 = (bf16[32,7296]{1,0:T(8,128)(2,1)}, bf16[32,7296]{1,0:T(8,128)(2,1)}, u32[]{:S(2)}, u32[]{:S(2)}) collective-permute-start(bf16[32,7296]{1,0:T(8,128)(2,1)} %collective-permute-done.9.refs_1_), channel_id=1, source_target_pairs={{0,1},{1,0},{2,3},{3,2},{4,5},{5,4},{6,7},{7,6},{8,9},{9,8},{10,11... | collective-permute-start | bytes 1400840 | tf_op jit(solution)/shard_map/ppermute | solution.py:30
  92.4 21.6 %collective-permute-start.6 = (bf16[64,7168]{1,0:T(8,128)(2,1)}, bf16[64,7168]{1,0:T(8,128)(2,1)}, u32[]{:S(2)}, u32[]{:S(2)}) collective-permute-start(bf16[64,7168]{1,0:T(8,128)(2,1)} %get-tuple-element.16), channel_id=1, source_target_pairs={{0,1},{1,0},{2,3},{3,2},{4,5},{5,4},{6,7},{7,6},{8,9},{9,8},{10,11... | collective-permute-start | bytes 2752520 | tf_op jit(solution)/shard_map/ppermute | solution.py:30
  93.1 16.6 %collective-permute-start.15 = (bf16[32,7296]{1,0:T(8,128)(2,1)S(1)}, bf16[32,7296]{1,0:T(8,128)(2,1)S(1)}, u32[]{:S(2)}, u32[]{:S(2)}) collective-permute-start(bf16[32,7296]{1,0:T(8,128)(2,1)S(1)} %collective-permute-done.13.refs_0_), channel_id=1, source_target_pairs={{0,1},{1,0},{2,3},{3,2},{4,5},{5,4},{6,7},{7,6},{8,9},{9,8},{10,11... | collective-permute-start | bytes 1400840 | tf_op jit(solution)/shard_map/ppermute | solution.py:30
  93.2 16.4 %collective-permute-start.16 = (bf16[32,7296]{1,0:T(8,128)(2,1)}, bf16[32,7296]{1,0:T(8,128)(2,1)S(1)}, u32[]{:S(2)}, u32[]{:S(2)}) collective-permute-start(bf16[32,7296]{1,0:T(8,128)(2,1)} %collective-permute-done.14.refs_1_), channel_id=1, source_target_pairs={{0,1},{1,0},{2,3},{3,2},{4,5},{5,4},{6,7},{7,6},{8,9},{9,8},{10,11... | collective-permute-start | bytes 1400840 | tf_op jit(solution)/shard_map/ppermute | solution.py:30
  104.5 14.7 %collective-permute-start.12 = (bf16[64,7168]{1,0:T(8,128)(2,1)S(1)}, bf16[64,7168]{1,0:T(8,128)(2,1)S(1)}, u32[]{:S(2)}, u32[]{:S(2)}) collective-permute-start(bf16[64,7168]{1,0:T(8,128)(2,1)S(1)} %get-tuple-element.18), channel_id=1, source_target_pairs={{0,1},{1,0},{2,3},{3,2},{4,5},{5,4},{6,7},{7,6},{8,9},{9,8},{10,11... | collective-permute-start | bytes 2752520 | tf_op jit(solution)/shard_map/ppermute | solution.py:30
  109.2 32.6 %collective-permute-start.1 = (bf16[64,7168]{1,0:T(8,128)(2,1)S(1)}, bf16[64,7168]{1,0:T(8,128)(2,1)S(1)}, u32[]{:S(2)}, u32[]{:S(2)}) collective-permute-start(bf16[64,7168]{1,0:T(8,128)(2,1)S(1)} %get-tuple-element.14), channel_id=1, source_target_pairs={{0,1},{1,0},{2,3},{3,2},{4,5},{5,4},{6,7},{7,6},{8,9},{9,8},{10,11... | collective-permute-start | bytes 2752520 | tf_op jit(solution)/shard_map/ppermute | solution.py:30
  115.4 26.5 %collective-permute-start.20 = (bf16[32,7168]{1,0:T(8,128)(2,1)S(1)}, bf16[32,7168]{1,0:T(8,128)(2,1)S(1)}, u32[]{:S(2)}, u32[]{:S(2)}) collective-permute-start(bf16[32,7168]{1,0:T(8,128)(2,1)S(1)} %get-tuple-element.34), channel_id=1, source_target_pairs={{0,32},{32,64},{64,96},{96,0},{1,33},{33,65},{65,97},{97,1},{2,34}... | collective-permute-start | bytes 1376264 | tf_op jit(solution)/shard_map/ppermute | solution.py:30
  115.5 26.4 %collective-permute-start.7 = (bf16[32,7168]{1,0:T(8,128)(2,1)S(1)}, bf16[32,7168]{1,0:T(8,128)(2,1)S(1)}, u32[]{:S(2)}, u32[]{:S(2)}) collective-permute-start(bf16[32,7168]{1,0:T(8,128)(2,1)S(1)} %get-tuple-element.33), channel_id=1, source_target_pairs={{0,96},{32,0},{64,32},{96,64},{1,97},{33,1},{65,33},{97,65},{2,98}... | collective-permute-start | bytes 1376264 | tf_op jit(solution)/shard_map/ppermute | solution.py:30
  117.8 20.3 %collective-permute-start.18 = (bf16[32,7168]{1,0:T(8,128)(2,1)S(1)}, bf16[32,7168]{1,0:T(8,128)(2,1)S(1)}, u32[]{:S(2)}, u32[]{:S(2)}) collective-permute-start(bf16[32,7168]{1,0:T(8,128)(2,1)S(1)} %get-tuple-element.35), channel_id=1, source_target_pairs={{0,32},{32,64},{64,96},{96,0},{1,33},{33,65},{65,97},{97,1},{2,34}... | collective-permute-start | bytes 1376264 | tf_op jit(solution)/shard_map/ppermute | solution.py:30
  119.3 20.2 %collective-permute-start.21 = (bf16[32,7168]{1,0:T(8,128)(2,1)S(1)}, bf16[32,7168]{1,0:T(8,128)(2,1)S(1)}, u32[]{:S(2)}, u32[]{:S(2)}) collective-permute-start(bf16[32,7168]{1,0:T(8,128)(2,1)S(1)} %get-tuple-element.36), channel_id=1, source_target_pairs={{0,96},{32,0},{64,32},{96,64},{1,97},{33,1},{65,33},{97,65},{2,98}... | collective-permute-start | bytes 1376264 | tf_op jit(solution)/shard_map/ppermute | solution.py:30
  139.6 12.0 %collective-permute-start.19 = (bf16[32,7168]{1,0:T(8,128)(2,1)S(1)}, bf16[32,7168]{1,0:T(8,128)(2,1)S(1)}, u32[]{:S(2)}, u32[]{:S(2)}) collective-permute-start(bf16[32,7168]{1,0:T(8,128)(2,1)S(1)} %get-tuple-element.25), channel_id=1, source_target_pairs={{0,32},{32,64},{64,96},{96,0},{1,33},{33,65},{65,97},{97,1},{2,34}... | collective-permute-start | bytes 1376264 | tf_op jit(solution)/shard_map/ppermute | solution.py:30
  139.9 13.1 %collective-permute-start.22 = (bf16[32,7168]{1,0:T(8,128)(2,1)S(1)}, bf16[32,7168]{1,0:T(8,128)(2,1)S(1)}, u32[]{:S(2)}, u32[]{:S(2)}) collective-permute-start(bf16[32,7168]{1,0:T(8,128)(2,1)S(1)} %get-tuple-element.26), channel_id=1, source_target_pairs={{0,96},{32,0},{64,32},{96,64},{1,97},{33,1},{65,33},{97,65},{2,98}... | collective-permute-start | bytes 1376264 | tf_op jit(solution)/shard_map/ppermute | solution.py:30
  153.7 10.8 %collective-permute-start.23 = (bf16[16,7168]{1,0:T(8,128)(2,1)S(1)}, bf16[16,7168]{1,0:T(8,128)(2,1)S(1)}, u32[]{:S(2)}, u32[]{:S(2)}) collective-permute-start(bf16[16,7168]{1,0:T(8,128)(2,1)S(1)} %get-tuple-element.31), channel_id=1, source_target_pairs={{0,2},{2,4},{4,6},{6,8},{8,10},{10,12},{12,14},{14,16},{16,18},{18... | collective-permute-start | bytes 688136 | tf_op jit(solution)/shard_map/ppermute | solution.py:30
  153.9 10.7 %collective-permute-start.24 = (bf16[16,7168]{1,0:T(8,128)(2,1)S(1)}, bf16[16,7168]{1,0:T(8,128)(2,1)S(1)}, u32[]{:S(2)}, u32[]{:S(2)}) collective-permute-start(bf16[16,7168]{1,0:T(8,128)(2,1)S(1)} %get-tuple-element.32), channel_id=1, source_target_pairs={{0,30},{2,0},{4,2},{6,4},{8,6},{10,8},{12,10},{14,12},{16,14},{18,... | collective-permute-start | bytes 688136 | tf_op jit(solution)/shard_map/ppermute | solution.py:30
  165.5 13.1 %collective-permute-start.27 = (bf16[4,7168]{1,0:T(4,128)(2,1)S(1)}, bf16[4,7168]{1,0:T(4,128)(2,1)S(1)}, u32[]{:S(2)}, u32[]{:S(2)}) collective-permute-start(bf16[4,7168]{1,0:T(4,128)(2,1)S(1)} %slice.146), channel_id=1, source_target_pairs={{0,16},{2,18},{4,20},{6,22},{8,24},{10,26},{12,28},{14,30},{16,0},... | collective-permute-start | bytes 172040 | tf_op jit(solution)/shard_map/ppermute | solution.py:30
  168.9 9.7 %collective-permute-start.28 = (bf16[4,7168]{1,0:T(4,128)(2,1)S(1)}, bf16[4,7168]{1,0:T(4,128)(2,1)S(1)}, u32[]{:S(2)}, u32[]{:S(2)}) collective-permute-start(bf16[4,7168]{1,0:T(4,128)(2,1)S(1)} %get-tuple-element.37), channel_id=1, source_target_pairs={{0,8},{2,10},{4,12},{6,14},{8,16},{10,18},{12,20},{14,22},{16,24},... | collective-permute-start | bytes 172040 | tf_op jit(solution)/shard_map/ppermute | solution.py:30
  (20 other events, 72.4 us)

commit v5 on v4

--- a/solution.py
+++ b/solution.py
@@ -133,23 +133,22 @@
     )(pltpu.with_memory_space_constraint(value, pltpu.VMEM))
 
 
-def near_sum(kept, pieces):
-    got = []
-    for piece, k in zip(pieces, (1, -1, 2, -2)):
-        got.append(give_to(piece, "ep_1", k))
-    total = kept + got[0].astype(HIGH) + got[1].astype(HIGH)
-    half = got[2].shape[-2]
-    top = total[..., :half, :] + got[2].astype(HIGH) + got[3].astype(HIGH)
-    return jnp.concatenate([top, total[..., half:, :]], axis=-2)
-
-
-def far_sum(rows):
-    count = rows.shape[-2] // 4
-    total = rows[..., :count, :]
-    for i, k in enumerate(FAR):
-        piece = rows[..., (i + 1) * count : (i + 2) * count, :]
-        total = total + give_to(piece.astype(LOW), "ep_1", k).astype(HIGH)
-    return total
+def sum_along_z(rows):
+    def received(piece, offset):
+        return give_to(piece.astype(LOW), "ep_1", offset).astype(HIGH)
+
+    n = rows.shape[0] // 16
+    plus = received(rows[4 * n : 8 * n], 1)
+    minus = received(rows[8 * n : 12 * n], -1)
+    plus_two = received(rows[12 * n : 14 * n], 2)
+    minus_two = received(rows[14 * n :], -2)
+    near = rows[: 4 * n] + plus + minus
+    pieces = near[2 * n : 3 * n].astype(LOW), near[3 * n :].astype(LOW), near[: 2 * n]
+    low_b, low_c, top = lax.optimization_barrier(pieces)
+    total = received(low_b, FAR[1]) + received(low_c, FAR[2])
+    top = copied(top)
+    top = top + plus_two + minus_two
+    return top[:n] + received(top[n:], FAR[0]) + total
 
 
 def layer(tokens, routes, gates, gate_weight, up_weight, down_weight):
@@ -190,9 +189,7 @@
     bottom = near_total[half:] + below_b.astype(HIGH) + above_a.astype(HIGH)
     total = jnp.concatenate([top, bottom], axis=0).astype(LOW)
     total = jnp.dot(order, total, preferred_element_type=HIGH)
-    n = total.shape[0] // 8
-    cut = [total[i * n : j * n].astype(LOW) for i, j in ((2, 4), (4, 6), (6, 7), (7, 8))]
-    return far_sum(near_sum(total[: 2 * n], cut)).astype(LOW)
+    return sum_along_z(total).astype(LOW)
 
 
 def solution(mesh):
@@ -207,6 +204,4 @@
         P(None, EP),
         P(EP, None),
     )
-    return jax.shard_map(
-        layer, mesh=torus, in_specs=placed, out_specs=P(GROUPS_EP, None), check_vma=False
-    )
+    return jax.shard_map(layer, mesh=torus, in_specs=placed, out_specs=P(GROUPS_EP, None), check_vma=False)

time: 184 us -> 184 us (level)
  no operation moved by 1% of the time
where the time goes in v5:
time: 184 us; the launch traced here: 183 us
  blocking collectives  53.7 us (29%)
  waiting for transfers between devices  50.9 us (28%)
  starting transfers between devices  36.3 us (20%)
  local copies, waits for them, and re-layouts  19.1 us (10%)
  Pallas kernels  17.8 us (10%)
  other arithmetic  4.94 us (3%)
    all_gather x1, blocking collectives, layer(): lax.all_gather(own, 'ep_1', axis=0, tiled=True)  53.7 us
    ppermute x24, waiting for transfers between devices, give_to(): lax.ppermute(value, axis, [(i, (i + offset) % count) for i in range(count)])  42.3 us
    ppermute x24, starting transfers between devices, give_to(): lax.ppermute(value, axis, [(i, (i + offset) % count) for i in range(count)])  26.6 us
    unnamed x29, local copies, waits for them, and re-layouts  17.9 us
    pallas_call x4, Pallas kernels, expert_of(): pl.pallas_call(functools.partial(expert_kernel, len(blocks)), in_specs=[p...  17.8 us
    ppermute x6, starting transfers between devices, take_from(): lax.ppermute(value, axis, [((i + offset) % count, i) for i in range(count)])  9.71 us
    ppermute x6, waiting for transfers between devices, take_from(): lax.ppermute(value, axis, [((i + offset) % count, i) for i in range(count)])  8.61 us
  transfers between devices with their start and end apart: 30, of which 10 were waited for; matrix products, arithmetic and copies ran while one was open for 1% of the time, Pallas kernels for 10%

profile of v5, /device:TPU:38, one launch (start us, length us, event | category | flops | bytes accessed | tf_op | source)
XLA Modules:
  0.0 183.4 jit_solution(9372706275703519327)
XLA Ops:
  1.7 53.7 %all-gather = bf16[16,4,7296]{2,1,0:T(4,128)(2,1)S(1)} all-gather(bf16[1,4,7296]{2,1,0:T(4,128)(2,1)S(1)} %maximum_bitcast_fusion), channel_id=1, replica_groups=mesh['groups'=2,'ep_0'=4,'ep_1'=16,'ep_2'=2] {'ep_1'}, dimensions={0}, use_global_device_ids=true | all-gather | bytes 992256 | tf_op jit(solution)/shard_map/all_gather | solution.py:169
  57.2 2.5 %collective-permute-start.3 = (bf16[32,7296]{1,0:T(8,128)(2,1)S(1)}, bf16[32,7296]{1,0:T(8,128)(2,1)S(1)}, u32[]{:S(2)}, u32[]{:S(2)}) collective-permute-start(bf16[32,7296]{1,0:T(8,128)(2,1)S(1)} %get-tuple-element.34), channel_id=1, source_target_pairs={{96,0},{0,32},{32,64},{64,96},{97,1},{1,33},{33,65},{65,97},{98,2}... | collective-permute-start | bytes 1400840 | tf_op jit(solution)/shard_map/ppermute | solution.py:25
  59.7 3.2 %collective-permute-start.9 = (bf16[32,7296]{1,0:T(8,128)(2,1)}, bf16[32,7296]{1,0:T(8,128)(2,1)}, u32[]{:S(2)}, u32[]{:S(2)}) collective-permute-start(bf16[32,7296]{1,0:T(8,128)(2,1)} %get-tuple-element.33), channel_id=1, source_target_pairs={{96,0},{0,32},{32,64},{64,96},{97,1},{1,33},{33,65},{65,97},{98,2}... | collective-permute-start | bytes 1400840 | tf_op jit(solution)/shard_map/ppermute | solution.py:25
  62.9 5.6 %collective-permute-done.2.refs_0_ = bf16[32,7296]{1,0:T(8,128)(2,1)S(1)} collective-permute-done((bf16[32,7296]{1,0:T(8,128)(2,1)}, bf16[32,7296]{1,0:T(8,128)(2,1)S(1)}, u32[]{:S(2)}, u32[]{:S(2)}) %collective-permute-start.2) | collective-permute-done | bytes 466976 | tf_op jit(solution)/shard_map/ppermute | solution.py:25
  70.6 3.0 %collective-permute-done.8.refs_0_ = bf16[32,7296]{1,0:T(8,128)(2,1)} collective-permute-done((bf16[32,7296]{1,0:T(8,128)(2,1)S(1)}, bf16[32,7296]{1,0:T(8,128)(2,1)}, u32[]{:S(2)}, u32[]{:S(2)}) %collective-permute-start.8) | collective-permute-done | bytes 466976 | tf_op jit(solution)/shard_map/ppermute | solution.py:25
  74.9 3.2 %collective-permute-start.14 = (bf16[32,7296]{1,0:T(8,128)(2,1)}, bf16[32,7296]{1,0:T(8,128)(2,1)}, u32[]{:S(2)}, u32[]{:S(2)}) collective-permute-start(bf16[32,7296]{1,0:T(8,128)(2,1)} %collective-permute-done.9.refs_1_), channel_id=1, source_target_pairs={{96,0},{0,32},{32,64},{64,96},{97,1},{1,33},{33,65},{65,97},{98,2}... | collective-permute-start | bytes 1400840 | tf_op jit(solution)/shard_map/ppermute | solution.py:25
  78.2 2.0 %copy-done = bf16[7168,256]{1,0:T(8,128)(2,1)S(1)} copy-done((bf16[7168,256]{1,0:T(8,128)(2,1)S(1)}, bf16[7168,256]{1,0:T(8,128)(2,1)}, u32[]{:S(2)}) %copy-start) | copy-done | bytes 3670040
  80.2 2.0 %copy-done.3 = bf16[7168,256]{1,0:T(8,128)(2,1)S(1)} copy-done((bf16[7168,256]{1,0:T(8,128)(2,1)S(1)}, bf16[7168,256]{1,0:T(8,128)(2,1)}, u32[]{:S(2)}) %copy-start.3) | copy-done | bytes 3670040
  82.3 2.0 %copy-done.5 = bf16[256,7168]{1,0:T(8,128)(2,1)S(1)} copy-done((bf16[256,7168]{1,0:T(8,128)(2,1)S(1)}, bf16[256,7168]{1,0:T(8,128)(2,1)}, u32[]{:S(2)}) %copy-start.5) | copy-done | bytes 3670040
  87.4 5.0 %expert.5 = (f32[64,7168]{1,0:T(8,128)S(1)}, bf16[64,7168]{1,0:T(8,128)(2,1)}) custom-call(s32[1]{0:T(128)} %bitcast.expert_ref, bf16[32,7296]{1,0:T(8,128)(2,1)S(1)} %copy-done.8, bf16[32,7296]{1,0:T(8,128)(2,1)S(1)} %copy-done.10, bf16[32,7296]{1,0:T(8,128)(2,1)S(1)} %copy-done.12, bf16[32,7296]{1,0:T(8,128)(2,1)} %collective-permute-done.5.refs_3_, ...), custom_call_target="tpu_custom_call" | custom-call | flops 1409286144 | bytes 16515072 | tf_op jit(solution)/shard_map/expert/pallas_call | solution.py:100
  95.9 2.0 %copy-done.4 = bf16[7168,256]{1,0:T(8,128)(2,1)S(1)} copy-done((bf16[7168,256]{1,0:T(8,128)(2,1)S(1)}, bf16[7168,256]{1,0:T(8,128)(2,1)}, u32[]{:S(2)}) %copy-start.4) | copy-done | bytes 3670040
  97.9 2.0 %copy-done.6 = bf16[256,7168]{1,0:T(8,128)(2,1)S(1)} copy-done((bf16[256,7168]{1,0:T(8,128)(2,1)S(1)}, bf16[256,7168]{1,0:T(8,128)(2,1)}, u32[]{:S(2)}) %copy-start.6) | copy-done | bytes 3670040
  99.9 4.6 %expert.6 = (f32[64,7168]{1,0:T(8,128)S(1)}, bf16[64,7168]{1,0:T(8,128)(2,1)S(1)}) custom-call(s32[1]{0:T(128)} %bitcast.expert_ref, bf16[32,7296]{1,0:T(8,128)(2,1)} %collective-permute-done.8.refs_0_, bf16[32,7296]{1,0:T(8,128)(2,1)} %collective-permute-done.9.refs_1_, bf16[32,7296]{1,0:T(8,128)(2,1)} %collective-permute-done.10.refs_2_, ...), custom_call_target="tpu_custom_call" | custom-call | flops 1409286144 | bytes 16515072 | tf_op jit(solution)/shard_map/expert/pallas_call | solution.py:100
  105.0 4.2 %expert.4 = (f32[64,7168]{1,0:T(8,128)S(1)}, bf16[64,7168]{1,0:T(8,128)(2,1)S(1)}) custom-call(s32[1]{0:T(128)} %bitcast.expert_ref, bf16[64,7296]{1,0:T(8,128)(2,1)S(1)} %reshape.23.refs_0_, bf16[64,7296]{1,0:T(8,128)(2,1)} %collective-permute-done.refs_1_, bf16[7168,256]{1,0:T(8,128)(2,1)S(1)} %copy-done.2, bf16[7168,256]{1,0:T(8,128)(2,1)S(1)} %copy-done.4, ...), custom_call_target="tpu_custom_call" | custom-call | flops 1409286144 | bytes 16515072 | tf_op jit(solution)/shard_map/expert/pallas_call | solution.py:100
  109.7 4.0 %expert.7 = (f32[64,7168]{1,0:T(8,128)S(1)}, bf16[64,7168]{1,0:T(8,128)(2,1)S(1)}) custom-call(s32[1]{0:T(128)} %bitcast.expert_ref, bf16[32,7296]{1,0:T(8,128)(2,1)S(1)} %collective-permute-done.13.refs_0_, bf16[32,7296]{1,0:T(8,128)(2,1)} %collective-permute-done.14.refs_1_, bf16[32,7296]{1,0:T(8,128)(2,1)S(1)} %collective-permute-done.15.refs_2_, ...), custom_call_target="tpu_custom_call" | custom-call | flops 1409286144 | bytes 16515072 | tf_op jit(solution)/shard_map/expert/pallas_call | solution.py:100
  120.1 18.0 %collective-permute-done.18 = bf16[32,7168]{1,0:T(8,128)(2,1)S(1)} collective-permute-done((bf16[32,7168]{1,0:T(8,128)(2,1)S(1)}, bf16[32,7168]{1,0:T(8,128)(2,1)S(1)}, u32[]{:S(2)}, u32[]{:S(2)}) %collective-permute-start.18) | collective-permute-done | bytes 458784 | tf_op jit(solution)/shard_map/ppermute | solution.py:30
  141.9 9.7 %collective-permute-done.19 = bf16[32,7168]{1,0:T(8,128)(2,1)S(1)} collective-permute-done((bf16[32,7168]{1,0:T(8,128)(2,1)S(1)}, bf16[32,7168]{1,0:T(8,128)(2,1)S(1)}, u32[]{:S(2)}, u32[]{:S(2)}) %collective-permute-start.19) | collective-permute-done | bytes 458784 | tf_op jit(solution)/shard_map/ppermute | solution.py:30
  153.9 3.2 %collective-permute-start.24 = (bf16[16,7168]{1,0:T(8,128)(2,1)S(1)}, bf16[16,7168]{1,0:T(8,128)(2,1)S(1)}, u32[]{:S(2)}, u32[]{:S(2)}) collective-permute-start(bf16[16,7168]{1,0:T(8,128)(2,1)S(1)} %get-tuple-element.38), channel_id=1, source_target_pairs={{0,30},{2,0},{4,2},{6,4},{8,6},{10,8},{12,10},{14,12},{16,14},{18,... | collective-permute-start | bytes 688136 | tf_op jit(solution)/shard_map/ppermute | solution.py:30
  157.3 4.1 %collective-permute-start.26 = (bf16[8,7168]{1,0:T(8,128)(2,1)S(1)}, bf16[8,7168]{1,0:T(8,128)(2,1)S(1)}, u32[]{:S(2)}, u32[]{:S(2)}) collective-permute-start(bf16[8,7168]{1,0:T(8,128)(2,1)S(1)} %get-tuple-element.36), channel_id=1, source_target_pairs={{0,28},{2,30},{4,0},{6,2},{8,4},{10,6},{12,8},{14,10},{16,12},{18,... | collective-permute-start | bytes 344072 | tf_op jit(solution)/shard_map/ppermute | solution.py:30
  161.4 3.2 %collective-permute-done.23 = bf16[16,7168]{1,0:T(8,128)(2,1)S(1)} collective-permute-done((bf16[16,7168]{1,0:T(8,128)(2,1)S(1)}, bf16[16,7168]{1,0:T(8,128)(2,1)S(1)}, u32[]{:S(2)}, u32[]{:S(2)}) %collective-permute-start.23) | collective-permute-done | bytes 229408 | tf_op jit(solution)/shard_map/ppermute | solution.py:30
  165.6 3.3 %collective-permute-start.27 = (bf16[4,7168]{1,0:T(4,128)(2,1)S(1)}, bf16[4,7168]{1,0:T(4,128)(2,1)S(1)}, u32[]{:S(2)}, u32[]{:S(2)}) collective-permute-start(bf16[4,7168]{1,0:T(4,128)(2,1)S(1)} %slice.138), channel_id=1, source_target_pairs={{0,16},{2,18},{4,20},{6,22},{8,24},{10,26},{12,28},{14,30},{16,0},... | collective-permute-start | bytes 172040 | tf_op jit(solution)/shard_map/ppermute | solution.py:30
  168.9 4.4 %collective-permute-start.28 = (bf16[4,7168]{1,0:T(4,128)(2,1)S(1)}, bf16[4,7168]{1,0:T(4,128)(2,1)S(1)}, u32[]{:S(2)}, u32[]{:S(2)}) collective-permute-start(bf16[4,7168]{1,0:T(4,128)(2,1)S(1)} %get-tuple-element.25), channel_id=1, source_target_pairs={{0,8},{2,10},{4,12},{6,14},{8,16},{10,18},{12,20},{14,22},{16,24},... | collective-permute-start | bytes 172040 | tf_op jit(solution)/shard_map/ppermute | solution.py:30
  174.8 3.8 %collective-permute-done.27 = bf16[4,7168]{1,0:T(4,128)(2,1)S(1)} collective-permute-done((bf16[4,7168]{1,0:T(4,128)(2,1)S(1)}, bf16[4,7168]{1,0:T(4,128)(2,1)S(1)}, u32[]{:S(2)}, u32[]{:S(2)}) %collective-permute-start.27) | collective-permute-done | bytes 57376 | tf_op jit(solution)/shard_map/ppermute | solution.py:30
  178.7 4.0 %collective-permute-done.29 = bf16[4,7168]{1,0:T(4,128)(2,1)S(1)} collective-permute-done((bf16[4,7168]{1,0:T(4,128)(2,1)S(1)}, bf16[4,7168]{1,0:T(4,128)(2,1)S(1)}, u32[]{:S(2)}, u32[]{:S(2)}) %collective-permute-start.29) | collective-permute-done | bytes 57376 | tf_op jit(solution)/shard_map/ppermute | solution.py:30
  (98 shorter events, 29.9 us)
Async XLA Ops:
  56.5 12.1 %collective-permute-start.2 = (bf16[32,7296]{1,0:T(8,128)(2,1)}, bf16[32,7296]{1,0:T(8,128)(2,1)S(1)}, u32[]{:S(2)}, u32[]{:S(2)}) collective-permute-start(bf16[32,7296]{1,0:T(8,128)(2,1)} %get-tuple-element.33), channel_id=1, source_target_pairs={{32,0},{64,32},{96,64},{0,96},{33,1},{65,33},{97,65},{1,97},{34,2}... | collective-permute-start | bytes 1400840 | tf_op jit(solution)/shard_map/ppermute | solution.py:25
  57.2 12.2 %collective-permute-start.3 = (bf16[32,7296]{1,0:T(8,128)(2,1)S(1)}, bf16[32,7296]{1,0:T(8,128)(2,1)S(1)}, u32[]{:S(2)}, u32[]{:S(2)}) collective-permute-start(bf16[32,7296]{1,0:T(8,128)(2,1)S(1)} %get-tuple-element.34), channel_id=1, source_target_pairs={{96,0},{0,32},{32,64},{64,96},{97,1},{1,33},{33,65},{65,97},{98,2}... | collective-permute-start | bytes 1400840 | tf_op jit(solution)/shard_map/ppermute | solution.py:25
  59.7 13.9 %collective-permute-start.8 = (bf16[32,7296]{1,0:T(8,128)(2,1)S(1)}, bf16[32,7296]{1,0:T(8,128)(2,1)}, u32[]{:S(2)}, u32[]{:S(2)}) collective-permute-start(bf16[32,7296]{1,0:T(8,128)(2,1)S(1)} %get-tuple-element.34), channel_id=1, source_target_pairs={{32,0},{64,32},{96,64},{0,96},{33,1},{65,33},{97,65},{1,97},{34,2}... | collective-permute-start | bytes 1400840 | tf_op jit(solution)/shard_map/ppermute | solution.py:25
  59.7 13.9 %collective-permute-start.9 = (bf16[32,7296]{1,0:T(8,128)(2,1)}, bf16[32,7296]{1,0:T(8,128)(2,1)}, u32[]{:S(2)}, u32[]{:S(2)}) collective-permute-start(bf16[32,7296]{1,0:T(8,128)(2,1)} %get-tuple-element.33), channel_id=1, source_target_pairs={{96,0},{0,32},{32,64},{64,96},{97,1},{1,33},{33,65},{65,97},{98,2}... | collective-permute-start | bytes 1400840 | tf_op jit(solution)/shard_map/ppermute | solution.py:25
  73.6 18.7 %collective-permute-start.13 = (bf16[32,7296]{1,0:T(8,128)(2,1)}, bf16[32,7296]{1,0:T(8,128)(2,1)S(1)}, u32[]{:S(2)}, u32[]{:S(2)}) collective-permute-start(bf16[32,7296]{1,0:T(8,128)(2,1)} %collective-permute-done.8.refs_0_), channel_id=1, source_target_pairs={{32,0},{64,32},{96,64},{0,96},{33,1},{65,33},{97,65},{1,97},{34,2}... | collective-permute-start | bytes 1400840 | tf_op jit(solution)/shard_map/ppermute | solution.py:25
  73.7 31.3 %collective-permute-start = (bf16[64,7296]{1,0:T(8,128)(2,1)S(1)}, bf16[64,7296]{1,0:T(8,128)(2,1)}, u32[]{:S(2)}, u32[]{:S(2)}) collective-permute-start(bf16[64,7296]{1,0:T(8,128)(2,1)S(1)} %reshape.23.refs_0_), channel_id=1, source_target_pairs={{0,1},{1,0},{2,3},{3,2},{4,5},{5,4},{6,7},{7,6},{8,9},{9,8},{10,11... | collective-permute-start | bytes 2801672 | tf_op jit(solution)/shard_map/ppermute | solution.py:30
  73.7 19.6 %collective-permute-start.10 = (bf16[32,7296]{1,0:T(8,128)(2,1)}, bf16[32,7296]{1,0:T(8,128)(2,1)}, u32[]{:S(2)}, u32[]{:S(2)}) collective-permute-start(bf16[32,7296]{1,0:T(8,128)(2,1)} %collective-permute-done.8.refs_0_), channel_id=1, source_target_pairs={{0,1},{1,0},{2,3},{3,2},{4,5},{5,4},{6,7},{7,6},{8,9},{9,8},{10,11... | collective-permute-start | bytes 1400840 | tf_op jit(solution)/shard_map/ppermute | solution.py:30
  74.9 18.1 %collective-permute-start.14 = (bf16[32,7296]{1,0:T(8,128)(2,1)}, bf16[32,7296]{1,0:T(8,128)(2,1)}, u32[]{:S(2)}, u32[]{:S(2)}) collective-permute-start(bf16[32,7296]{1,0:T(8,128)(2,1)} %collective-permute-done.9.refs_1_), channel_id=1, source_target_pairs={{96,0},{0,32},{32,64},{64,96},{97,1},{1,33},{33,65},{65,97},{98,2}... | collective-permute-start | bytes 1400840 | tf_op jit(solution)/shard_map/ppermute | solution.py:25
  78.2 15.6 %collective-permute-start.11 = (bf16[32,7296]{1,0:T(8,128)(2,1)}, bf16[32,7296]{1,0:T(8,128)(2,1)}, u32[]{:S(2)}, u32[]{:S(2)}) collective-permute-start(bf16[32,7296]{1,0:T(8,128)(2,1)} %collective-permute-done.9.refs_1_), channel_id=1, source_target_pairs={{0,1},{1,0},{2,3},{3,2},{4,5},{5,4},{6,7},{7,6},{8,9},{9,8},{10,11... | collective-permute-start | bytes 1400840 | tf_op jit(solution)/shard_map/ppermute | solution.py:30
  92.4 21.6 %collective-permute-start.6 = (bf16[64,7168]{1,0:T(8,128)(2,1)}, bf16[64,7168]{1,0:T(8,128)(2,1)}, u32[]{:S(2)}, u32[]{:S(2)}) collective-permute-start(bf16[64,7168]{1,0:T(8,128)(2,1)} %get-tuple-element.19), channel_id=1, source_target_pairs={{0,1},{1,0},{2,3},{3,2},{4,5},{5,4},{6,7},{7,6},{8,9},{9,8},{10,11... | collective-permute-start | bytes 2752520 | tf_op jit(solution)/shard_map/ppermute | solution.py:30
  93.1 16.6 %collective-permute-start.15 = (bf16[32,7296]{1,0:T(8,128)(2,1)S(1)}, bf16[32,7296]{1,0:T(8,128)(2,1)S(1)}, u32[]{:S(2)}, u32[]{:S(2)}) collective-permute-start(bf16[32,7296]{1,0:T(8,128)(2,1)S(1)} %collective-permute-done.13.refs_0_), channel_id=1, source_target_pairs={{0,1},{1,0},{2,3},{3,2},{4,5},{5,4},{6,7},{7,6},{8,9},{9,8},{10,11... | collective-permute-start | bytes 1400840 | tf_op jit(solution)/shard_map/ppermute | solution.py:30
  93.2 16.4 %collective-permute-start.16 = (bf16[32,7296]{1,0:T(8,128)(2,1)}, bf16[32,7296]{1,0:T(8,128)(2,1)S(1)}, u32[]{:S(2)}, u32[]{:S(2)}) collective-permute-start(bf16[32,7296]{1,0:T(8,128)(2,1)} %collective-permute-done.14.refs_1_), channel_id=1, source_target_pairs={{0,1},{1,0},{2,3},{3,2},{4,5},{5,4},{6,7},{7,6},{8,9},{9,8},{10,11... | collective-permute-start | bytes 1400840 | tf_op jit(solution)/shard_map/ppermute | solution.py:30
  104.5 14.7 %collective-permute-start.12 = (bf16[64,7168]{1,0:T(8,128)(2,1)S(1)}, bf16[64,7168]{1,0:T(8,128)(2,1)S(1)}, u32[]{:S(2)}, u32[]{:S(2)}) collective-permute-start(bf16[64,7168]{1,0:T(8,128)(2,1)S(1)} %get-tuple-element.21), channel_id=1, source_target_pairs={{0,1},{1,0},{2,3},{3,2},{4,5},{5,4},{6,7},{7,6},{8,9},{9,8},{10,11... | collective-permute-start | bytes 2752520 | tf_op jit(solution)/shard_map/ppermute | solution.py:30
  109.2 32.6 %collective-permute-start.1 = (bf16[64,7168]{1,0:T(8,128)(2,1)S(1)}, bf16[64,7168]{1,0:T(8,128)(2,1)S(1)}, u32[]{:S(2)}, u32[]{:S(2)}) collective-permute-start(bf16[64,7168]{1,0:T(8,128)(2,1)S(1)} %get-tuple-element.17), channel_id=1, source_target_pairs={{0,1},{1,0},{2,3},{3,2},{4,5},{5,4},{6,7},{7,6},{8,9},{9,8},{10,11... | collective-permute-start | bytes 2752520 | tf_op jit(solution)/shard_map/ppermute | solution.py:30
  115.4 26.5 %collective-permute-start.20 = (bf16[32,7168]{1,0:T(8,128)(2,1)S(1)}, bf16[32,7168]{1,0:T(8,128)(2,1)S(1)}, u32[]{:S(2)}, u32[]{:S(2)}) collective-permute-start(bf16[32,7168]{1,0:T(8,128)(2,1)S(1)} %get-tuple-element.40), channel_id=1, source_target_pairs={{0,32},{32,64},{64,96},{96,0},{1,33},{33,65},{65,97},{97,1},{2,34}... | collective-permute-start | bytes 1376264 | tf_op jit(solution)/shard_map/ppermute | solution.py:30
  115.5 26.4 %collective-permute-start.7 = (bf16[32,7168]{1,0:T(8,128)(2,1)S(1)}, bf16[32,7168]{1,0:T(8,128)(2,1)S(1)}, u32[]{:S(2)}, u32[]{:S(2)}) collective-permute-start(bf16[32,7168]{1,0:T(8,128)(2,1)S(1)} %get-tuple-element.39), channel_id=1, source_target_pairs={{0,96},{32,0},{64,32},{96,64},{1,97},{33,1},{65,33},{97,65},{2,98}... | collective-permute-start | bytes 1376264 | tf_op jit(solution)/shard_map/ppermute | solution.py:30
  117.8 20.3 %collective-permute-start.18 = (bf16[32,7168]{1,0:T(8,128)(2,1)S(1)}, bf16[32,7168]{1,0:T(8,128)(2,1)S(1)}, u32[]{:S(2)}, u32[]{:S(2)}) collective-permute-start(bf16[32,7168]{1,0:T(8,128)(2,1)S(1)} %get-tuple-element.41), channel_id=1, source_target_pairs={{0,32},{32,64},{64,96},{96,0},{1,33},{33,65},{65,97},{97,1},{2,34}... | collective-permute-start | bytes 1376264 | tf_op jit(solution)/shard_map/ppermute | solution.py:30
  119.3 20.2 %collective-permute-start.21 = (bf16[32,7168]{1,0:T(8,128)(2,1)S(1)}, bf16[32,7168]{1,0:T(8,128)(2,1)S(1)}, u32[]{:S(2)}, u32[]{:S(2)}) collective-permute-start(bf16[32,7168]{1,0:T(8,128)(2,1)S(1)} %get-tuple-element.42), channel_id=1, source_target_pairs={{0,96},{32,0},{64,32},{96,64},{1,97},{33,1},{65,33},{97,65},{2,98}... | collective-permute-start | bytes 1376264 | tf_op jit(solution)/shard_map/ppermute | solution.py:30
  139.6 12.0 %collective-permute-start.19 = (bf16[32,7168]{1,0:T(8,128)(2,1)S(1)}, bf16[32,7168]{1,0:T(8,128)(2,1)S(1)}, u32[]{:S(2)}, u32[]{:S(2)}) collective-permute-start(bf16[32,7168]{1,0:T(8,128)(2,1)S(1)} %get-tuple-element.31), channel_id=1, source_target_pairs={{0,32},{32,64},{64,96},{96,0},{1,33},{33,65},{65,97},{97,1},{2,34}... | collective-permute-start | bytes 1376264 | tf_op jit(solution)/shard_map/ppermute | solution.py:30
  139.9 13.1 %collective-permute-start.22 = (bf16[32,7168]{1,0:T(8,128)(2,1)S(1)}, bf16[32,7168]{1,0:T(8,128)(2,1)S(1)}, u32[]{:S(2)}, u32[]{:S(2)}) collective-permute-start(bf16[32,7168]{1,0:T(8,128)(2,1)S(1)} %get-tuple-element.32), channel_id=1, source_target_pairs={{0,96},{32,0},{64,32},{96,64},{1,97},{33,1},{65,33},{97,65},{2,98}... | collective-permute-start | bytes 1376264 | tf_op jit(solution)/shard_map/ppermute | solution.py:30
  153.7 10.8 %collective-permute-start.23 = (bf16[16,7168]{1,0:T(8,128)(2,1)S(1)}, bf16[16,7168]{1,0:T(8,128)(2,1)S(1)}, u32[]{:S(2)}, u32[]{:S(2)}) collective-permute-start(bf16[16,7168]{1,0:T(8,128)(2,1)S(1)} %get-tuple-element.37), channel_id=1, source_target_pairs={{0,2},{2,4},{4,6},{6,8},{8,10},{10,12},{12,14},{14,16},{16,18},{18... | collective-permute-start | bytes 688136 | tf_op jit(solution)/shard_map/ppermute | solution.py:30
  153.9 10.7 %collective-permute-start.24 = (bf16[16,7168]{1,0:T(8,128)(2,1)S(1)}, bf16[16,7168]{1,0:T(8,128)(2,1)S(1)}, u32[]{:S(2)}, u32[]{:S(2)}) collective-permute-start(bf16[16,7168]{1,0:T(8,128)(2,1)S(1)} %get-tuple-element.38), channel_id=1, source_target_pairs={{0,30},{2,0},{4,2},{6,4},{8,6},{10,8},{12,10},{14,12},{16,14},{18,... | collective-permute-start | bytes 688136 | tf_op jit(solution)/shard_map/ppermute | solution.py:30
  165.6 13.1 %collective-permute-start.27 = (bf16[4,7168]{1,0:T(4,128)(2,1)S(1)}, bf16[4,7168]{1,0:T(4,128)(2,1)S(1)}, u32[]{:S(2)}, u32[]{:S(2)}) collective-permute-start(bf16[4,7168]{1,0:T(4,128)(2,1)S(1)} %slice.138), channel_id=1, source_target_pairs={{0,16},{2,18},{4,20},{6,22},{8,24},{10,26},{12,28},{14,30},{16,0},... | collective-permute-start | bytes 172040 | tf_op jit(solution)/shard_map/ppermute | solution.py:30
  168.9 9.8 %collective-permute-start.28 = (bf16[4,7168]{1,0:T(4,128)(2,1)S(1)}, bf16[4,7168]{1,0:T(4,128)(2,1)S(1)}, u32[]{:S(2)}, u32[]{:S(2)}) collective-permute-start(bf16[4,7168]{1,0:T(4,128)(2,1)S(1)} %get-tuple-element.25), channel_id=1, source_target_pairs={{0,8},{2,10},{4,12},{6,14},{8,16},{10,18},{12,20},{14,22},{16,24},... | collective-permute-start | bytes 172040 | tf_op jit(solution)/shard_map/ppermute | solution.py:30
  (20 other events, 72.5 us)

commit v6 on v5

--- a/solution.py
+++ b/solution.py
@@ -15,8 +15,7 @@
 VMEM_LIMIT = 8 * 2**20
 EP = ("ep_0", "ep_1", "ep_2")
 GROUPS_EP = ("groups", "ep_0", "ep_1", "ep_2")
-FAR = (8, 4, 12)
-Z_OFFSETS = (0, 8, 4, 12, 1, 9, 5, 13, 15, 7, 3, 11, 2, 10, 14, 6)
+Z_OFFSETS = (4, 0, 12, 8, 5, 1, 13, 9, 3, 15, 11, 7, 6, 2, 14, 10)
 LOW, HIGH = jnp.bfloat16, jnp.float32
 
 
@@ -143,12 +142,12 @@
     plus_two = received(rows[12 * n : 14 * n], 2)
     minus_two = received(rows[14 * n :], -2)
     near = rows[: 4 * n] + plus + minus
-    pieces = near[2 * n : 3 * n].astype(LOW), near[3 * n :].astype(LOW), near[: 2 * n]
-    low_b, low_c, top = lax.optimization_barrier(pieces)
-    total = received(low_b, FAR[1]) + received(low_c, FAR[2])
-    top = copied(top)
-    top = top + plus_two + minus_two
-    return top[:n] + received(top[n:], FAR[0]) + total
+    far_a, near = lax.optimization_barrier((near[3 * n :].astype(LOW), near))
+    far_a = received(far_a, 8)
+    near = copied(near)
+    far_b = received(near[:n] + plus_two[:n], 4)
+    far_c = received(near[2 * n : 3 * n] + minus_two[n:], 12)
+    return near[n : 2 * n] + plus_two[n:] + minus_two[:n] + far_a + far_b + far_c
 
 
 def layer(tokens, routes, gates, gate_weight, up_weight, down_weight):

time: 184 us -> 188 us (1.022)
  waiting for transfers between devices: 50.9 us -> 54.4 us
    ppermute x24, waiting for transfers between devices: 42.3 us -> 45.8 us  [give_to(): lax.ppermute(value, axis, [(i, (i + offset) % count) for i in range(count)])]
  transfers between devices with their start and end apart: 30 -> 30, of which waited for: 10 -> 8; matrix products, arithmetic and copies ran while one was open for 1% -> 1% of each run, Pallas kernels for 10% -> 10%
where the time goes in v6:
time: 188 us; the launch traced here: 187 us
  waiting for transfers between devices  54.4 us (29%)
  blocking collectives  53.7 us (29%)
  starting transfers between devices  36.3 us (19%)
  local copies, waits for them, and re-layouts  19 us (10%)
  Pallas kernels  17.8 us (9%)
  other arithmetic  5.04 us (3%)
    all_gather x1, blocking collectives, layer(): lax.all_gather(own, 'ep_1', axis=0, tiled=True)  53.7 us
    ppermute x24, waiting for transfers between devices, give_to(): lax.ppermute(value, axis, [(i, (i + offset) % count) for i in range(count)])  45.8 us
    ppermute x24, starting transfers between devices, give_to(): lax.ppermute(value, axis, [(i, (i + offset) % count) for i in range(count)])  26.6 us
    unnamed x29, local copies, waits for them, and re-layouts  17.9 us
    pallas_call x4, Pallas kernels, expert_of(): pl.pallas_call(functools.partial(expert_kernel, len(blocks)), in_specs=[p...  17.8 us
    ppermute x6, starting transfers between devices, take_from(): lax.ppermute(value, axis, [((i + offset) % count, i) for i in range(count)])  9.71 us
    ppermute x6, waiting for transfers between devices, take_from(): lax.ppermute(value, axis, [((i + offset) % count, i) for i in range(count)])  8.62 us
  transfers between devices with their start and end apart: 30, of which 8 were waited for; matrix products, arithmetic and copies ran while one was open for 1% of the time, Pallas kernels for 10%

profile of v6, /device:TPU:38, one launch (start us, length us, event | category | flops | bytes accessed | tf_op | source)
XLA Modules:
  0.0 186.9 jit_solution(8144876385288548553)
XLA Ops:
  1.7 53.7 %all-gather = bf16[16,4,7296]{2,1,0:T(4,128)(2,1)S(1)} all-gather(bf16[1,4,7296]{2,1,0:T(4,128)(2,1)S(1)} %maximum_bitcast_fusion), channel_id=1, replica_groups=mesh['groups'=2,'ep_0'=4,'ep_1'=16,'ep_2'=2] {'ep_1'}, dimensions={0}, use_global_device_ids=true | all-gather | bytes 992256 | tf_op jit(solution)/shard_map/all_gather | solution.py:168
  57.2 2.5 %collective-permute-start.3 = (bf16[32,7296]{1,0:T(8,128)(2,1)S(1)}, bf16[32,7296]{1,0:T(8,128)(2,1)S(1)}, u32[]{:S(2)}, u32[]{:S(2)}) collective-permute-start(bf16[32,7296]{1,0:T(8,128)(2,1)S(1)} %get-tuple-element.30), channel_id=1, source_target_pairs={{96,0},{0,32},{32,64},{64,96},{97,1},{1,33},{33,65},{65,97},{98,2}... | collective-permute-start | bytes 1400840 | tf_op jit(solution)/shard_map/ppermute | solution.py:24
  59.7 3.2 %collective-permute-start.9 = (bf16[32,7296]{1,0:T(8,128)(2,1)}, bf16[32,7296]{1,0:T(8,128)(2,1)}, u32[]{:S(2)}, u32[]{:S(2)}) collective-permute-start(bf16[32,7296]{1,0:T(8,128)(2,1)} %get-tuple-element.29), channel_id=1, source_target_pairs={{96,0},{0,32},{32,64},{64,96},{97,1},{1,33},{33,65},{65,97},{98,2}... | collective-permute-start | bytes 1400840 | tf_op jit(solution)/shard_map/ppermute | solution.py:24
  62.9 5.6 %collective-permute-done.2.refs_0_ = bf16[32,7296]{1,0:T(8,128)(2,1)S(1)} collective-permute-done((bf16[32,7296]{1,0:T(8,128)(2,1)}, bf16[32,7296]{1,0:T(8,128)(2,1)S(1)}, u32[]{:S(2)}, u32[]{:S(2)}) %collective-permute-start.2) | collective-permute-done | bytes 466976 | tf_op jit(solution)/shard_map/ppermute | solution.py:24
  70.6 3.0 %collective-permute-done.8.refs_0_ = bf16[32,7296]{1,0:T(8,128)(2,1)} collective-permute-done((bf16[32,7296]{1,0:T(8,128)(2,1)S(1)}, bf16[32,7296]{1,0:T(8,128)(2,1)}, u32[]{:S(2)}, u32[]{:S(2)}) %collective-permute-start.8) | collective-permute-done | bytes 466976 | tf_op jit(solution)/shard_map/ppermute | solution.py:24
  74.9 3.2 %collective-permute-start.14 = (bf16[32,7296]{1,0:T(8,128)(2,1)}, bf16[32,7296]{1,0:T(8,128)(2,1)}, u32[]{:S(2)}, u32[]{:S(2)}) collective-permute-start(bf16[32,7296]{1,0:T(8,128)(2,1)} %collective-permute-done.9.refs_1_), channel_id=1, source_target_pairs={{96,0},{0,32},{32,64},{64,96},{97,1},{1,33},{33,65},{65,97},{98,2}... | collective-permute-start | bytes 1400840 | tf_op jit(solution)/shard_map/ppermute | solution.py:24
  78.2 2.0 %copy-done = bf16[7168,256]{1,0:T(8,128)(2,1)S(1)} copy-done((bf16[7168,256]{1,0:T(8,128)(2,1)S(1)}, bf16[7168,256]{1,0:T(8,128)(2,1)}, u32[]{:S(2)}) %copy-start) | copy-done | bytes 3670040
  80.2 2.0 %copy-done.3 = bf16[7168,256]{1,0:T(8,128)(2,1)S(1)} copy-done((bf16[7168,256]{1,0:T(8,128)(2,1)S(1)}, bf16[7168,256]{1,0:T(8,128)(2,1)}, u32[]{:S(2)}) %copy-start.3) | copy-done | bytes 3670040
  82.3 2.0 %copy-done.5 = bf16[256,7168]{1,0:T(8,128)(2,1)S(1)} copy-done((bf16[256,7168]{1,0:T(8,128)(2,1)S(1)}, bf16[256,7168]{1,0:T(8,128)(2,1)}, u32[]{:S(2)}) %copy-start.5) | copy-done | bytes 3670040
  87.4 5.0 %expert.5 = (f32[64,7168]{1,0:T(8,128)S(1)}, bf16[64,7168]{1,0:T(8,128)(2,1)}) custom-call(s32[1]{0:T(128)} %bitcast.expert_ref, bf16[32,7296]{1,0:T(8,128)(2,1)S(1)} %copy-done.8, bf16[32,7296]{1,0:T(8,128)(2,1)S(1)} %copy-done.10, bf16[32,7296]{1,0:T(8,128)(2,1)S(1)} %copy-done.12, bf16[32,7296]{1,0:T(8,128)(2,1)} %collective-permute-done.5.refs_3_, ...), custom_call_target="tpu_custom_call" | custom-call | flops 1409286144 | bytes 16515072 | tf_op jit(solution)/shard_map/expert/pallas_call | solution.py:99
  93.8 2.0 %copy-done.1 = bf16[7168,256]{1,0:T(8,128)(2,1)S(1)} copy-done((bf16[7168,256]{1,0:T(8,128)(2,1)S(1)}, bf16[7168,256]{1,0:T(8,128)(2,1)}, u32[]{:S(2)}) %copy-start.1) | copy-done | bytes 3670040
  95.8 2.0 %copy-done.4 = bf16[7168,256]{1,0:T(8,128)(2,1)S(1)} copy-done((bf16[7168,256]{1,0:T(8,128)(2,1)S(1)}, bf16[7168,256]{1,0:T(8,128)(2,1)}, u32[]{:S(2)}) %copy-start.4) | copy-done | bytes 3670040
  97.9 2.0 %copy-done.6 = bf16[256,7168]{1,0:T(8,128)(2,1)S(1)} copy-done((bf16[256,7168]{1,0:T(8,128)(2,1)S(1)}, bf16[256,7168]{1,0:T(8,128)(2,1)}, u32[]{:S(2)}) %copy-start.6) | copy-done | bytes 3670040
  99.9 4.6 %expert.6 = (f32[64,7168]{1,0:T(8,128)S(1)}, bf16[64,7168]{1,0:T(8,128)(2,1)S(1)}) custom-call(s32[1]{0:T(128)} %bitcast.expert_ref, bf16[32,7296]{1,0:T(8,128)(2,1)} %collective-permute-done.8.refs_0_, bf16[32,7296]{1,0:T(8,128)(2,1)} %collective-permute-done.9.refs_1_, bf16[32,7296]{1,0:T(8,128)(2,1)} %collective-permute-done.10.refs_2_, ...), custom_call_target="tpu_custom_call" | custom-call | flops 1409286144 | bytes 16515072 | tf_op jit(solution)/shard_map/expert/pallas_call | solution.py:99
  105.0 4.2 %expert.4 = (f32[64,7168]{1,0:T(8,128)S(1)}, bf16[64,7168]{1,0:T(8,128)(2,1)S(1)}) custom-call(s32[1]{0:T(128)} %bitcast.expert_ref, bf16[64,7296]{1,0:T(8,128)(2,1)S(1)} %reshape.23.refs_0_, bf16[64,7296]{1,0:T(8,128)(2,1)} %collective-permute-done.refs_1_, bf16[7168,256]{1,0:T(8,128)(2,1)S(1)} %copy-done.2, bf16[7168,256]{1,0:T(8,128)(2,1)S(1)} %copy-done.4, ...), custom_call_target="tpu_custom_call" | custom-call | flops 1409286144 | bytes 16515072 | tf_op jit(solution)/shard_map/expert/pallas_call | solution.py:99
  109.7 4.0 %expert.7 = (f32[64,7168]{1,0:T(8,128)S(1)}, bf16[64,7168]{1,0:T(8,128)(2,1)S(1)}) custom-call(s32[1]{0:T(128)} %bitcast.expert_ref, bf16[32,7296]{1,0:T(8,128)(2,1)S(1)} %collective-permute-done.13.refs_0_, bf16[32,7296]{1,0:T(8,128)(2,1)} %collective-permute-done.14.refs_1_, bf16[32,7296]{1,0:T(8,128)(2,1)S(1)} %collective-permute-done.15.refs_2_, ...), custom_call_target="tpu_custom_call" | custom-call | flops 1409286144 | bytes 16515072 | tf_op jit(solution)/shard_map/expert/pallas_call | solution.py:99
  120.1 18.0 %collective-permute-done.18 = bf16[32,7168]{1,0:T(8,128)(2,1)S(1)} collective-permute-done((bf16[32,7168]{1,0:T(8,128)(2,1)S(1)}, bf16[32,7168]{1,0:T(8,128)(2,1)S(1)}, u32[]{:S(2)}, u32[]{:S(2)}) %collective-permute-start.18) | collective-permute-done | bytes 458784 | tf_op jit(solution)/shard_map/ppermute | solution.py:29
  141.9 9.7 %collective-permute-done.19 = bf16[32,7168]{1,0:T(8,128)(2,1)S(1)} collective-permute-done((bf16[32,7168]{1,0:T(8,128)(2,1)S(1)}, bf16[32,7168]{1,0:T(8,128)(2,1)S(1)}, u32[]{:S(2)}, u32[]{:S(2)}) %collective-permute-start.19) | collective-permute-done | bytes 458784 | tf_op jit(solution)/shard_map/ppermute | solution.py:29
  153.9 3.2 %collective-permute-start.24 = (bf16[16,7168]{1,0:T(8,128)(2,1)S(1)}, bf16[16,7168]{1,0:T(8,128)(2,1)S(1)}, u32[]{:S(2)}, u32[]{:S(2)}) collective-permute-start(bf16[16,7168]{1,0:T(8,128)(2,1)S(1)} %get-tuple-element.32), channel_id=1, source_target_pairs={{0,30},{2,0},{4,2},{6,4},{8,6},{10,8},{12,10},{14,12},{16,14},{18,... | collective-permute-start | bytes 688136 | tf_op jit(solution)/shard_map/ppermute | solution.py:29
  157.2 4.1 %collective-permute-start.26 = (bf16[8,7168]{1,0:T(8,128)(2,1)S(1)}, bf16[8,7168]{1,0:T(8,128)(2,1)S(1)}, u32[]{:S(2)}, u32[]{:S(2)}) collective-permute-start(bf16[8,7168]{1,0:T(8,128)(2,1)S(1)} %get-tuple-element.34), channel_id=1, source_target_pairs={{0,28},{2,30},{4,0},{6,2},{8,4},{10,6},{12,8},{14,10},{16,12},{18,... | collective-permute-start | bytes 344072 | tf_op jit(solution)/shard_map/ppermute | solution.py:29
  161.3 4.1 %collective-permute-done.25 = bf16[8,7168]{1,0:T(8,128)(2,1)S(1)} collective-permute-done((bf16[8,7168]{1,0:T(8,128)(2,1)S(1)}, bf16[8,7168]{1,0:T(8,128)(2,1)S(1)}, u32[]{:S(2)}, u32[]{:S(2)}) %collective-permute-start.25) | collective-permute-done | bytes 114720 | tf_op jit(solution)/shard_map/ppermute | solution.py:29
  166.9 4.9 %collective-permute-start.29 = (bf16[4,7168]{1,0:T(4,128)(2,1)S(1)}, bf16[4,7168]{1,0:T(4,128)(2,1)S(1)}, u32[]{:S(2)}, u32[]{:S(2)}) collective-permute-start(bf16[4,7168]{1,0:T(4,128)(2,1)S(1)} %get-tuple-element.40), channel_id=1, source_target_pairs={{0,24},{2,26},{4,28},{6,30},{8,0},{10,2},{12,4},{14,6},{16,8},{18,... | collective-permute-start | bytes 172040 | tf_op jit(solution)/shard_map/ppermute | solution.py:29
  171.8 3.2 %collective-permute-start.27 = (bf16[4,7168]{1,0:T(4,128)(2,1)S(1)}, bf16[4,7168]{1,0:T(4,128)(2,1)S(1)}, u32[]{:S(2)}, u32[]{:S(2)}) collective-permute-start(bf16[4,7168]{1,0:T(4,128)(2,1)S(1)} %slice.167), channel_id=1, source_target_pairs={{0,16},{2,18},{4,20},{6,22},{8,24},{10,26},{12,28},{14,30},{16,0},... | collective-permute-start | bytes 172040 | tf_op jit(solution)/shard_map/ppermute | solution.py:29
  175.0 11.2 %collective-permute-done.27 = bf16[4,7168]{1,0:T(4,128)(2,1)S(1)} collective-permute-done((bf16[4,7168]{1,0:T(4,128)(2,1)S(1)}, bf16[4,7168]{1,0:T(4,128)(2,1)S(1)}, u32[]{:S(2)}, u32[]{:S(2)}) %collective-permute-start.27) | collective-permute-done | bytes 57376 | tf_op jit(solution)/shard_map/ppermute | solution.py:29
  (98 shorter events, 27.0 us)
Async XLA Ops:
  56.5 12.1 %collective-permute-start.2 = (bf16[32,7296]{1,0:T(8,128)(2,1)}, bf16[32,7296]{1,0:T(8,128)(2,1)S(1)}, u32[]{:S(2)}, u32[]{:S(2)}) collective-permute-start(bf16[32,7296]{1,0:T(8,128)(2,1)} %get-tuple-element.29), channel_id=1, source_target_pairs={{32,0},{64,32},{96,64},{0,96},{33,1},{65,33},{97,65},{1,97},{34,2}... | collective-permute-start | bytes 1400840 | tf_op jit(solution)/shard_map/ppermute | solution.py:24
  57.2 12.2 %collective-permute-start.3 = (bf16[32,7296]{1,0:T(8,128)(2,1)S(1)}, bf16[32,7296]{1,0:T(8,128)(2,1)S(1)}, u32[]{:S(2)}, u32[]{:S(2)}) collective-permute-start(bf16[32,7296]{1,0:T(8,128)(2,1)S(1)} %get-tuple-element.30), channel_id=1, source_target_pairs={{96,0},{0,32},{32,64},{64,96},{97,1},{1,33},{33,65},{65,97},{98,2}... | collective-permute-start | bytes 1400840 | tf_op jit(solution)/shard_map/ppermute | solution.py:24
  59.7 13.9 %collective-permute-start.8 = (bf16[32,7296]{1,0:T(8,128)(2,1)S(1)}, bf16[32,7296]{1,0:T(8,128)(2,1)}, u32[]{:S(2)}, u32[]{:S(2)}) collective-permute-start(bf16[32,7296]{1,0:T(8,128)(2,1)S(1)} %get-tuple-element.30), channel_id=1, source_target_pairs={{32,0},{64,32},{96,64},{0,96},{33,1},{65,33},{97,65},{1,97},{34,2}... | collective-permute-start | bytes 1400840 | tf_op jit(solution)/shard_map/ppermute | solution.py:24
  59.7 13.9 %collective-permute-start.9 = (bf16[32,7296]{1,0:T(8,128)(2,1)}, bf16[32,7296]{1,0:T(8,128)(2,1)}, u32[]{:S(2)}, u32[]{:S(2)}) collective-permute-start(bf16[32,7296]{1,0:T(8,128)(2,1)} %get-tuple-element.29), channel_id=1, source_target_pairs={{96,0},{0,32},{32,64},{64,96},{97,1},{1,33},{33,65},{65,97},{98,2}... | collective-permute-start | bytes 1400840 | tf_op jit(solution)/shard_map/ppermute | solution.py:24
  73.6 18.7 %collective-permute-start.13 = (bf16[32,7296]{1,0:T(8,128)(2,1)}, bf16[32,7296]{1,0:T(8,128)(2,1)S(1)}, u32[]{:S(2)}, u32[]{:S(2)}) collective-permute-start(bf16[32,7296]{1,0:T(8,128)(2,1)} %collective-permute-done.8.refs_0_), channel_id=1, source_target_pairs={{32,0},{64,32},{96,64},{0,96},{33,1},{65,33},{97,65},{1,97},{34,2}... | collective-permute-start | bytes 1400840 | tf_op jit(solution)/shard_map/ppermute | solution.py:24
  73.6 31.4 %collective-permute-start = (bf16[64,7296]{1,0:T(8,128)(2,1)S(1)}, bf16[64,7296]{1,0:T(8,128)(2,1)}, u32[]{:S(2)}, u32[]{:S(2)}) collective-permute-start(bf16[64,7296]{1,0:T(8,128)(2,1)S(1)} %reshape.23.refs_0_), channel_id=1, source_target_pairs={{0,1},{1,0},{2,3},{3,2},{4,5},{5,4},{6,7},{7,6},{8,9},{9,8},{10,11... | collective-permute-start | bytes 2801672 | tf_op jit(solution)/shard_map/ppermute | solution.py:29
  73.6 19.6 %collective-permute-start.10 = (bf16[32,7296]{1,0:T(8,128)(2,1)}, bf16[32,7296]{1,0:T(8,128)(2,1)}, u32[]{:S(2)}, u32[]{:S(2)}) collective-permute-start(bf16[32,7296]{1,0:T(8,128)(2,1)} %collective-permute-done.8.refs_0_), channel_id=1, source_target_pairs={{0,1},{1,0},{2,3},{3,2},{4,5},{5,4},{6,7},{7,6},{8,9},{9,8},{10,11... | collective-permute-start | bytes 1400840 | tf_op jit(solution)/shard_map/ppermute | solution.py:29
  74.9 18.1 %collective-permute-start.14 = (bf16[32,7296]{1,0:T(8,128)(2,1)}, bf16[32,7296]{1,0:T(8,128)(2,1)}, u32[]{:S(2)}, u32[]{:S(2)}) collective-permute-start(bf16[32,7296]{1,0:T(8,128)(2,1)} %collective-permute-done.9.refs_1_), channel_id=1, source_target_pairs={{96,0},{0,32},{32,64},{64,96},{97,1},{1,33},{33,65},{65,97},{98,2}... | collective-permute-start | bytes 1400840 | tf_op jit(solution)/shard_map/ppermute | solution.py:24
  78.2 15.6 %collective-permute-start.11 = (bf16[32,7296]{1,0:T(8,128)(2,1)}, bf16[32,7296]{1,0:T(8,128)(2,1)}, u32[]{:S(2)}, u32[]{:S(2)}) collective-permute-start(bf16[32,7296]{1,0:T(8,128)(2,1)} %collective-permute-done.9.refs_1_), channel_id=1, source_target_pairs={{0,1},{1,0},{2,3},{3,2},{4,5},{5,4},{6,7},{7,6},{8,9},{9,8},{10,11... | collective-permute-start | bytes 1400840 | tf_op jit(solution)/shard_map/ppermute | solution.py:29
  92.4 21.6 %collective-permute-start.6 = (bf16[64,7168]{1,0:T(8,128)(2,1)}, bf16[64,7168]{1,0:T(8,128)(2,1)}, u32[]{:S(2)}, u32[]{:S(2)}) collective-permute-start(bf16[64,7168]{1,0:T(8,128)(2,1)} %get-tuple-element.18), channel_id=1, source_target_pairs={{0,1},{1,0},{2,3},{3,2},{4,5},{5,4},{6,7},{7,6},{8,9},{9,8},{10,11... | collective-permute-start | bytes 2752520 | tf_op jit(solution)/shard_map/ppermute | solution.py:29
  93.1 16.6 %collective-permute-start.15 = (bf16[32,7296]{1,0:T(8,128)(2,1)S(1)}, bf16[32,7296]{1,0:T(8,128)(2,1)S(1)}, u32[]{:S(2)}, u32[]{:S(2)}) collective-permute-start(bf16[32,7296]{1,0:T(8,128)(2,1)S(1)} %collective-permute-done.13.refs_0_), channel_id=1, source_target_pairs={{0,1},{1,0},{2,3},{3,2},{4,5},{5,4},{6,7},{7,6},{8,9},{9,8},{10,11... | collective-permute-start | bytes 1400840 | tf_op jit(solution)/shard_map/ppermute | solution.py:29
  93.2 16.4 %collective-permute-start.16 = (bf16[32,7296]{1,0:T(8,128)(2,1)}, bf16[32,7296]{1,0:T(8,128)(2,1)S(1)}, u32[]{:S(2)}, u32[]{:S(2)}) collective-permute-start(bf16[32,7296]{1,0:T(8,128)(2,1)} %collective-permute-done.14.refs_1_), channel_id=1, source_target_pairs={{0,1},{1,0},{2,3},{3,2},{4,5},{5,4},{6,7},{7,6},{8,9},{9,8},{10,11... | collective-permute-start | bytes 1400840 | tf_op jit(solution)/shard_map/ppermute | solution.py:29
  104.5 14.8 %collective-permute-start.12 = (bf16[64,7168]{1,0:T(8,128)(2,1)S(1)}, bf16[64,7168]{1,0:T(8,128)(2,1)S(1)}, u32[]{:S(2)}, u32[]{:S(2)}) collective-permute-start(bf16[64,7168]{1,0:T(8,128)(2,1)S(1)} %get-tuple-element.20), channel_id=1, source_target_pairs={{0,1},{1,0},{2,3},{3,2},{4,5},{5,4},{6,7},{7,6},{8,9},{9,8},{10,11... | collective-permute-start | bytes 2752520 | tf_op jit(solution)/shard_map/ppermute | solution.py:29
  109.2 32.6 %collective-permute-start.1 = (bf16[64,7168]{1,0:T(8,128)(2,1)S(1)}, bf16[64,7168]{1,0:T(8,128)(2,1)S(1)}, u32[]{:S(2)}, u32[]{:S(2)}) collective-permute-start(bf16[64,7168]{1,0:T(8,128)(2,1)S(1)} %get-tuple-element.16), channel_id=1, source_target_pairs={{0,1},{1,0},{2,3},{3,2},{4,5},{5,4},{6,7},{7,6},{8,9},{9,8},{10,11... | collective-permute-start | bytes 2752520 | tf_op jit(solution)/shard_map/ppermute | solution.py:29
  115.4 26.5 %collective-permute-start.20 = (bf16[32,7168]{1,0:T(8,128)(2,1)S(1)}, bf16[32,7168]{1,0:T(8,128)(2,1)S(1)}, u32[]{:S(2)}, u32[]{:S(2)}) collective-permute-start(bf16[32,7168]{1,0:T(8,128)(2,1)S(1)} %get-tuple-element.36), channel_id=1, source_target_pairs={{0,32},{32,64},{64,96},{96,0},{1,33},{33,65},{65,97},{97,1},{2,34}... | collective-permute-start | bytes 1376264 | tf_op jit(solution)/shard_map/ppermute | solution.py:29
  115.5 26.4 %collective-permute-start.7 = (bf16[32,7168]{1,0:T(8,128)(2,1)S(1)}, bf16[32,7168]{1,0:T(8,128)(2,1)S(1)}, u32[]{:S(2)}, u32[]{:S(2)}) collective-permute-start(bf16[32,7168]{1,0:T(8,128)(2,1)S(1)} %get-tuple-element.35), channel_id=1, source_target_pairs={{0,96},{32,0},{64,32},{96,64},{1,97},{33,1},{65,33},{97,65},{2,98}... | collective-permute-start | bytes 1376264 | tf_op jit(solution)/shard_map/ppermute | solution.py:29
  117.8 20.3 %collective-permute-start.18 = (bf16[32,7168]{1,0:T(8,128)(2,1)S(1)}, bf16[32,7168]{1,0:T(8,128)(2,1)S(1)}, u32[]{:S(2)}, u32[]{:S(2)}) collective-permute-start(bf16[32,7168]{1,0:T(8,128)(2,1)S(1)} %get-tuple-element.37), channel_id=1, source_target_pairs={{0,32},{32,64},{64,96},{96,0},{1,33},{33,65},{65,97},{97,1},{2,34}... | collective-permute-start | bytes 1376264 | tf_op jit(solution)/shard_map/ppermute | solution.py:29
  119.3 20.2 %collective-permute-start.21 = (bf16[32,7168]{1,0:T(8,128)(2,1)S(1)}, bf16[32,7168]{1,0:T(8,128)(2,1)S(1)}, u32[]{:S(2)}, u32[]{:S(2)}) collective-permute-start(bf16[32,7168]{1,0:T(8,128)(2,1)S(1)} %get-tuple-element.38), channel_id=1, source_target_pairs={{0,96},{32,0},{64,32},{96,64},{1,97},{33,1},{65,33},{97,65},{2,98}... | collective-permute-start | bytes 1376264 | tf_op jit(solution)/shard_map/ppermute | solution.py:29
  139.6 12.0 %collective-permute-start.19 = (bf16[32,7168]{1,0:T(8,128)(2,1)S(1)}, bf16[32,7168]{1,0:T(8,128)(2,1)S(1)}, u32[]{:S(2)}, u32[]{:S(2)}) collective-permute-start(bf16[32,7168]{1,0:T(8,128)(2,1)S(1)} %get-tuple-element.27), channel_id=1, source_target_pairs={{0,32},{32,64},{64,96},{96,0},{1,33},{33,65},{65,97},{97,1},{2,34}... | collective-permute-start | bytes 1376264 | tf_op jit(solution)/shard_map/ppermute | solution.py:29
  139.9 13.1 %collective-permute-start.22 = (bf16[32,7168]{1,0:T(8,128)(2,1)S(1)}, bf16[32,7168]{1,0:T(8,128)(2,1)S(1)}, u32[]{:S(2)}, u32[]{:S(2)}) collective-permute-start(bf16[32,7168]{1,0:T(8,128)(2,1)S(1)} %get-tuple-element.28), channel_id=1, source_target_pairs={{0,96},{32,0},{64,32},{96,64},{1,97},{33,1},{65,33},{97,65},{2,98}... | collective-permute-start | bytes 1376264 | tf_op jit(solution)/shard_map/ppermute | solution.py:29
  153.7 11.8 %collective-permute-start.23 = (bf16[16,7168]{1,0:T(8,128)(2,1)S(1)}, bf16[16,7168]{1,0:T(8,128)(2,1)S(1)}, u32[]{:S(2)}, u32[]{:S(2)}) collective-permute-start(bf16[16,7168]{1,0:T(8,128)(2,1)S(1)} %get-tuple-element.31), channel_id=1, source_target_pairs={{0,2},{2,4},{4,6},{6,8},{8,10},{10,12},{12,14},{14,16},{16,18},{18... | collective-permute-start | bytes 688136 | tf_op jit(solution)/shard_map/ppermute | solution.py:29
  153.9 11.6 %collective-permute-start.24 = (bf16[16,7168]{1,0:T(8,128)(2,1)S(1)}, bf16[16,7168]{1,0:T(8,128)(2,1)S(1)}, u32[]{:S(2)}, u32[]{:S(2)}) collective-permute-start(bf16[16,7168]{1,0:T(8,128)(2,1)S(1)} %get-tuple-element.32), channel_id=1, source_target_pairs={{0,30},{2,0},{4,2},{6,4},{8,6},{10,8},{12,10},{14,12},{16,14},{18,... | collective-permute-start | bytes 688136 | tf_op jit(solution)/shard_map/ppermute | solution.py:29
  165.7 9.2 %collective-permute-start.28 = (bf16[4,7168]{1,0:T(4,128)(2,1)S(1)}, bf16[4,7168]{1,0:T(4,128)(2,1)S(1)}, u32[]{:S(2)}, u32[]{:S(2)}) collective-permute-start(bf16[4,7168]{1,0:T(4,128)(2,1)S(1)} %get-tuple-element.39), channel_id=1, source_target_pairs={{0,8},{2,10},{4,12},{6,14},{8,16},{10,18},{12,20},{14,22},{16,24},... | collective-permute-start | bytes 172040 | tf_op jit(solution)/shard_map/ppermute | solution.py:29
  171.8 14.4 %collective-permute-start.27 = (bf16[4,7168]{1,0:T(4,128)(2,1)S(1)}, bf16[4,7168]{1,0:T(4,128)(2,1)S(1)}, u32[]{:S(2)}, u32[]{:S(2)}) collective-permute-start(bf16[4,7168]{1,0:T(4,128)(2,1)S(1)} %slice.167), channel_id=1, source_target_pairs={{0,16},{2,18},{4,20},{6,22},{8,24},{10,26},{12,28},{14,30},{16,0},... | collective-permute-start | bytes 172040 | tf_op jit(solution)/shard_map/ppermute | solution.py:29
  (20 other events, 71.2 us)
